TPU v7x, 8 devices: a whole 2x2x1 slice. The times are simulated.
8 devices in a mesh: rep: 1 (over z), fsdp: 8 (over y, x, core).
Axes of the slice: x: 2, y: 2, z: 1, core: 2. Of those that a mesh axis runs over, the one named last changes fastest.
Arguments:
- tokens: bfloat16 [16384, 4096], P(('rep', 'fsdp'))
- norm_w: float32 [2, 4096], replicated
- router_w: bfloat16 [2, 4096, 8], replicated
- w_gate: bfloat16 [2, 8, 4096, 1376], P(None, None, None, 'fsdp')
- w_up: bfloat16 [2, 8, 4096, 1376], P(None, None, None, 'fsdp')
- w_down: bfloat16 [2, 8, 1376, 4096], P(None, None, 'fsdp')
- route_ids: int32 [2, 16384, 2], P(None, ('rep', 'fsdp'))
Outputs:
- output: bfloat16 [16384, 4096], P(('rep', 'fsdp'))
All inputs are finite; a program needn't handle non-finite values.
Results may differ from a plain program's by a relative error of at most 0.0118026.
Values are sent between devices in bfloat16 or wider.
A program may use at most 1 GiB of HBM per device.

v0:
```python
import jax
import jax.numpy as jnp
from jax import lax
from jax.sharding import PartitionSpec as P

NORM_EPS = 1e-5


def norm_route(resid, norm_w, router_w, route_ids):
    resid_f = resid.astype(jnp.float32)
    inv_rms = lax.rsqrt(jnp.mean(resid_f * resid_f, axis=-1, keepdims=True) + NORM_EPS)
    hidden = (resid_f * inv_rms * norm_w).astype(jnp.bfloat16)
    logits = jnp.dot(hidden, router_w, preferred_element_type=jnp.float32)
    picked = jnp.take_along_axis(logits, route_ids, axis=1)
    return hidden, jax.nn.softmax(picked, axis=-1)


def expert_ffn(hidden, gate_probs, route_ids, w_gate, w_up, w_down):
    n_tok, top_k = route_ids.shape
    n_exp = w_gate.shape[0]
    flat_ids = route_ids.reshape(-1)
    sort_order = jnp.argsort(flat_ids, stable=True)
    tok_of_row = sort_order // top_k
    group_sizes = jnp.sum((flat_ids[:, None] == jnp.arange(n_exp, dtype=jnp.int32)[None, :]).astype(jnp.int32), axis=0)
    gathered = hidden[tok_of_row]
    up_gate = lax.ragged_dot(gathered, w_gate, group_sizes, preferred_element_type=jnp.float32)
    up_lin = lax.ragged_dot(gathered, w_up, group_sizes, preferred_element_type=jnp.float32)
    act_bf16 = (jax.nn.silu(up_gate) * up_lin).astype(jnp.bfloat16)
    down_out = lax.ragged_dot(act_bf16, w_down, group_sizes, preferred_element_type=jnp.float32)
    weighted = down_out * gate_probs.reshape(-1)[sort_order][:, None]
    return jax.ops.segment_sum(weighted, tok_of_row, num_segments=n_tok)


def solution(mesh):
    def local_fn(tokens, norm_w, router_w, w_gate, w_up, w_down, route_ids):
        resid = tokens
        for layer_idx in range(norm_w.shape[0]):
            gate_full = lax.all_gather(w_gate[layer_idx], "fsdp", axis=2, tiled=True)
            up_full = lax.all_gather(w_up[layer_idx], "fsdp", axis=2, tiled=True)
            down_full = lax.all_gather(w_down[layer_idx], "fsdp", axis=1, tiled=True)
            hidden, gate_probs = norm_route(resid, norm_w[layer_idx], router_w[layer_idx], route_ids[layer_idx])
            moe_sum = expert_ffn(hidden, gate_probs, route_ids[layer_idx], gate_full, up_full, down_full)
            resid = (resid.astype(jnp.float32) + moe_sum).astype(jnp.bfloat16)
        return resid

    row_spec = P(("rep", "fsdp"), None)
    col_spec = P(None, None, None, "fsdp")
    return jax.shard_map(
        local_fn,
        mesh=mesh,
        in_specs=(row_spec, P(), P(), col_spec, col_spec, P(None, None, "fsdp", None), P(None, ("rep", "fsdp"), None)),
        out_specs=row_spec,
        check_vma=False,
    )
```

profile of v0, /device:TPU:0, one launch (start us, length us, event | category | flops | bytes accessed | tf_op | source)
XLA Modules:
  0.0 2762.4 jit_solution(14233157189404908555)
XLA Ops:
  6.5 16.3 slice_bitcast_fusion.2
  22.9 16.2 slice_bitcast_fusion.1
  39.2 16.2 slice_bitcast_fusion
  55.5 0.5 all-gather.19.cloned.1.call-update
  56.1 0.5 all-gather.21.cloned.1.call-update
  56.7 0.5 all-gather.23.cloned.1.call-update
  57.2 0.6 fusion.21
  58.7 5.8 sort.31
  64.5 0.7 convert_reduce_fusion.1
  65.1 1.6 ragged-dot-metadata.1
  67.1 0.5 reshape.124
  67.6 22.1 convert_element_type.32
  89.7 7.5 multiply_reduce_fusion.1
  97.2 0.6 fusion.11
  97.8 0.6 fusion.20
  98.5 8.7 multiply_convert_fusion.1
  107.1 63.8 %gather_fusion = bf16[4096,4096]{1,0:T(8,128)(2,1)} fusion(bf16[2048,4096]{1,0:T(8,128)(2,1)} %multiply_convert_fusion.1, s32[4096]{0:T(1024)S(1)} %get-tuple-element.50), kind=kCustom, calls=%fused_computation.2 | custom fusion | bytes 67125248 | tf_op jit(solution)/shard_map/gather | solution.py:25
  170.9 10.2 fusion.6
  181.1 24.5 gather_fusion.4
  205.6 1.0 reshape.127
  207.0 0.7 fusion.1
  207.7 1.1 fusion
  208.8 0.5 reshape.38
  209.7 0.5 reshape_squeeze.7
  210.5 1.1 reshape.129
  211.6 5.8 sort.32
  217.3 0.7 convert_reduce_fusion
  218.0 1.6 ragged-dot-metadata
  219.6 40.4 %gather_fusion.1 = f32[4096]{0:T(1024)} fusion(f32[4096]{0:T(1024)S(1)} %reshape.38, s32[4096]{0:T(1024)S(1)} %copy-done.16), kind=kCustom, calls=%fused_computation.3 | custom fusion | bytes 49152 | tf_op jit(solution)/shard_map/gather | solution.py:30
  260.1 0.6 fusion.13
  260.7 160.0 %all-gather.13.cloned.1.call-done = bf16[1,8,4096,1376]{2,1,0,3:T(8,128)(2,1)} async-done(((bf16[1,8,4096,172]{2,1,0,3:T(8,128)(2,1)}), bf16[1,8,4096,1376]{2,1,0,3:T(8,128)(2,1)}) %all-gather.13.cloned.1.call-update) | async-done | bytes 90177552 | tf_op jit(solution)/shard_map/all_gather | solution.py:38
  420.8 114.5 %copy.38 = bf16[1,8,4096,1376]{3,2,1,0:T(8,128)(2,1)} copy(bf16[1,8,4096,1376]{2,1,0,3:T(8,128)(2,1)} %all-gather.13.cloned.1.call-done) | data formatting | bytes 180355072 | tf_op jit(solution)/shard_map/all_gather | solution.py:38
  535.2 282.3 %all-gather.15.cloned.1.call-done = bf16[1,8,4096,1376]{2,1,0,3:T(8,128)(2,1)} async-done(((bf16[1,8,4096,172]{2,1,0,3:T(8,128)(2,1)}), bf16[1,8,4096,1376]{2,1,0,3:T(8,128)(2,1)}) %all-gather.15.cloned.1.call-update) | async-done | bytes 90177552 | tf_op jit(solution)/shard_map/all_gather | solution.py:39
  817.6 114.4 %copy.40 = bf16[1,8,4096,1376]{3,2,1,0:T(8,128)(2,1)} copy(bf16[1,8,4096,1376]{2,1,0,3:T(8,128)(2,1)} %all-gather.15.cloned.1.call-done) | data formatting | bytes 180355072 | tf_op jit(solution)/shard_map/all_gather | solution.py:39
  932.0 282.4 %all-gather.17.cloned.1.call-done = bf16[1,8,1376,4096]{3,1,0,2:T(8,128)(2,1)} async-done(((bf16[1,8,172,4096]{3,1,0,2:T(8,128)(2,1)}), bf16[1,8,1376,4096]{3,1,0,2:T(8,128)(2,1)}) %all-gather.17.cloned.1.call-update) | async-done | bytes 90177552 | tf_op jit(solution)/shard_map/all_gather | solution.py:40
  1214.4 74.0 %copy.61 = bf16[1,8,1376,4096]{3,2,1,0:T(8,128)(2,1)} copy(bf16[1,8,1376,4096]{3,1,0,2:T(8,128)(2,1)} %all-gather.17.cloned.1.call-done) | data formatting | bytes 180355072 | tf_op jit(solution)/shard_map/all_gather | solution.py:40
  1288.3 93.6 %ragged-dot-none.5 = f32[4096,1376]{1,0:T(8,128)} custom-call(s32[1]{0:T(128)} %get-tuple-element.22, s32[9]{0:T(128)} %get-tuple-element.23, s32[23]{0:T(128)} %get-tuple-element.24, s32[23]{0:T(128)} %get-tuple-element.25, s32[1]{0:T(128)} %get-tuple-element.22, bf16[4096,4096]{1,0:T(8,128)(2,1)} %gather_fusion, bf16[8,4096,1376]{2,1,0:T(8,128)(2,1)} %bitcast.1), custom_call_target="tpu_custom_call" | custom-call | flops 46170898432 | bytes 146276384 | tf_op jit(solution)/shard_map/ragged_dot_general/ragged-dot-none
  1382.0 93.7 %ragged-dot-none.4 = f32[4096,1376]{1,0:T(8,128)} custom-call(s32[1]{0:T(128)} %get-tuple-element.22, s32[9]{0:T(128)} %get-tuple-element.23, s32[23]{0:T(128)} %get-tuple-element.24, s32[23]{0:T(128)} %get-tuple-element.25, s32[1]{0:T(128)} %get-tuple-element.22, bf16[4096,4096]{1,0:T(8,128)(2,1)} %gather_fusion, bf16[8,4096,1376]{2,1,0:T(8,128)(2,1)} %bitcast.2), custom_call_target="tpu_custom_call" | custom-call | flops 46170898432 | bytes 146276384 | tf_op jit(solution)/shard_map/ragged_dot_general/ragged-dot-none
  1475.7 19.6 multiply_convert_fusion.3
  1495.3 97.6 %ragged-dot-none.3 = f32[4096,4096]{1,0:T(8,128)} custom-call(s32[1]{0:T(128)} %get-tuple-element.22, s32[9]{0:T(128)} %get-tuple-element.23, s32[23]{0:T(128)} %get-tuple-element.24, s32[23]{0:T(128)} %get-tuple-element.25, s32[1]{0:T(128)} %get-tuple-element.22, bf16[4096,1376]{1,0:T(8,128)(2,1)} %multiply_convert_fusion.3, bf16[8,1376,4096]{2,1,0:T(8,128)(2,1)} %bitcast.63), custom_call_target="tpu_custom_call" | custom-call | flops 46170898432 | bytes 168558624 | tf_op jit(solution)/shard_map/ragged_dot_general/ragged-dot-none
  1592.8 44.6 %broadcast_multiply_fusion.1 = f32[4096,4096]{1,0:T(8,128)} fusion(f32[4096,4096]{1,0:T(8,128)} %ragged-dot-none.3, f32[4096]{0:T(1024)S(1)} %copy-done.13), kind=kLoop, calls=%fused_computation.13 | loop fusion | flops 16777216 | bytes 134234112 | tf_op jit(solution)/shard_map/mul | solution.py:30
  1637.5 118.5 %scatter_fusion = f32[2048,4096]{1,0:T(8,128)} fusion(f32[2048,4096]{1,0:T(8,128)} %convert_element_type.32, s32[4096]{0:T(1024)S(1)} %copy-done.10, f32[4096,4096]{1,0:T(8,128)} %broadcast_multiply_fusion.1), kind=kCustom, calls=%fused_computation.6 | custom fusion | flops 16777216 | bytes 201342976 | tf_op jit(solution)/shard_map/scatter-add | solution.py:31
  1756.0 15.1 multiply_reduce_fusion
  1771.0 5.1 copy-done
  1776.1 16.8 multiply_convert_fusion
  1792.9 10.2 fusion.4
  1803.1 24.5 gather_fusion.5
  1827.7 1.0 reshape.132
  1829.1 0.7 fusion.3
  1829.7 0.7 fusion.2
  1830.5 0.5 reshape.39
  1830.9 63.9 %gather_fusion.2 = bf16[4096,4096]{1,0:T(8,128)(2,1)} fusion(bf16[2048,4096]{1,0:T(8,128)(2,1)} %get-tuple-element.34, s32[4096]{0:T(1024)S(1)} %copy-done.11), kind=kCustom, calls=%fused_computation.4 | custom fusion | bytes 67125248 | tf_op jit(solution)/shard_map/gather | solution.py:25
  1894.8 40.5 %gather_fusion.3 = f32[4096]{0:T(1024)} fusion(f32[4096]{0:T(1024)S(1)} %reshape.39, s32[4096]{0:T(1024)S(1)} %copy-done.15), kind=kCustom, calls=%fused_computation.5 | custom fusion | bytes 49152 | tf_op jit(solution)/shard_map/gather | solution.py:30
  1935.3 114.5 %copy.45 = bf16[1,8,4096,1376]{3,2,1,0:T(8,128)(2,1)} copy(bf16[1,8,4096,1376]{2,1,0,3:T(8,128)(2,1)} %all-gather.19.cloned.1.call-done) | data formatting | bytes 180355072 | tf_op jit(solution)/shard_map/all_gather | solution.py:38
  2049.7 114.4 %copy.47 = bf16[1,8,4096,1376]{3,2,1,0:T(8,128)(2,1)} copy(bf16[1,8,4096,1376]{2,1,0,3:T(8,128)(2,1)} %all-gather.21.cloned.1.call-done) | data formatting | bytes 180355072 | tf_op jit(solution)/shard_map/all_gather | solution.py:39
  2164.1 93.0 %ragged-dot-none.2 = f32[4096,1376]{1,0:T(8,128)} custom-call(s32[1]{0:T(128)} %get-tuple-element.10, s32[9]{0:T(128)} %get-tuple-element.11, s32[23]{0:T(128)} %get-tuple-element.12, s32[23]{0:T(128)} %get-tuple-element.13, s32[1]{0:T(128)} %get-tuple-element.10, bf16[4096,4096]{1,0:T(8,128)(2,1)} %gather_fusion.2, bf16[8,4096,1376]{2,1,0:T(8,128)(2,1)} %bitcast.8), custom_call_target="tpu_custom_call" | custom-call | flops 46170898432 | bytes 146276384 | tf_op jit(solution)/shard_map/ragged_dot_general/ragged-dot-none
  2257.1 93.0 %ragged-dot-none.1 = f32[4096,1376]{1,0:T(8,128)} custom-call(s32[1]{0:T(128)} %get-tuple-element.10, s32[9]{0:T(128)} %get-tuple-element.11, s32[23]{0:T(128)} %get-tuple-element.12, s32[23]{0:T(128)} %get-tuple-element.13, s32[1]{0:T(128)} %get-tuple-element.10, bf16[4096,4096]{1,0:T(8,128)(2,1)} %gather_fusion.2, bf16[8,4096,1376]{2,1,0:T(8,128)(2,1)} %bitcast.9), custom_call_target="tpu_custom_call" | custom-call | flops 46170898432 | bytes 146276384 | tf_op jit(solution)/shard_map/ragged_dot_general/ragged-dot-none
  2350.1 19.6 multiply_convert_fusion.2
  2369.7 34.6 %all-gather.23.cloned.1.call-done = bf16[1,8,1376,4096]{3,1,0,2:T(8,128)(2,1)} async-done(((bf16[1,8,172,4096]{3,1,0,2:T(8,128)(2,1)}), bf16[1,8,1376,4096]{3,1,0,2:T(8,128)(2,1)}) %all-gather.23.cloned.1.call-update) | async-done | bytes 90177552 | tf_op jit(solution)/shard_map/all_gather | solution.py:40
  2404.3 73.9 %copy.60 = bf16[1,8,1376,4096]{3,2,1,0:T(8,128)(2,1)} copy(bf16[1,8,1376,4096]{3,1,0,2:T(8,128)(2,1)} %all-gather.23.cloned.1.call-done) | data formatting | bytes 180355072 | tf_op jit(solution)/shard_map/all_gather | solution.py:40
  2478.2 97.1 %ragged-dot-none = f32[4096,4096]{1,0:T(8,128)} custom-call(s32[1]{0:T(128)} %get-tuple-element.10, s32[9]{0:T(128)} %get-tuple-element.11, s32[23]{0:T(128)} %get-tuple-element.12, s32[23]{0:T(128)} %get-tuple-element.13, s32[1]{0:T(128)} %get-tuple-element.10, bf16[4096,1376]{1,0:T(8,128)(2,1)} %multiply_convert_fusion.2, bf16[8,1376,4096]{2,1,0:T(8,128)(2,1)} %bitcast.62), custom_call_target="tpu_custom_call" | custom-call | flops 46170898432 | bytes 168558624 | tf_op jit(solution)/shard_map/ragged_dot_general/ragged-dot-none
  2575.4 44.7 %broadcast_multiply_fusion = f32[4096,4096]{1,0:T(8,128)} fusion(f32[4096,4096]{1,0:T(8,128)} %ragged-dot-none, f32[4096]{0:T(1024)S(1)} %copy-done.14), kind=kLoop, calls=%fused_computation.10 | loop fusion | flops 16777216 | bytes 134234112 | tf_op jit(solution)/shard_map/mul | solution.py:30
  2620.1 117.9 %scatter_fusion.1 = f32[2048,4096]{1,0:T(8,128)} fusion(f32[2048,4096]{1,0:T(8,128)} %get-tuple-element.35, s32[4096]{0:T(1024)S(1)} %copy-done.8, f32[4096,4096]{1,0:T(8,128)} %broadcast_multiply_fusion), kind=kCustom, calls=%fused_computation.7 | custom fusion | flops 16777216 | bytes 201342976 | tf_op jit(solution)/shard_map/scatter-add | solution.py:31
  2738.0 17.4 convert_element_type.41
  (68 shorter events, 3.0 us)
Async XLA Ops:
  6.5 414.2 %all-gather.13.cloned.1.call-start = ((), (), s32[]{:S(2)}) async-start(), calls=%async_computation | async-start | bytes 101449728 | tf_op jit(solution)/shard_map/all_gather | solution.py:38
  22.9 794.7 %all-gather.15.cloned.1.call-start = ((), (), s32[]{:S(2)}) async-start(), calls=%async_computation.1 | async-start | bytes 101449728 | tf_op jit(solution)/shard_map/all_gather | solution.py:39
  39.2 1175.2 %all-gather.17.cloned.1.call-start = ((), (), s32[]{:S(2)}) async-start(), calls=%async_computation.2 | async-start | bytes 101449728 | tf_op jit(solution)/shard_map/all_gather | solution.py:40
  55.5 1.8 copy-start.17
  55.5 1879.8 %all-gather.19.cloned.1.call-start = ((), (), s32[]{:S(2)}) async-start(), calls=%async_computation.3 | async-start | bytes 101449728 | tf_op jit(solution)/shard_map/all_gather | solution.py:38
  56.1 1993.7 %all-gather.21.cloned.1.call-start = ((), (), s32[]{:S(2)}) async-start(), calls=%async_computation.4 | async-start | bytes 101449728 | tf_op jit(solution)/shard_map/all_gather | solution.py:39
  56.7 2347.7 %all-gather.23.cloned.1.call-start = ((), (), s32[]{:S(2)}) async-start(), calls=%async_computation.5 | async-start | bytes 101449728 | tf_op jit(solution)/shard_map/all_gather | solution.py:40
  58.2 8.5 copy-start.4
  67.6 30.2 %copy-start.18 = (f32[2,4096]{1,0:T(2,128)S(1)}, f32[2,4096]{1,0:T(2,128)}, u32[]{:S(2)}) copy-start(f32[2,4096]{1,0:T(2,128)} %param.10) | copy-start | bytes 98308
  67.6 30.8 %slice-start = ((s8[16777216]{0:T(1024)(128)(4,1)}), s8[4194304]{0:T(1024)(128)(4,1)S(1)}, s32[]{:S(2)}) async-start(s8[16777216]{0:T(1024)(128)(4,1)} %bitcast.64), calls=%async_computation.6 | async-start | bytes 8388608
  67.6 30.8 %slice-start.1 = ((s8[16777216]{0:T(1024)(128)(4,1)}), s8[4194304]{0:T(1024)(128)(4,1)S(1)}, s32[]{:S(2)}) async-start(s8[16777216]{0:T(1024)(128)(4,1)} %bitcast.64), calls=%async_computation.7 | async-start | bytes 8388608
  67.6 30.8 %slice-start.2 = ((s8[16777216]{0:T(1024)(128)(4,1)}), s8[4194304]{0:T(1024)(128)(4,1)S(1)}, s32[]{:S(2)}) async-start(s8[16777216]{0:T(1024)(128)(4,1)} %bitcast.64), calls=%async_computation.8 | async-start | bytes 8388608
  89.7 8.8 slice-start.3
  107.1 63.8 %copy-start.6 = (bf16[2,4096,8]{1,2,0:T(8,128)(2,1)S(1)}, bf16[2,4096,8]{1,2,0:T(8,128)(2,1)}, u32[]{:S(2)}) copy-start(bf16[2,4096,8]{1,2,0:T(8,128)(2,1)} %param.11) | copy-start | bytes 393220
  181.1 25.6 copy-start.5
  181.1 28.2 %copy-start.12 = (s32[1,2048,2]{1,2,0:T(2,128)S(1)}, s32[1,2048,2]{1,2,0:T(2,128)}, u32[]{:S(2)}) copy-start(s32[1,2048,2]{1,2,0:T(2,128)} %get-tuple-element.44) | copy-start | bytes 49156
  181.1 38.5 %copy-start.16 = (s32[4096]{0:T(1024)S(1)}, s32[4096]{0:T(1024)}, u32[]{:S(2)}) copy-start(s32[4096]{0:T(1024)} %get-tuple-element.49) | copy-start | bytes 49156
  209.7 325.6 %copy-start.2 = (s32[1,2048,2]{2,1,0:T(8,128)}, s32[1,2048,2]{2,1,0:T(8,128)S(1)}, u32[]{:S(2)}) copy-start(s32[1,2048,2]{2,1,0:T(8,128)S(1)} %copy.54) | copy-start | bytes 49156
  1495.3 97.6 %copy-start.13 = (f32[4096]{0:T(1024)S(1)}, f32[4096]{0:T(1024)}, u32[]{:S(2)}) copy-start(f32[4096]{0:T(1024)} %gather_fusion.1) | copy-start | bytes 49156
  1592.8 44.7 %copy-start.10 = (s32[4096]{0:T(1024)S(1)}, s32[4096]{0:T(1024)}, u32[]{:S(2)}) copy-start(s32[4096]{0:T(1024)} %get-tuple-element.51) | copy-start | bytes 49156
  1756.0 20.2 copy-start
  1756.0 20.2 copy-start.9
  1776.1 16.8 copy-start.7
  1776.1 27.0 copy-start.1
  1803.1 25.6 copy-start.3
  1803.1 27.8 %copy-start.11 = (s32[4096]{0:T(1024)S(1)}, s32[4096]{0:T(1024)}, u32[]{:S(2)}) copy-start(s32[4096]{0:T(1024)} %get-tuple-element.47) | copy-start | bytes 49156
  1830.9 63.9 %copy-start.15 = (s32[4096]{0:T(1024)S(1)}, s32[4096]{0:T(1024)}, u32[]{:S(2)}) copy-start(s32[4096]{0:T(1024)} %get-tuple-element.46) | copy-start | bytes 49156
  2478.2 97.1 %copy-start.14 = (f32[4096]{0:T(1024)S(1)}, f32[4096]{0:T(1024)}, u32[]{:S(2)}) copy-start(f32[4096]{0:T(1024)} %gather_fusion.3) | copy-start | bytes 49156
  2575.3 44.7 %copy-start.8 = (s32[4096]{0:T(1024)S(1)}, s32[4096]{0:T(1024)}, u32[]{:S(2)}) copy-start(s32[4096]{0:T(1024)} %get-tuple-element.48) | copy-start | bytes 49156
Sparse Core Ops, SparseCore 0:
  23.0 397.7 all-gather.12
  422.6 394.9 all-gather.14
  819.4 394.9 all-gather.16
  1216.1 394.9 all-gather.18
  1612.7 394.9 all-gather.20
  2009.4 394.9 all-gather.22
where the time goes:
time: 2780 us; the launch traced here: 2760 us
  local copies, waits for them, and re-layouts  924 us (33%)
  waiting for transfers between devices  761 us (27%)
  Pallas kernels  571 us (21%)
  other arithmetic  471 us (17%)
    another operation x6, Pallas kernels  568 us
    all_gather x2, waiting for transfers between devices, local_fn(): down_full = lax.all_gather(w_down[layer_idx], 'fsdp', axis=1, tiled=True)  317 us
    all_gather x2, waiting for transfers between devices, local_fn(): up_full = lax.all_gather(w_up[layer_idx], 'fsdp', axis=2, tiled=True)  282 us
    scatter-add x2, other arithmetic, expert_ffn(): return jax.ops.segment_sum(weighted, tok_of_row, num_segments=n_tok)  236 us
    all_gather x2, local copies, waits for them, and re-layouts, local_fn(): gate_full = lax.all_gather(w_gate[layer_idx], 'fsdp', axis=2, tiled=True)  229 us
    all_gather x2, local copies, waits for them, and re-layouts, local_fn(): up_full = lax.all_gather(w_up[layer_idx], 'fsdp', axis=2, tiled=True)  229 us
    all_gather x2, waiting for transfers between devices, local_fn(): gate_full = lax.all_gather(w_gate[layer_idx], 'fsdp', axis=2, tiled=True)  160 us
    all_gather x2, local copies, waits for them, and re-layouts, local_fn(): down_full = lax.all_gather(w_down[layer_idx], 'fsdp', axis=1, tiled=True)  148 us
  transfers between devices with their start and end apart: 6, of which 4 were waited for; matrix products, arithmetic and copies ran while one was open for 41% of the time, Pallas kernels for 17%

commit v1 on v0

v1 whole, which is shorter than its diff:
```python
import functools

import jax
import jax.numpy as jnp
from jax import lax
from jax.experimental import pallas as pl
from jax.experimental.pallas import tpu as pltpu
from jax.sharding import PartitionSpec as P


EPS = 1e-5
TM = 256
DC = 256
NG = 4
CAP = 256
SIDE_RANKS = {4: ((4, 7), (5, 6)), 2: ((2, 5, 7), (3, 4, 6))}
VMEM = 66 * 1000 * 1000


def pad16(n):
    return (n + 15) // 16 * 16


def prep_body(groups, n_exp, s_ref, *refs):
    srcs, outs, sel = refs[:3], refs[3:-1], refs[-1]
    n = sum(groups)
    wide = sel.shape[0] // n

    @pl.when(pl.program_id(0) == 0)
    def _():
        col = lax.broadcasted_iota(jnp.int32, (wide, sel.shape[1]), 1)
        line = lax.broadcasted_iota(jnp.int32, (wide, sel.shape[1]), 0)
        for k in range(n):
            sel[k * wide:(k + 1) * wide, :] = (col == line * n_exp + s_ref[k]).astype(jnp.bfloat16)

    for m in range(3):
        k = 0
        for out, size in zip(outs, groups):
            for j in range(size):
                out[j, m] = jnp.dot(sel[k * wide:(k + 1) * wide, :], srcs[m][0], preferred_element_type=jnp.float32).astype(jnp.bfloat16)
                k += 1


def prep(layer, experts, groups, w_gate, w_up, w_down):
    n_exp, width, inner = w_gate.shape[1:]
    wide = pad16(inner)
    lines = [jnp.transpose(w, order).reshape(w.shape[0], inner * n_exp, width) for w, order in ((w_gate, (0, 3, 1, 2)), (w_up, (0, 3, 1, 2)), (w_down, (0, 2, 1, 3)))]
    n = sum(groups)
    return pl.pallas_call(
        functools.partial(prep_body, groups, n_exp),
        out_shape=[jax.ShapeDtypeStruct((g, 3, wide, width), jnp.bfloat16) for g in groups],
        grid_spec=pltpu.PrefetchScalarGridSpec(
            num_scalar_prefetch=1,
            grid=(width // DC,),
            in_specs=[pl.BlockSpec((1, inner * n_exp, DC), lambda c, s: (layer, 0, c))] * 3,
            out_specs=[pl.BlockSpec((g, 3, wide, DC), lambda c, s: (0, 0, 0, c)) for g in groups],
            scratch_shapes=[pltpu.VMEM((n * wide, inner * n_exp), jnp.bfloat16)],
        ),
        compiler_params=pltpu.CompilerParams(vmem_limit_bytes=VMEM),
        cost_estimate=pl.CostEstimate(flops=n * 600_000_000, bytes_accessed=70_000_000 + n * 4_300_000, transcendentals=0),
        name="prep",
    )(experts, *lines)


def expert_body(pieces, n_w, aliased, s_ref, h_ref, *refs):
    w_refs = refs[:n_w]
    o_ref = refs[n_w + (1 if aliased else 0)]
    w1, w3, w2, act, sems = refs[n_w + (2 if aliased else 1):]
    wide = w1.shape[0] // len(pieces)
    i = pl.program_id(0)

    def copies(m, dst):
        out = []
        for p, (r, lead) in enumerate(pieces):
            src = w_refs[r].at[lead + (m,)] if isinstance(lead, tuple) else w_refs[r].at[lead, m]
            out.append(pltpu.make_async_copy(src, dst.at[pl.ds(p * wide, wide)], sems.at[m, p]))
        return out

    @pl.when(i == 0)
    def _():
        for m, dst in enumerate((w1, w3, w2)):
            for c in copies(m, dst):
                c.start()
        for m, dst in enumerate((w1, w3)):
            for c in copies(m, dst):
                c.wait()

    nt = (((1,), (1,)), ((), ()))

    @pl.when(i < s_ref[1])
    def _():
        cols = w1.shape[0]
        steps = (cols + 255) // 256

        def up(c, carry):
            at = pl.multiple_of(jnp.minimum(c * 256, cols - 256), 128)
            h = h_ref[...]
            u = lax.dot_general(h, w1[pl.ds(at, 256), :], nt, preferred_element_type=jnp.float32)
            v = lax.dot_general(h, w3[pl.ds(at, 256), :], nt, preferred_element_type=jnp.float32)
            act[:, pl.ds(at, 256)] = (jax.nn.silu(u) * v).astype(jnp.bfloat16)
            return carry

        lax.fori_loop(0, steps, up, 0)

    @pl.when(i == 0)
    def _():
        for c in copies(2, w2):
            c.wait()

    @pl.when(i < s_ref[1])
    def _():
        def down(c, carry):
            at = pl.multiple_of(c * 512, 512)
            o_ref[:, pl.ds(at, 512)] = jnp.dot(act[...], w2[:, pl.ds(at, 512)], preferred_element_type=jnp.float32)
            return carry

        lax.fori_loop(0, o_ref.shape[1] // 512, down, 0)


def expert(scalars, rows, weights, pieces, out, max_tiles, out_rows):
    width = rows.shape[1]
    wide = weights[0].shape[-2]
    cols = wide * len(pieces)
    aliased = out is not None
    at = lambda i, s: (s[0] + jnp.minimum(i, s[1] - 1), 0)
    to = lambda i, s: (s[2] + jnp.minimum(i, s[1] - 1), 0)
    anywhere = pl.BlockSpec(memory_space=pl.ANY)
    return pl.pallas_call(
        functools.partial(expert_body, pieces, len(weights), aliased),
        out_shape=jax.ShapeDtypeStruct((out_rows, width), jnp.float32),
        grid_spec=pltpu.PrefetchScalarGridSpec(
            num_scalar_prefetch=1,
            grid=(max_tiles,),
            in_specs=[pl.BlockSpec((TM, width), at)] + [anywhere] * (len(weights) + aliased),
            out_specs=pl.BlockSpec((TM, width), to),
            scratch_shapes=[pltpu.VMEM((cols, width), jnp.bfloat16)] * 3
            + [pltpu.VMEM((TM, cols), jnp.bfloat16), pltpu.SemaphoreType.DMA((3, len(pieces)))],
        ),
        input_output_aliases={2 + len(weights): 0} if aliased else {},
        compiler_params=pltpu.CompilerParams(vmem_limit_bytes=VMEM),
        cost_estimate=pl.CostEstimate(flops=3_000_000_000, bytes_accessed=60_000_000, transcendentals=0),
        name="expert",
    )(scalars, rows, *weights, *((out,) if aliased else ()))


def prefix(onehot):
    n, k = onehot.shape
    blocks = onehot.astype(jnp.float32).reshape(n // 128, 128, k)
    lower = (jnp.arange(128)[:, None] > jnp.arange(128)[None, :]).astype(jnp.float32)
    inside = jnp.einsum("ij,bjk->bik", lower, blocks)
    sums = blocks.sum(axis=1)
    nb = n // 128
    before = jnp.einsum("ij,jk->ik", (jnp.arange(nb)[:, None] > jnp.arange(nb)[None, :]).astype(jnp.float32), sums)
    return (inside + before[:, None, :]).reshape(n, k).astype(jnp.int32), sums.sum(axis=0).astype(jnp.int32)


def row_plan(slot0, slot1, n_local):
    n_tok = slot0.shape[0]
    flat = jnp.concatenate([slot0, slot1])
    onehot = flat[:, None] == jnp.arange(n_local)[None, :]
    within, counts = prefix(onehot)
    tiles = jnp.maximum((counts + TM - 1) // TM, 1)
    lower = jnp.arange(n_local)[:, None] > jnp.arange(n_local)[None, :]
    first = jnp.sum(jnp.where(lower, tiles[None, :], 0), axis=1)
    pos = jnp.sum(jnp.where(onehot, within + first[None, :] * TM, 0), axis=1)
    n = 2 * n_tok
    spare = jnp.where(jnp.arange(TM)[None, :] < (tiles * TM - counts)[:, None], jnp.arange(n_local)[:, None], n_local)
    keys = jnp.concatenate([flat, spare.reshape(-1)])
    order = lax.sort(keys * 8192 + jnp.arange(keys.shape[0], dtype=jnp.int32)) & 8191
    token = jnp.where(order < n, order % n_tok, 0)
    scalars = jnp.stack([first, tiles, first], axis=1).astype(jnp.int32)
    return token, pos[:n_tok], pos[n_tok:], scalars


def pick(table, index, size):
    return jnp.sum(jnp.where(index[..., None] == jnp.arange(size), table, 0), axis=-1)


def norm_gates(x, norm_w, router_w, ids0, ids1):
    xf = x.astype(jnp.float32)
    inv = lax.rsqrt(jnp.mean(xf * xf, axis=-1, keepdims=True) + EPS)
    h = (xf * inv * norm_w).astype(jnp.bfloat16)
    r = jnp.dot(h, router_w, preferred_element_type=jnp.float32)
    n_exp = router_w.shape[1]
    r0 = jnp.sum(jnp.where(ids0[:, None] == jnp.arange(n_exp), r, 0.0), axis=-1)
    r1 = jnp.sum(jnp.where(ids1[:, None] == jnp.arange(n_exp), r, 0.0), axis=-1)
    g = jax.nn.softmax(jnp.stack([r0, r1], axis=-1), axis=-1)
    return h, g[:, :1], g[:, 1:]


def take(table, index):
    return table.at[index].get(mode="promise_in_bounds")


def weighed(out, pos, gate, here):
    return jnp.where(here[:, None], gate * take(out, jnp.where(here, pos, 0)), 0.0)


def solution(mesh):
    n_dev = mesh.shape["fsdp"]

    def hop(a, bit):
        return lax.ppermute(a, "fsdp", [(i, i ^ bit) for i in range(n_dev)])

    def general(x, norm_w, router_w, w_gate, w_up, w_down, ids):
        n_layers, n_exp = w_gate.shape[:2]
        n_tok = x.shape[0]
        for l in range(n_layers):
            token, pos0, pos1, scalars = row_plan(ids[l, 0], ids[l, 1], n_exp)
            h, g0, g1 = norm_gates(x, norm_w[l], router_w[l], ids[l, 0], ids[l, 1])
            rows = take(h, token)

            def step(e, out, l=l, rows=rows, scalars=scalars):
                w = prep(l, e[None].astype(jnp.int32), (1,), w_gate, w_up, w_down)[0][0]
                full = lax.all_gather(w, "fsdp")
                s = lax.dynamic_index_in_dim(scalars, e, 0, keepdims=False)
                return expert(s, rows, [full], [(0, p) for p in range(n_dev)], out, n_tok // TM, rows.shape[0])

            out = lax.fori_loop(0, n_exp, step, jnp.zeros(rows.shape, jnp.float32))
            x = (x.astype(jnp.float32) + (g0 * take(out, pos0) + g1 * take(out, pos1))).astype(jnp.bfloat16)
        return x

    def local_fn(tokens, norm_w, router_w, w_gate, w_up, w_down, route_ids):
        n_layers, n_exp = w_gate.shape[:2]
        n_tok = tokens.shape[0]
        n_light = (n_exp - NG) // 2
        n_local = NG + n_light
        me = lax.axis_index("fsdp")
        ids = jnp.swapaxes(route_ids, 1, 2)
        every = lax.all_gather(ids, "fsdp")
        hits = every[..., None] == jnp.arange(n_exp)
        load = jnp.sum(hits.astype(jnp.int32), axis=(0, 2, 3))
        earlier = jnp.arange(n_exp)[None, :] < jnp.arange(n_exp)[:, None]
        ahead = (load[:, None, :] > load[:, :, None]) | ((load[:, None, :] == load[:, :, None]) & earlier[None])
        rank = jnp.sum(ahead.astype(jnp.int32), axis=2)
        by_rank = jnp.sum(jnp.where(rank[:, None, :] == jnp.arange(n_exp)[None, :, None], jnp.arange(n_exp), 0), axis=2).astype(jnp.int32)
        home_of = [-1] * (NG - 1) + [-2] + [0] * (n_exp - NG)
        local_of = list(range(n_exp))
        for side, ranks in enumerate(SIDE_RANKS[NG]):
            for j, k in enumerate(ranks):
                home_of[k], local_of[k] = side, NG + j
        home = pick(jnp.array(home_of), rank, n_exp)
        local = pick(jnp.array(local_of), rank, n_exp)
        at_home = jnp.sum(jnp.where(hits, home[None, :, None, None, :], 0), axis=-1)
        lend = [n_dev // 2 if l % 2 == 0 else n_dev // 4 for l in range(n_layers)]
        share = [n_dev // 4 if l % 2 == 0 else n_dev // 2 for l in range(n_layers)]
        side_of = jnp.stack([(jnp.arange(n_dev) // bit) % 2 for bit in lend], axis=1)
        mine_side = jnp.stack([(me // bit) % 2 for bit in lend])
        needs = [jnp.any(at_home == v, axis=2) for v in (0, 1)]
        late = jnp.any(at_home == -2, axis=2)
        lent = jnp.where(side_of[:, :, None] == 0, needs[1], needs[0])
        n_lent = jnp.sum(lent.astype(jnp.int32), axis=2)
        ok = jnp.all(n_lent <= CAP) & ~jnp.any(needs[0] & needs[1]) & ~jnp.any(lent & late)

        def adaptive(x, norm_w, router_w, w_gate, w_up, w_down, ids):
            mine = lax.dynamic_index_in_dim(every, me, 0, keepdims=False)
            my_local = jnp.sum(jnp.where(mine[..., None] == jnp.arange(n_exp), local[:, None, None, :], 0), axis=-1)
            my_lent = lax.dynamic_index_in_dim(lent, me, 0, keepdims=False)
            sides = [jnp.array(r) for r in SIDE_RANKS[NG]]
            ones = (1,) * (NG - 1)
            chosen = [[jnp.where(mine_side[l] == v, by_rank[l][sides[0]], by_rank[l][sides[1]]) for v in (0, 1)] for l in range(n_layers)]

            def gathers(l, heavy, light):
                first = prep(l, heavy[:1], (1,), w_gate, w_up, w_down)
                rest = prep(l, jnp.concatenate([heavy[1:NG], light]), ones + (n_light, n_light), w_gate, w_up, w_down)
                return [lax.all_gather(w[0], "fsdp") for w in first + rest[:NG - 1]], *rest[NG - 1:]

            full, own, other = gathers(0, by_rank[0], jnp.concatenate(chosen[0]))
            own_x, sent = hop(own, share[0]), hop(other, lend[0])
            for l in range(n_layers):
                key = jnp.where(my_lent[l], 0, 8192) + jnp.arange(n_tok, dtype=jnp.int32)
                code = (my_local[l, 0] * 16 + my_local[l, 1]) * 64 + mine[l, 0] * 8 + mine[l, 1]
                code = jnp.where(my_lent[l], code, (n_local * 16 + n_local) * 64)
                key, code = lax.sort((key, code), num_keys=1)
                place = jnp.minimum(prefix(my_lent[l][:, None])[0][:, 0], CAP - 1)
                code = hop(code[:CAP], lend[l])
                ids0 = jnp.concatenate([mine[l, 0], code // 8 % 8])
                ids1 = jnp.concatenate([mine[l, 1], code % 8])
                slot0 = jnp.concatenate([jnp.where(my_lent[l], n_local, my_local[l, 0]), code // 1024])
                slot1 = jnp.concatenate([jnp.where(my_lent[l], n_local, my_local[l, 1]), code // 64 % 16])
                token, pos0, pos1, scalars = row_plan(slot0, slot1, n_local)
                guest = hop(take(x, (key & 8191)[:CAP]), lend[l])
                both = jnp.concatenate([x, guest])
                h, g0, g1 = norm_gates(both, norm_w[l], router_w[l], ids0, ids1)
                rows = take(h, token)
                max_tiles = (n_tok + CAP) // TM
                whole = [(0, p) for p in range(n_dev)]
                gathered = lambda k, out: expert(scalars[k], rows, [full[k]], whole, out, max_tiles, rows.shape[0])
                if l:
                    far = hop(sent, share[l])
                    beside = [hop(w, 1) for w in (own, own_x, sent)]
                    out = gathered(0, None)
                else:
                    out = gathered(0, None)
                    own_x, sent, out = lax.optimization_barrier((own_x, sent, out))
                    far = hop(sent, share[l])
                    beside = [hop(w, 1) for w in (own, own_x, sent)]
                if l + 1 < n_layers:
                    heavy, light, out = lax.optimization_barrier((by_rank[l + 1], jnp.concatenate(chosen[l + 1]), out))
                    coming, own2, other2 = gathers(l + 1, heavy, light)
                for k in range(1, NG - 1):
                    out = gathered(k, out)
                far, out = lax.optimization_barrier((far, out))
                eight = [own, own_x, sent, far] + beside + [hop(far, 1)]
                if l + 1 < n_layers:
                    own2, other2, _ = lax.optimization_barrier((own2, other2, far))
                    own_x2, sent2 = hop(own2, share[l + 1]), hop(other2, lend[l + 1])
                for j in range(n_light):
                    out = expert(scalars[NG + j], rows, eight, [(p, j) for p in range(n_dev)], out, max_tiles, rows.shape[0])
                last = NG - 1
                here0, here1 = slot0 != last, slot1 != last
                part = both.astype(jnp.float32) + (weighed(out, pos0, g0, here0) + weighed(out, pos1, g1, here1))
                back = hop(part[n_tok:].astype(jnp.bfloat16), lend[l])
                part = jnp.where(my_lent[l][:, None], take(back, place).astype(jnp.float32), part[:n_tok])
                part, late_full = lax.optimization_barrier((part, full[last]))
                at_last = scalars[last] * jnp.array([1, 1, 0])
                final = expert(at_last, rows, [late_full], whole, None, max_tiles, n_tok)
                use0, use1 = ~here0[:n_tok], ~here1[:n_tok]
                pos = jnp.where(use0, pos0[:n_tok], pos1[:n_tok]) - scalars[last, 0] * TM
                gate = jnp.where(use0[:, None], g0[:n_tok], g1[:n_tok])
                x = (part + weighed(final, pos, gate, use0 | use1)).astype(jnp.bfloat16)
                if l + 1 < n_layers:
                    x, own_x2, sent2 = lax.optimization_barrier((x, own_x2, sent2))
                    full, own, own_x, sent = coming, own2, own_x2, sent2
            return x

        return lax.cond(ok, adaptive, general, tokens, norm_w, router_w, w_gate, w_up, w_down, ids)

    row_spec = P(("rep", "fsdp"), None)
    col_spec = P(None, None, None, "fsdp")
    return jax.shard_map(
        local_fn,
        mesh=mesh,
        in_specs=(row_spec, P(), P(), col_spec, col_spec, P(None, None, "fsdp", None), P(None, ("rep", "fsdp"), None)),
        out_specs=row_spec,
        check_vma=False,
    )
```

time: 2780 us -> 2550 us (0.917)
  local copies, waits for them, and re-layouts: 924 us -> 499 us
  Pallas kernels: 571 us -> 808 us
  other arithmetic: 471 us -> 331 us
  waiting for transfers between devices: 761 us -> 816 us
    pallas_call x0 -> x16, Pallas kernels: none -> 808 us  [the longest x12 656 us: expert(): pl.pallas_call(functools.partial(expert_body, pieces, len(weights), alias...]
    ppermute x0 -> x20, waiting for transfers between devices: none -> 688 us  [hop(): return lax.ppermute(a, 'fsdp', [(i, i ^ bit) for i in range(n_dev)])]
    all_gather x6 -> x8, waiting for transfers between devices: 759 us -> 126 us  [gathers(): lax.all_gather(w[0], 'fsdp')]
    all_gather x6 -> x0, local copies, waits for them, and re-layouts: 606 us -> none  [the longest x2 229 us: local_fn(): gate_full = lax.all_gather(w_gate[layer_idx], 'fsdp', axis=2, tiled=True)]
    another operation x6 -> x0, Pallas kernels: 568 us -> none
    scatter-add x2 -> x0, other arithmetic: 236 us -> none  [expert_ffn(): return jax.ops.segment_sum(weighted, tok_of_row, num_segments=n_tok)]
    gather x10 -> x16, local copies, waits for them, and re-layouts: 261 us -> 486 us  [the longest x12 483 us: take(): return table.at[index].get(mode='promise_in_bounds')]
    add x0 -> x4, other arithmetic: none -> 100 us  [the longest x2 100 us: adaptive(): both.astype(jnp.float32)]
  transfers between devices with their start and end apart: 6 -> 28, of which waited for: 4 -> 9; matrix products, arithmetic and copies ran while one was open for 41% -> 31% of each run, Pallas kernels for 17% -> 29%
where the time goes in v1:
time: 2550 us; the launch traced here: 2540 us
  waiting for transfers between devices  816 us (32%)
  Pallas kernels  808 us (32%)
  local copies, waits for them, and re-layouts  499 us (20%)
  other arithmetic  331 us (13%)
  starting transfers between devices  25.7 us (1%)
    ppermute x20, waiting for transfers between devices, hop(): return lax.ppermute(a, 'fsdp', [(i, i ^ bit) for i in range(n_dev)])  688 us
    pallas_call x12, Pallas kernels, expert(): pl.pallas_call(functools.partial(expert_body, pieces, len(weights), alias...  656 us
    gather x12, local copies, waits for them, and re-layouts, take(): return table.at[index].get(mode='promise_in_bounds')  483 us
    pallas_call x4, Pallas kernels, prep(): pl.pallas_call(functools.partial(prep_body, groups, n_exp), out_shape=[ja...  153 us
    all_gather x8, waiting for transfers between devices, gathers(): lax.all_gather(w[0], 'fsdp')  126 us
    add x2, other arithmetic, adaptive(): both.astype(jnp.float32)  100 us
    select_n x2, other arithmetic, adaptive(): jnp.where(my_lent[l][:, None], take(back, place).astype(jnp.float32), par...  58.8 us
    convert_element_type x2, other arithmetic, adaptive(): x = (part + weighed(final, pos, gate, use0 | use1)).astype(jnp.bfloat16)  56.1 us
  transfers between devices with their start and end apart: 28, of which 9 were waited for; matrix products, arithmetic and copies ran while one was open for 31% of the time, Pallas kernels for 29%

profile of v1, /device:TPU:0, one launch (start us, length us, event | category | flops | bytes accessed | tf_op | source)
XLA Modules:
  0.0 2540.8 jit_solution(11922064164168956986)
XLA Ops:
  6.5 14.4 all-gather
  23.5 1.4 and_reduce_fusion
  28.5 2505.2 %conditional.1 = (bf16[2048,4096]{1,0:T(8,128)(2,1)}) conditional(s32[]{:T(128)} %convert_element_type.245, (bf16[2048,4096]{1,0:T(8,128)(2,1)}, s32[2,2,2048]{2,1,0:T(2,128)}, f32[2,4096]{1,0:T(2,128)}, bf16[2,4096,8]{1,2,0:T(8,128)(2,1)}, bf16[2,8,4096,172]{2,1,3,0:T(8,128)(2,1)}, /*index=5*/bf16[2,8,4096,172]{2,1,3,0:T(8,128)(2,1)}, ...), branch_computations={%region_11.34_spmd, %region_34.60_spmd} | conditional | flops 46453825536 | bytes 4033207552 | solution.py:327
  33.5 21.3 prep.15
  57.0 54.7 %prep.14 = (bf16[1,3,176,4096]{3,2,1,0:T(8,128)(2,1)}, bf16[1,3,176,4096]{3,2,1,0:T(8,128)(2,1)}, bf16[1,3,176,4096]{3,2,1,0:T(8,128)(2,1)}, bf16[2,3,176,4096]{3,2,1,0:T(8,128)(2,1)}, bf16[2,3,176,4096]{3,2,1,0:T(8,128)(2,1)}) custom-call(s32[7]{0:T(128)} %pad_add_fusion.10.s_ref, bf16[2,1376,4096]{2,1,0:T(8,128)(2,1)} %bitcast.304, ...), custom_call_target="tpu_custom_call" | custom-call | flops 4200000000 | bytes 100100000 | tf_op jit(solution)/shard_map/cond/branch_1_fun/prep/pallas_call | solution.py:49
  115.5 5.1 sort.98
  120.9 5.1 sort.100
  126.0 1.3 collective-permute-start.13
  127.3 13.1 gather_fusion
  141.2 1.8 collective-permute-start.2
  147.9 6.8 sort.99
  157.6 0.9 multiply_reduce_fusion
  158.5 75.6 %collective-permute-done = bf16[256,4096]{1,0:T(8,128)(2,1)S(1)} collective-permute-done((bf16[256,4096]{1,0:T(8,128)(2,1)}, bf16[256,4096]{1,0:T(8,128)(2,1)S(1)}, u32[]{:S(2)}, u32[]{:S(2)}) %collective-permute-start) | collective-permute-done | bytes 2097184 | tf_op jit(solution)/shard_map/cond/branch_1_fun/ppermute | solution.py:203
  234.1 14.1 fusion.47
  248.2 20.8 fusion.49
  269.1 91.7 %gather_fusion.1 = bf16[6144,4096]{1,0:T(8,128)(2,1)} fusion(bf16[2304,4096]{1,0:T(8,128)(2,1)} %fusion.49, s32[6144]{0:T(1024)S(1)} %fusion.80), kind=kCustom, calls=%fused_computation.7 | custom fusion | bytes 100687872 | tf_op jit(solution)/shard_map/cond/branch_1_fun/gather | solution.py:192
  360.9 124.2 %expert.22.refs_1_ = f32[6144,4096]{1,0:T(8,128)} custom-call(s32[3]{0:T(128)} %get-tuple-element.655.s_ref, bf16[6144,4096]{1,0:T(8,128)(2,1)} %gather_fusion.1, bf16[8,3,176,4096]{3,2,1,0:T(8,128)(2,1)} %all-gather.12.cloned.1.call-done.refs_0_), custom_call_target="tpu_custom_call" | custom-call | flops 3000000000 | bytes 60000000 | tf_op jit(solution)/shard_map/cond/branch_1_fun/expert/pallas_call | solution.py:128
  485.0 4.3 collective-permute-done.2.refs_1_
  489.3 89.9 %collective-permute-done.3.refs_2_ = bf16[2,3,176,4096]{3,2,1,0:T(8,128)(2,1)} collective-permute-done((bf16[2,3,176,4096]{3,2,1,0:T(8,128)(2,1)}, bf16[2,3,176,4096]{3,2,1,0:T(8,128)(2,1)}, u32[]{:S(2)}, u32[]{:S(2)}) %collective-permute-start.3) | collective-permute-done | bytes 8650784 | tf_op jit(solution)/shard_map/cond/branch_1_fun/ppermute | solution.py:203
  579.2 22.6 prep.17
  602.6 54.1 %prep.16 = (bf16[1,3,176,4096]{3,2,1,0:T(8,128)(2,1)}, bf16[1,3,176,4096]{3,2,1,0:T(8,128)(2,1)}, bf16[1,3,176,4096]{3,2,1,0:T(8,128)(2,1)}, bf16[2,3,176,4096]{3,2,1,0:T(8,128)(2,1)}, bf16[2,3,176,4096]{3,2,1,0:T(8,128)(2,1)}) custom-call(s32[7]{0:T(128)} %pad_add_fusion.12.s_ref, bf16[2,1376,4096]{2,1,0:T(8,128)(2,1)} %bitcast.306, ...), custom_call_target="tpu_custom_call" | custom-call | flops 4200000000 | bytes 100100000 | tf_op jit(solution)/shard_map/cond/branch_1_fun/prep/pallas_call | solution.py:49
  659.1 50.3 %expert.23.refs_1_ = f32[6144,4096]{1,0:T(8,128)} custom-call(s32[3]{0:T(128)} %get-tuple-element.653.s_ref, bf16[6144,4096]{1,0:T(8,128)(2,1)} %gather_fusion.1, bf16[8,3,176,4096]{3,2,1,0:T(8,128)(2,1)} %all-gather.16.cloned.1.call-done.refs_0_, f32[6144,4096]{1,0:T(8,128)} %expert.22.refs_1_), custom_call_target="tpu_custom_call", output_to_operand_aliasing={{}: (3, {})} | custom-call | flops 3000000000 | bytes 60000000 | tf_op jit(solution)/shard_map/cond/branch_1_fun/expert/pallas_call | solution.py:128
  709.4 125.6 %all-gather.14.cloned.1.call-done.refs_0_ = bf16[8,3,176,4096]{3,2,1,0:T(8,128)(2,1)} async-done(((bf16[1,3,176,4096]{3,2,1,0:T(8,128)(2,1)}), bf16[8,3,176,4096]{3,2,1,0:T(8,128)(2,1)}) %all-gather.14.cloned.1.call-update) | async-done | bytes 34603024 | tf_op jit(solution)/shard_map/cond/branch_1_fun/all_gather | solution.py:266
  835.1 52.7 %expert.24.refs_8_ = f32[6144,4096]{1,0:T(8,128)} custom-call(s32[3]{0:T(128)} %get-tuple-element.654.s_ref, bf16[6144,4096]{1,0:T(8,128)(2,1)} %gather_fusion.1, bf16[8,3,176,4096]{3,2,1,0:T(8,128)(2,1)} %all-gather.14.cloned.1.call-done.refs_0_, f32[6144,4096]{1,0:T(8,128)} %expert.23.refs_1_), custom_call_target="tpu_custom_call", output_to_operand_aliasing={{}: (3, {})} | custom-call | flops 3000000000 | bytes 60000000 | tf_op jit(solution)/shard_map/cond/branch_1_fun/expert/pallas_call | solution.py:128
  887.8 119.4 %collective-permute-done.4.refs_3_ = bf16[2,3,176,4096]{3,2,1,0:T(8,128)(2,1)} collective-permute-done((bf16[2,3,176,4096]{3,2,1,0:T(8,128)(2,1)}, bf16[2,3,176,4096]{3,2,1,0:T(8,128)(2,1)}, u32[]{:S(2)}, u32[]{:S(2)}) %collective-permute-start.4) | collective-permute-done | bytes 8650784 | tf_op jit(solution)/shard_map/cond/branch_1_fun/ppermute | solution.py:203
  1010.2 11.5 select_reduce_fusion.9
  1023.1 38.0 %expert.25.refs_8_ = f32[6144,4096]{1,0:T(8,128)} custom-call(s32[3]{0:T(128)} %get-tuple-element.652.s_ref, bf16[6144,4096]{1,0:T(8,128)(2,1)} %gather_fusion.1, bf16[2,3,176,4096]{3,2,1,0:T(8,128)(2,1)} %get-tuple-element.396.refs_0_, bf16[2,3,176,4096]{3,2,1,0:T(8,128)(2,1)} %collective-permute-done.2.refs_1_, ...), custom_call_target="tpu_custom_call", output_to_operand_aliasing={{}: (10, {})} | custom-call | flops 3000000000 | bytes 60000000 | tf_op jit(solution)/shard_map/cond/branch_1_fun/expert/pallas_call | solution.py:128
  1061.1 26.0 %expert.26 = f32[6144,4096]{1,0:T(8,128)} custom-call(s32[3]{0:T(128)} %get-tuple-element.656.s_ref, bf16[6144,4096]{1,0:T(8,128)(2,1)} %gather_fusion.1, bf16[2,3,176,4096]{3,2,1,0:T(8,128)(2,1)} %get-tuple-element.396.refs_0_, bf16[2,3,176,4096]{3,2,1,0:T(8,128)(2,1)} %collective-permute-done.2.refs_1_, ...), custom_call_target="tpu_custom_call", output_to_operand_aliasing={{}: (10, {})} | custom-call | flops 3000000000 | bytes 60000000 | tf_op jit(solution)/shard_map/cond/branch_1_fun/expert/pallas_call | solution.py:128
  1087.2 39.7 %gather_fusion.6 = f32[2304,4096]{1,0:T(8,128)} fusion(f32[6144,4096]{1,0:T(8,128)} %expert.26, s32[3072]{0:T(1024)S(1)} %copy-done.57), kind=kCustom, calls=%fused_computation.12 | custom fusion | bytes 75506688 | tf_op jit(solution)/shard_map/cond/branch_1_fun/gather | solution.py:192
  1126.9 52.9 %gather_fusion.7 = f32[2304,4096]{1,0:T(8,128)} fusion(f32[6144,4096]{1,0:T(8,128)} %expert.26, s32[3072]{0:T(1024)S(1)} %copy-done.58), kind=kCustom, calls=%fused_computation.13 | custom fusion | bytes 75506688 | tf_op jit(solution)/shard_map/cond/branch_1_fun/gather | solution.py:192
  1179.9 50.1 %convert_add_fusion.5 = f32[2304,4096]{1,0:T(8,128)} fusion(f32[2304,4096]{1,0:T(8,128)} %gather_fusion.7, f32[2304,4096]{1,0:T(8,128)} %gather_fusion.6, f32[2304]{0:T(1024)S(1)} %copy-done.64, f32[2304]{0:T(1024)S(1)} %copy-done.63, pred[2304]{0:T(1024)(128)(4,1)S(1)} %copy-done.78, pred[2304]{0:T(1024)(128)(4,1)S(1)} %copy-done.67, ...), kind=kLoop, calls=%fused_computation.155 | loop fusion | flops 94371840 | bytes 132143616 | tf_op jit(solution)/shard_map/cond/branch_1_fun/add | solution.py:312
  1229.9 2.5 slice.500
  1232.4 3.6 collective-permute-start.9
  1239.4 76.3 %collective-permute-done.9 = bf16[256,4096]{1,0:T(8,128)(2,1)S(1)} collective-permute-done((bf16[256,4096]{1,0:T(8,128)(2,1)S(1)}, bf16[256,4096]{1,0:T(8,128)(2,1)S(1)}, u32[]{:S(2)}, u32[]{:S(2)}) %collective-permute-start.9) | collective-permute-done | bytes 2097184 | tf_op jit(solution)/shard_map/cond/branch_1_fun/ppermute | solution.py:203
  1315.8 14.2 gather_fusion.8
  1330.0 31.2 %slice_select_fusion.1 = f32[2048,4096]{1,0:T(8,128)} fusion(f32[2304,4096]{1,0:T(8,128)} %convert_add_fusion.5, bf16[2048,4096]{1,0:T(8,128)(2,1)} %gather_fusion.8, pred[2048]{0:T(1024)(128)(4,1)S(1)} %copy-done.56), kind=kLoop, calls=%fused_computation.165 | loop fusion | flops 16777216 | bytes 83888128 | tf_op jit(solution)/shard_map/cond/branch_1_fun/jit(_where)/select_n | solution.py:314
  1361.2 37.8 %expert.27 = f32[2048,4096]{1,0:T(8,128)} custom-call(s32[3]{0:T(128)} %get-tuple-element.651.s_ref, bf16[6144,4096]{1,0:T(8,128)(2,1)} %gather_fusion.1, bf16[8,3,176,4096]{3,2,1,0:T(8,128)(2,1)} %all-gather.18.cloned.1.call-done.refs_0_), custom_call_target="tpu_custom_call" | custom-call | flops 3000000000 | bytes 60000000 | tf_op jit(solution)/shard_map/cond/branch_1_fun/expert/pallas_call | solution.py:128
  1399.0 38.1 %gather_fusion.9 = f32[2048,4096]{1,0:T(8,128)} fusion(f32[2048,4096]{1,0:T(8,128)} %expert.27, s32[2048]{0:T(1024)S(1)} %get-tuple-element.702), kind=kCustom, calls=%fused_computation.15 | custom fusion | bytes 67117056 | tf_op jit(solution)/shard_map/cond/branch_1_fun/gather | solution.py:192
  1437.2 28.5 %add_convert_fusion.1 = bf16[2048,4096]{1,0:T(8,128)(2,1)} fusion(f32[2048,4096]{1,0:T(8,128)} %slice_select_fusion.1, f32[2048,4096]{1,0:T(8,128)} %gather_fusion.9, f32[2048]{0:T(1024)S(1)} %bitcast.366, pred[2048]{0:T(1024)(128)(4,1)S(1)} %copy-done.87), kind=kLoop, calls=%fused_computation.167 | loop fusion | flops 33554432 | bytes 83896320 | tf_op jit(solution)/shard_map/cond/branch_1_fun/convert_element_type | solution.py:321
  1465.7 192.3 %collective-permute-done.10.refs_1_ = bf16[2,3,176,4096]{3,2,1,0:T(8,128)(2,1)} collective-permute-done((bf16[2,3,176,4096]{3,2,1,0:T(8,128)(2,1)}, bf16[2,3,176,4096]{3,2,1,0:T(8,128)(2,1)}, u32[]{:S(2)}, u32[]{:S(2)}) %collective-permute-start.10) | collective-permute-done | bytes 8650784 | tf_op jit(solution)/shard_map/cond/branch_1_fun/ppermute | solution.py:203
  1658.0 2.5 collective-permute-start.14
  1661.2 13.2 gather_fusion.10
  1674.4 6.8 sort.101
  1682.4 85.5 %collective-permute-done.12 = bf16[256,4096]{1,0:T(8,128)(2,1)S(1)} collective-permute-done((bf16[256,4096]{1,0:T(8,128)(2,1)}, bf16[256,4096]{1,0:T(8,128)(2,1)S(1)}, u32[]{:S(2)}, u32[]{:S(2)}) %collective-permute-start.12) | collective-permute-done | bytes 2097184 | tf_op jit(solution)/shard_map/cond/branch_1_fun/ppermute | solution.py:203
  1767.9 13.7 fusion.50
  1781.6 21.2 fusion.52
  1802.8 91.9 %gather_fusion.11 = bf16[6144,4096]{1,0:T(8,128)(2,1)} fusion(bf16[2304,4096]{1,0:T(8,128)(2,1)} %fusion.52, s32[6144]{0:T(1024)S(1)} %fusion.81), kind=kCustom, calls=%fused_computation.17 | custom fusion | bytes 100687872 | tf_op jit(solution)/shard_map/cond/branch_1_fun/gather | solution.py:192
  1894.8 124.1 %expert.28.refs_1_ = f32[6144,4096]{1,0:T(8,128)} custom-call(s32[3]{0:T(128)} %get-tuple-element.647.s_ref, bf16[6144,4096]{1,0:T(8,128)(2,1)} %gather_fusion.11, bf16[8,3,176,4096]{3,2,1,0:T(8,128)(2,1)} %all-gather.24.cloned.1.call-done.refs_0_), custom_call_target="tpu_custom_call" | custom-call | flops 3000000000 | bytes 60000000 | tf_op jit(solution)/shard_map/cond/branch_1_fun/expert/pallas_call | solution.py:128
  2019.0 50.6 %expert.29.refs_1_ = f32[6144,4096]{1,0:T(8,128)} custom-call(s32[3]{0:T(128)} %get-tuple-element.648.s_ref, bf16[6144,4096]{1,0:T(8,128)(2,1)} %gather_fusion.11, bf16[8,3,176,4096]{3,2,1,0:T(8,128)(2,1)} %all-gather.22.cloned.1.call-done.refs_0_, f32[6144,4096]{1,0:T(8,128)} %expert.28.refs_1_), custom_call_target="tpu_custom_call", output_to_operand_aliasing={{}: (3, {})} | custom-call | flops 3000000000 | bytes 60000000 | tf_op jit(solution)/shard_map/cond/branch_1_fun/expert/pallas_call | solution.py:128
  2069.8 50.8 %expert.30.refs_8_ = f32[6144,4096]{1,0:T(8,128)} custom-call(s32[3]{0:T(128)} %get-tuple-element.649.s_ref, bf16[6144,4096]{1,0:T(8,128)(2,1)} %gather_fusion.11, bf16[8,3,176,4096]{3,2,1,0:T(8,128)(2,1)} %all-gather.20.cloned.1.call-done.refs_0_, f32[6144,4096]{1,0:T(8,128)} %expert.29.refs_1_), custom_call_target="tpu_custom_call", output_to_operand_aliasing={{}: (3, {})} | custom-call | flops 3000000000 | bytes 60000000 | tf_op jit(solution)/shard_map/cond/branch_1_fun/expert/pallas_call | solution.py:128
  2120.6 11.9 collective-permute-start.18
  2135.5 11.3 select_reduce_fusion.7
  2148.2 37.9 %expert.31.refs_8_ = f32[6144,4096]{1,0:T(8,128)} custom-call(s32[3]{0:T(128)} %get-tuple-element.646.s_ref, bf16[6144,4096]{1,0:T(8,128)(2,1)} %gather_fusion.11, bf16[2,3,176,4096]{3,2,1,0:T(8,128)(2,1)} %get-tuple-element.415.refs_0_, bf16[2,3,176,4096]{3,2,1,0:T(8,128)(2,1)} %collective-permute-done.10.refs_1_, ...), custom_call_target="tpu_custom_call", output_to_operand_aliasing={{}: (10, {})} | custom-call | flops 3000000000 | bytes 60000000 | tf_op jit(solution)/shard_map/cond/branch_1_fun/expert/pallas_call | solution.py:128
  2186.1 25.4 %expert.32 = f32[6144,4096]{1,0:T(8,128)} custom-call(s32[3]{0:T(128)} %get-tuple-element.650.s_ref, bf16[6144,4096]{1,0:T(8,128)(2,1)} %gather_fusion.11, bf16[2,3,176,4096]{3,2,1,0:T(8,128)(2,1)} %get-tuple-element.415.refs_0_, bf16[2,3,176,4096]{3,2,1,0:T(8,128)(2,1)} %collective-permute-done.10.refs_1_, ...), custom_call_target="tpu_custom_call", output_to_operand_aliasing={{}: (10, {})} | custom-call | flops 3000000000 | bytes 60000000 | tf_op jit(solution)/shard_map/cond/branch_1_fun/expert/pallas_call | solution.py:128
  2211.6 37.3 %gather_fusion.12 = f32[2304,4096]{1,0:T(8,128)} fusion(f32[6144,4096]{1,0:T(8,128)} %expert.32, s32[3072]{0:T(1024)S(1)} %copy-done.59), kind=kCustom, calls=%fused_computation.18 | custom fusion | bytes 75506688 | tf_op jit(solution)/shard_map/cond/branch_1_fun/gather | solution.py:192
  2248.9 38.9 %gather_fusion.13 = f32[2304,4096]{1,0:T(8,128)} fusion(f32[6144,4096]{1,0:T(8,128)} %expert.32, s32[3072]{0:T(1024)S(1)} %copy-done.60), kind=kCustom, calls=%fused_computation.19 | custom fusion | bytes 75506688 | tf_op jit(solution)/shard_map/cond/branch_1_fun/gather | solution.py:192
  2287.9 49.9 %convert_add_fusion.4 = f32[2304,4096]{1,0:T(8,128)} fusion(f32[2304,4096]{1,0:T(8,128)} %gather_fusion.13, f32[2304,4096]{1,0:T(8,128)} %gather_fusion.12, f32[2304]{0:T(1024)S(1)} %copy-done.62, f32[2304]{0:T(1024)S(1)} %copy-done.61, pred[2304]{0:T(1024)(128)(4,1)S(1)} %copy-done.77, pred[2304]{0:T(1024)(128)(4,1)S(1)} %copy-done.68, ...), kind=kLoop, calls=%fused_computation.152 | loop fusion | flops 94371840 | bytes 132143616 | tf_op jit(solution)/shard_map/cond/branch_1_fun/add | solution.py:312
  2337.8 2.5 slice.499
  2343.1 45.0 %collective-permute-done.19 = bf16[256,4096]{1,0:T(8,128)(2,1)S(1)} collective-permute-done((bf16[256,4096]{1,0:T(8,128)(2,1)S(1)}, bf16[256,4096]{1,0:T(8,128)(2,1)S(1)}, u32[]{:S(2)}, u32[]{:S(2)}) %collective-permute-start.19) | collective-permute-done | bytes 2097184 | tf_op jit(solution)/shard_map/cond/branch_1_fun/ppermute | solution.py:203
  2388.0 14.0 gather_fusion.14
  2402.0 27.6 %slice_select_fusion = f32[2048,4096]{1,0:T(8,128)} fusion(f32[2304,4096]{1,0:T(8,128)} %convert_add_fusion.4, bf16[2048,4096]{1,0:T(8,128)(2,1)} %gather_fusion.14, pred[2048]{0:T(1024)(128)(4,1)S(1)} %copy-done.54), kind=kLoop, calls=%fused_computation.164 | loop fusion | flops 16777216 | bytes 83888128 | tf_op jit(solution)/shard_map/cond/branch_1_fun/jit(_where)/select_n | solution.py:314
  2429.6 37.9 %expert.33 = f32[2048,4096]{1,0:T(8,128)} custom-call(s32[3]{0:T(128)} %get-tuple-element.645.s_ref, bf16[6144,4096]{1,0:T(8,128)(2,1)} %gather_fusion.11, bf16[8,3,176,4096]{3,2,1,0:T(8,128)(2,1)} %all-gather.26.cloned.1.call-done.refs_0_), custom_call_target="tpu_custom_call" | custom-call | flops 3000000000 | bytes 60000000 | tf_op jit(solution)/shard_map/cond/branch_1_fun/expert/pallas_call | solution.py:128
  2467.6 38.3 %gather_fusion.15 = f32[2048,4096]{1,0:T(8,128)} fusion(f32[2048,4096]{1,0:T(8,128)} %expert.33, s32[2048]{0:T(1024)S(1)} %get-tuple-element.694), kind=kCustom, calls=%fused_computation.21 | custom fusion | bytes 67117056 | tf_op jit(solution)/shard_map/cond/branch_1_fun/gather | solution.py:192
  2505.8 27.6 %add_convert_fusion = bf16[2048,4096]{1,0:T(8,128)(2,1)} fusion(f32[2048,4096]{1,0:T(8,128)} %slice_select_fusion, f32[2048,4096]{1,0:T(8,128)} %gather_fusion.15, f32[2048]{0:T(1024)S(1)} %bitcast.365, pred[2048]{0:T(1024)(128)(4,1)S(1)} %copy-done.88), kind=kLoop, calls=%fused_computation.166 | loop fusion | flops 33554432 | bytes 83896320 | tf_op jit(solution)/shard_map/cond/branch_1_fun/convert_element_type | solution.py:321
  (356 shorter events, 38.7 us)
Async XLA Ops:
  32.1 328.8 %all-gather.12.cloned.1.call-start = ((), (), s32[]{:S(2)}) async-start(), calls=%async_computation | async-start | bytes 38928384 | tf_op jit(solution)/shard_map/cond/branch_1_fun/all_gather | solution.py:266
  54.8 604.3 %all-gather.16.cloned.1.call-start = ((), (), s32[]{:S(2)}) async-start(), calls=%async_computation.2 | async-start | bytes 38928384 | tf_op jit(solution)/shard_map/cond/branch_1_fun/all_gather | solution.py:266
  54.9 88.9 %copy-start.2 = (s32[8]{0:T(128)}, s32[8]{0:T(128)S(1)}, u32[]{:S(2)}) copy-start(s32[8]{0:T(128)S(1)} %get-tuple-element.411) | copy-start | bytes 100 | tf_op jit(solution)/shard_map/cond
  111.7 723.3 %all-gather.14.cloned.1.call-start = ((), (), s32[]{:S(2)}) async-start(), calls=%async_computation.1 | async-start | bytes 38928384 | tf_op jit(solution)/shard_map/cond/branch_1_fun/all_gather | solution.py:266
  112.5 1248.7 %all-gather.18.cloned.1.call-start = ((), (), s32[]{:S(2)}) async-start(), calls=%async_computation.3 | async-start | bytes 38928384 | tf_op jit(solution)/shard_map/cond/branch_1_fun/all_gather | solution.py:266
  113.0 1781.7 %all-gather.24.cloned.1.call-start = ((), (), s32[]{:S(2)}) async-start(), calls=%async_computation.6 | async-start | bytes 38928384 | tf_op jit(solution)/shard_map/cond/branch_1_fun/all_gather | solution.py:266
  114.4 154.6 %copy-start.52 = (pred[2048]{0:T(1024)(128)(4,1)}, pred[2048]{0:T(1024)(128)(4,1)S(1)}, u32[]{:S(2)}) copy-start(pred[2048]{0:T(1024)(128)(4,1)S(1)} %get-tuple-element.634) | copy-start | bytes 6148 | tf_op jit(solution)/shard_map/cond
  114.4 154.6 %copy-start.55 = (pred[2048]{0:T(1024)(128)(4,1)}, pred[2048]{0:T(1024)(128)(4,1)S(1)}, u32[]{:S(2)}) copy-start(pred[2048]{0:T(1024)(128)(4,1)S(1)} %get-tuple-element.633) | copy-start | bytes 6148 | tf_op jit(solution)/shard_map/cond
  115.4 153.7 %copy-start.38 = (s32[1,1,2048]{2,1,0:T(1,128)}, s32[1,1,2048]{2,1,0:T(1,128)S(1)}, u32[]{:S(2)}) copy-start(s32[1,1,2048]{2,1,0:T(1,128)S(1)} %get-tuple-element.733) | copy-start | bytes 24580 | tf_op jit(solution)/shard_map/cond
  115.4 153.7 %copy-start.40 = (s32[1,1,2048]{2,1,0:T(1,128)}, s32[1,1,2048]{2,1,0:T(1,128)S(1)}, u32[]{:S(2)}) copy-start(s32[1,1,2048]{2,1,0:T(1,128)S(1)} %get-tuple-element.734) | copy-start | bytes 24580 | tf_op jit(solution)/shard_map/cond
  115.4 153.7 %copy-start.42 = (s32[1,1,2048]{2,1,0:T(1,128)}, s32[1,1,2048]{2,1,0:T(1,128)S(1)}, u32[]{:S(2)}) copy-start(s32[1,1,2048]{2,1,0:T(1,128)S(1)} %get-tuple-element.735) | copy-start | bytes 24580 | tf_op jit(solution)/shard_map/cond
  115.4 153.7 %copy-start.44 = (s32[1,1,2048]{2,1,0:T(1,128)}, s32[1,1,2048]{2,1,0:T(1,128)S(1)}, u32[]{:S(2)}) copy-start(s32[1,1,2048]{2,1,0:T(1,128)S(1)} %get-tuple-element.732) | copy-start | bytes 24580 | tf_op jit(solution)/shard_map/cond
  115.5 153.6 %copy-start.23 = (s32[2048]{0:T(1024)}, s32[2048]{0:T(1024)S(1)}, u32[]{:S(2)}) copy-start(s32[2048]{0:T(1024)S(1)} %get-tuple-element.709) | copy-start | bytes 24580 | tf_op jit(solution)/shard_map/cond
  120.6 25.2 collective-permute-start.1
  120.9 148.2 %copy-start.21 = (s32[2048]{0:T(1024)}, s32[2048]{0:T(1024)S(1)}, u32[]{:S(2)}) copy-start(s32[2048]{0:T(1024)S(1)} %get-tuple-element.701) | copy-start | bytes 24580 | tf_op jit(solution)/shard_map/cond
  126.0 19.8 collective-permute-start.13
  140.4 93.6 %collective-permute-start = (bf16[256,4096]{1,0:T(8,128)(2,1)}, bf16[256,4096]{1,0:T(8,128)(2,1)S(1)}, u32[]{:S(2)}, u32[]{:S(2)}) collective-permute-start(bf16[256,4096]{1,0:T(8,128)(2,1)} %gather_fusion), channel_id=1, source_target_pairs={{0,4},{1,5},{2,6},{3,7},{4,0},{5,1},{6,2},{7,3}} | collective-permute-start | bytes 6291464 | tf_op jit(solution)/shard_map/cond/branch_1_fun/ppermute | solution.py:203
  141.2 348.2 %collective-permute-start.2 = (bf16[2,3,176,4096]{3,2,1,0:T(8,128)(2,1)}, bf16[2,3,176,4096]{3,2,1,0:T(8,128)(2,1)}, u32[]{:S(2)}, u32[]{:S(2)}) collective-permute-start(bf16[2,3,176,4096]{3,2,1,0:T(8,128)(2,1)} %get-tuple-element.396.refs_0_), channel_id=1, source_target_pairs={{0,2},{1,3},{2,0},{3,1},{4,6},{5,7},{6,4},{7,5}} | collective-permute-start | bytes 25952264 | tf_op jit(solution)/shard_map/cond/branch_1_fun/ppermute | solution.py:203
  143.0 436.2 %collective-permute-start.3 = (bf16[2,3,176,4096]{3,2,1,0:T(8,128)(2,1)}, bf16[2,3,176,4096]{3,2,1,0:T(8,128)(2,1)}, u32[]{:S(2)}, u32[]{:S(2)}) collective-permute-start(bf16[2,3,176,4096]{3,2,1,0:T(8,128)(2,1)} %get-tuple-element.397), channel_id=1, source_target_pairs={{0,4},{1,5},{2,6},{3,7},{4,0},{5,1},{6,2},{7,3}} | collective-permute-start | bytes 25952264 | tf_op jit(solution)/shard_map/cond/branch_1_fun/ppermute | solution.py:203
  154.9 206.0 %copy-start.103 = (s32[6]{0:T(128)}, s32[6]{0:T(128)S(1)}, u32[]{:S(2)}) copy-start(s32[6]{0:T(128)S(1)} %select_reduce_fusion.14) | copy-start | bytes 76 | tf_op jit(solution)/shard_map/cond
  155.5 78.6 %copy-start.79 = (s32[256]{0:T(256)}, s32[256]{0:T(256)S(1)}, u32[]{:S(2)}) copy-start(s32[256]{0:T(256)S(1)} %get-tuple-element.746) | copy-start | bytes 3076 | tf_op jit(solution)/shard_map/cond
  155.5 78.6 %copy-start.81 = (s32[256]{0:T(256)}, s32[256]{0:T(256)S(1)}, u32[]{:S(2)}) copy-start(s32[256]{0:T(256)S(1)} %get-tuple-element.747) | copy-start | bytes 3076 | tf_op jit(solution)/shard_map/cond
  155.5 205.4 %copy-start.65 = (s32[6144]{0:T(1024)}, s32[6144]{0:T(1024)S(1)}, u32[]{:S(2)}) copy-start(s32[6144]{0:T(1024)S(1)} %get-tuple-element.745) | copy-start | bytes 73732 | tf_op jit(solution)/shard_map/cond
  234.1 126.7 %copy-start.5 = (bf16[256,4096]{1,0:T(8,128)(2,1)}, bf16[256,4096]{1,0:T(8,128)(2,1)S(1)}, u32[]{:S(2)}) copy-start(bf16[256,4096]{1,0:T(8,128)(2,1)S(1)} %collective-permute-done) | copy-start | bytes 6291460 | tf_op jit(solution)/shard_map/cond
  601.9 1417.1 %all-gather.22.cloned.1.call-start = ((), (), s32[]{:S(2)}) async-start(), calls=%async_computation.5 | async-start | bytes 38928384 | tf_op jit(solution)/shard_map/cond/branch_1_fun/all_gather | solution.py:266
  656.7 1412.9 %all-gather.20.cloned.1.call-start = ((), (), s32[]{:S(2)}) async-start(), calls=%async_computation.4 | async-start | bytes 38928384 | tf_op jit(solution)/shard_map/cond/branch_1_fun/all_gather | solution.py:266
  657.5 1772.2 %all-gather.26.cloned.1.call-start = ((), (), s32[]{:S(2)}) async-start(), calls=%async_computation.7 | async-start | bytes 38928384 | tf_op jit(solution)/shard_map/cond/branch_1_fun/all_gather | solution.py:266
  657.7 349.5 %collective-permute-start.4 = (bf16[2,3,176,4096]{3,2,1,0:T(8,128)(2,1)}, bf16[2,3,176,4096]{3,2,1,0:T(8,128)(2,1)}, u32[]{:S(2)}, u32[]{:S(2)}) collective-permute-start(bf16[2,3,176,4096]{3,2,1,0:T(8,128)(2,1)} %collective-permute-done.3.refs_2_), channel_id=1, source_target_pairs={{0,2},{1,3},{2,0},{3,1},{4,6},{5,7},{6,4},{7,5}} | collective-permute-start | bytes 25952264 | tf_op jit(solution)/shard_map/cond/branch_1_fun/ppermute | solution.py:203
  658.6 364.5 %collective-permute-start.5 = (bf16[2,3,176,4096]{3,2,1,0:T(8,128)(2,1)}, bf16[2,3,176,4096]{3,2,1,0:T(8,128)(2,1)}, u32[]{:S(2)}, u32[]{:S(2)}) collective-permute-start(bf16[2,3,176,4096]{3,2,1,0:T(8,128)(2,1)} %get-tuple-element.396.refs_0_), channel_id=1, source_target_pairs={{0,1},{1,0},{2,3},{3,2},{4,5},{5,4},{6,7},{7,6}} | collective-permute-start | bytes 25952264 | tf_op jit(solution)/shard_map/cond/branch_1_fun/ppermute | solution.py:203
  658.6 364.5 %collective-permute-start.7 = (bf16[2,3,176,4096]{3,2,1,0:T(8,128)(2,1)}, bf16[2,3,176,4096]{3,2,1,0:T(8,128)(2,1)}, u32[]{:S(2)}, u32[]{:S(2)}) collective-permute-start(bf16[2,3,176,4096]{3,2,1,0:T(8,128)(2,1)} %collective-permute-done.3.refs_2_), channel_id=1, source_target_pairs={{0,1},{1,0},{2,3},{3,2},{4,5},{5,4},{6,7},{7,6}} | collective-permute-start | bytes 25952264 | tf_op jit(solution)/shard_map/cond/branch_1_fun/ppermute | solution.py:203
  659.1 364.0 %collective-permute-start.6 = (bf16[2,3,176,4096]{3,2,1,0:T(8,128)(2,1)}, bf16[2,3,176,4096]{3,2,1,0:T(8,128)(2,1)}, u32[]{:S(2)}, u32[]{:S(2)}) collective-permute-start(bf16[2,3,176,4096]{3,2,1,0:T(8,128)(2,1)} %collective-permute-done.2.refs_1_), channel_id=1, source_target_pairs={{0,1},{1,0},{2,3},{3,2},{4,5},{5,4},{6,7},{7,6}} | collective-permute-start | bytes 25952264 | tf_op jit(solution)/shard_map/cond/branch_1_fun/ppermute | solution.py:203
  835.0 172.2 %copy-start.29 = (s32[2048]{0:T(1024)S(1)}, s32[2048]{0:T(1024)}, u32[]{:S(2)}) copy-start(s32[2048]{0:T(1024)} %copy-done.28) | copy-start | bytes 24580 | tf_op jit(solution)/shard_map/cond
  835.1 172.2 %copy-start.84 = (s32[256]{0:T(256)S(1)}, s32[256]{0:T(256)}, u32[]{:S(2)}) copy-start(s32[256]{0:T(256)} %copy-done.83) | copy-start | bytes 3076 | tf_op jit(solution)/shard_map/cond
  835.1 172.8 %copy-start.24 = (s32[2048]{0:T(1024)S(1)}, s32[2048]{0:T(1024)}, u32[]{:S(2)}) copy-start(s32[2048]{0:T(1024)} %copy-done.23) | copy-start | bytes 24580 | tf_op jit(solution)/shard_map/cond
  835.1 172.8 %copy-start.86 = (s32[256]{0:T(256)S(1)}, s32[256]{0:T(256)}, u32[]{:S(2)}) copy-start(s32[256]{0:T(256)} %copy-done.85) | copy-start | bytes 3076 | tf_op jit(solution)/shard_map/cond
  835.1 173.4 %copy-start.104 = (s32[6]{0:T(128)S(1)}, s32[6]{0:T(128)}, u32[]{:S(2)}) copy-start(s32[6]{0:T(128)} %copy-done.103) | copy-start | bytes 76 | tf_op jit(solution)/shard_map/cond
  835.1 173.4 %copy-start.90 = (bf16[36,6]{0,1:T(8,128)(2,1)S(1)}, bf16[36,6]{0,1:T(8,128)(2,1)}, u32[]{:S(2)}) copy-start(bf16[36,6]{0,1:T(8,128)(2,1)} %get-tuple-element.637) | copy-start | bytes 1300 | tf_op jit(solution)/shard_map/cond
  835.1 173.5 %copy-start.33 = (s32[36,128]{1,0:T(8,128)S(1)}, s32[36,128]{1,0:T(8,128)}, u32[]{:S(2)}) copy-start(s32[36,128]{1,0:T(8,128)} %copy-done.32) | copy-start | bytes 55300 | tf_op jit(solution)/shard_map/cond
  835.1 175.0 %copy-start.45 = (s32[1,1,2048]{2,1,0:T(1,128)S(1)}, s32[1,1,2048]{2,1,0:T(1,128)}, u32[]{:S(2)}) copy-start(s32[1,1,2048]{2,1,0:T(1,128)} %copy-done.44) | copy-start | bytes 24580 | tf_op jit(solution)/shard_map/cond
  835.1 175.0 %copy-start.94 = (s32[256]{0:T(256)S(1)}, s32[256]{0:T(256)}, u32[]{:S(2)}) copy-start(s32[256]{0:T(256)} %get-tuple-element.749) | copy-start | bytes 3076 | tf_op jit(solution)/shard_map/cond
  835.1 175.0 %copy-start.43 = (s32[1,1,2048]{2,1,0:T(1,128)S(1)}, s32[1,1,2048]{2,1,0:T(1,128)}, u32[]{:S(2)}) copy-start(s32[1,1,2048]{2,1,0:T(1,128)} %copy-done.42) | copy-start | bytes 24580 | tf_op jit(solution)/shard_map/cond
  835.1 175.0 %copy-start.93 = (s32[256]{0:T(256)S(1)}, s32[256]{0:T(256)}, u32[]{:S(2)}) copy-start(s32[256]{0:T(256)} %get-tuple-element.753) | copy-start | bytes 3076 | tf_op jit(solution)/shard_map/cond
  835.1 175.0 %copy-start.12 = (bf16[2,4096,8]{1,2,0:T(8,128)(2,1)S(1)}, bf16[2,4096,8]{1,2,0:T(8,128)(2,1)}, u32[]{:S(2)}) copy-start(bf16[2,4096,8]{1,2,0:T(8,128)(2,1)} %get-tuple-element.385) | copy-start | bytes 393220 | tf_op jit(solution)/shard_map/cond
  1007.2 15.9 collective-permute-start.8
  1232.4 83.4 %collective-permute-start.9 = (bf16[256,4096]{1,0:T(8,128)(2,1)S(1)}, bf16[256,4096]{1,0:T(8,128)(2,1)S(1)}, u32[]{:S(2)}, u32[]{:S(2)}) collective-permute-start(bf16[256,4096]{1,0:T(8,128)(2,1)S(1)} %slice.500), channel_id=1, source_target_pairs={{0,4},{1,5},{2,6},{3,7},{4,0},{5,1},{6,2},{7,3}} | collective-permute-start | bytes 6291464 | tf_op jit(solution)/shard_map/cond/branch_1_fun/ppermute | solution.py:203
  1238.8 419.2 %collective-permute-start.10 = (bf16[2,3,176,4096]{3,2,1,0:T(8,128)(2,1)}, bf16[2,3,176,4096]{3,2,1,0:T(8,128)(2,1)}, u32[]{:S(2)}, u32[]{:S(2)}) collective-permute-start(bf16[2,3,176,4096]{3,2,1,0:T(8,128)(2,1)} %get-tuple-element.415.refs_0_), channel_id=1, source_target_pairs={{0,4},{1,5},{2,6},{3,7},{4,0},{5,1},{6,2},{7,3}} | collective-permute-start | bytes 25952264 | tf_op jit(solution)/shard_map/cond/branch_1_fun/ppermute | solution.py:203
  1238.8 419.2 %collective-permute-start.11 = (bf16[2,3,176,4096]{3,2,1,0:T(8,128)(2,1)}, bf16[2,3,176,4096]{3,2,1,0:T(8,128)(2,1)}, u32[]{:S(2)}, u32[]{:S(2)}) collective-permute-start(bf16[2,3,176,4096]{3,2,1,0:T(8,128)(2,1)} %get-tuple-element.416), channel_id=1, source_target_pairs={{0,2},{1,3},{2,0},{3,1},{4,6},{5,7},{6,4},{7,5}} | collective-permute-start | bytes 25952264 | tf_op jit(solution)/shard_map/cond/branch_1_fun/ppermute | solution.py:203
  1437.2 237.2 %copy-start.96 = (s32[6]{0:T(128)S(1)}, s32[6]{0:T(128)}, u32[]{:S(2)}) copy-start(s32[6]{0:T(128)} %get-tuple-element.696) | copy-start | bytes 76 | tf_op jit(solution)/shard_map/cond
  1437.2 237.2 %copy-start.66 = (s32[6144]{0:T(1024)S(1)}, s32[6144]{0:T(1024)}, u32[]{:S(2)}) copy-start(s32[6144]{0:T(1024)} %copy-done.65) | copy-start | bytes 73732 | tf_op jit(solution)/shard_map/cond
  1465.7 315.9 %copy-start.46 = (f32[1,4096]{1,0:T(1,128)S(1)}, f32[1,4096]{1,0:T(1,128)}, u32[]{:S(2)}) copy-start(f32[1,4096]{1,0:T(1,128)} %get-tuple-element.727) | copy-start | bytes 49156 | tf_op jit(solution)/shard_map/cond
  1658.0 462.6 %collective-permute-start.14 = (bf16[2,3,176,4096]{3,2,1,0:T(8,128)(2,1)}, bf16[2,3,176,4096]{3,2,1,0:T(8,128)(2,1)}, u32[]{:S(2)}, u32[]{:S(2)}) collective-permute-start(bf16[2,3,176,4096]{3,2,1,0:T(8,128)(2,1)} %collective-permute-done.11.refs_2_), channel_id=1, source_target_pairs={{0,4},{1,5},{2,6},{3,7},{4,0},{5,1},{6,2},{7,3}} | collective-permute-start | bytes 25952264 | tf_op jit(solution)/shard_map/cond/branch_1_fun/ppermute | solution.py:203
  1674.3 93.6 %collective-permute-start.12 = (bf16[256,4096]{1,0:T(8,128)(2,1)}, bf16[256,4096]{1,0:T(8,128)(2,1)S(1)}, u32[]{:S(2)}, u32[]{:S(2)}) collective-permute-start(bf16[256,4096]{1,0:T(8,128)(2,1)} %gather_fusion.10), channel_id=1, source_target_pairs={{0,2},{1,3},{2,0},{3,1},{4,6},{5,7},{6,4},{7,5}} | collective-permute-start | bytes 6291464 | tf_op jit(solution)/shard_map/cond/branch_1_fun/ppermute | solution.py:203
  1681.3 466.9 %collective-permute-start.15 = (bf16[2,3,176,4096]{3,2,1,0:T(8,128)(2,1)}, bf16[2,3,176,4096]{3,2,1,0:T(8,128)(2,1)}, u32[]{:S(2)}, u32[]{:S(2)}) collective-permute-start(bf16[2,3,176,4096]{3,2,1,0:T(8,128)(2,1)} %get-tuple-element.415.refs_0_), channel_id=1, source_target_pairs={{0,1},{1,0},{2,3},{3,2},{4,5},{5,4},{6,7},{7,6}} | collective-permute-start | bytes 25952264 | tf_op jit(solution)/shard_map/cond/branch_1_fun/ppermute | solution.py:203
  1681.9 466.3 %collective-permute-start.17 = (bf16[2,3,176,4096]{3,2,1,0:T(8,128)(2,1)}, bf16[2,3,176,4096]{3,2,1,0:T(8,128)(2,1)}, u32[]{:S(2)}, u32[]{:S(2)}) collective-permute-start(bf16[2,3,176,4096]{3,2,1,0:T(8,128)(2,1)} %collective-permute-done.11.refs_2_), channel_id=1, source_target_pairs={{0,1},{1,0},{2,3},{3,2},{4,5},{5,4},{6,7},{7,6}} | collective-permute-start | bytes 25952264 | tf_op jit(solution)/shard_map/cond/branch_1_fun/ppermute | solution.py:203
  1681.9 466.3 %collective-permute-start.16 = (bf16[2,3,176,4096]{3,2,1,0:T(8,128)(2,1)}, bf16[2,3,176,4096]{3,2,1,0:T(8,128)(2,1)}, u32[]{:S(2)}, u32[]{:S(2)}) collective-permute-start(bf16[2,3,176,4096]{3,2,1,0:T(8,128)(2,1)} %collective-permute-done.10.refs_1_), channel_id=1, source_target_pairs={{0,1},{1,0},{2,3},{3,2},{4,5},{5,4},{6,7},{7,6}} | collective-permute-start | bytes 25952264 | tf_op jit(solution)/shard_map/cond/branch_1_fun/ppermute | solution.py:203
  1767.9 126.9 %copy-start.7 = (bf16[256,4096]{1,0:T(8,128)(2,1)}, bf16[256,4096]{1,0:T(8,128)(2,1)S(1)}, u32[]{:S(2)}) copy-start(bf16[256,4096]{1,0:T(8,128)(2,1)S(1)} %collective-permute-done.12) | copy-start | bytes 6291460 | tf_op jit(solution)/shard_map/cond
  2069.7 64.0 %copy-start.41 = (s32[1,1,2048]{2,1,0:T(1,128)S(1)}, s32[1,1,2048]{2,1,0:T(1,128)}, u32[]{:S(2)}) copy-start(s32[1,1,2048]{2,1,0:T(1,128)} %copy-done.40) | copy-start | bytes 24580 | tf_op jit(solution)/shard_map/cond
  2069.7 64.0 %copy-start.92 = (s32[256]{0:T(256)S(1)}, s32[256]{0:T(256)}, u32[]{:S(2)}) copy-start(s32[256]{0:T(256)} %get-tuple-element.744) | copy-start | bytes 3076 | tf_op jit(solution)/shard_map/cond
  2069.7 64.1 %copy-start.101 = (s32[6]{0:T(128)S(1)}, s32[6]{0:T(128)}, u32[]{:S(2)}) copy-start(s32[6]{0:T(128)} %copy-done.100) | copy-start | bytes 76 | tf_op jit(solution)/shard_map/cond
  2069.7 64.1 %copy-start.89 = (bf16[36,6]{0,1:T(8,128)(2,1)S(1)}, bf16[36,6]{0,1:T(8,128)(2,1)}, u32[]{:S(2)}) copy-start(bf16[36,6]{0,1:T(8,128)(2,1)} %get-tuple-element.635) | copy-start | bytes 1300 | tf_op jit(solution)/shard_map/cond
  2069.7 64.2 %copy-start.31 = (s32[36,128]{1,0:T(8,128)S(1)}, s32[36,128]{1,0:T(8,128)}, u32[]{:S(2)}) copy-start(s32[36,128]{1,0:T(8,128)} %copy-done.30) | copy-start | bytes 55300 | tf_op jit(solution)/shard_map/cond
  2069.7 65.7 %copy-start.13 = (bf16[2,4096,8]{1,2,0:T(8,128)(2,1)S(1)}, bf16[2,4096,8]{1,2,0:T(8,128)(2,1)}, u32[]{:S(2)}) copy-start(bf16[2,4096,8]{1,2,0:T(8,128)(2,1)} %get-tuple-element.385) | copy-start | bytes 393220 | tf_op jit(solution)/shard_map/cond
  2120.6 27.6 %collective-permute-start.18 = (bf16[2,3,176,4096]{3,2,1,0:T(8,128)(2,1)}, bf16[2,3,176,4096]{3,2,1,0:T(8,128)(2,1)}, u32[]{:S(2)}, u32[]{:S(2)}) collective-permute-start(bf16[2,3,176,4096]{3,2,1,0:T(8,128)(2,1)} %collective-permute-done.14.refs_3_), channel_id=1, source_target_pairs={{0,1},{1,0},{2,3},{3,2},{4,5},{5,4},{6,7},{7,6}} | collective-permute-start | bytes 25952264 | tf_op jit(solution)/shard_map/cond/branch_1_fun/ppermute | solution.py:203
  2340.3 47.8 %collective-permute-start.19 = (bf16[256,4096]{1,0:T(8,128)(2,1)S(1)}, bf16[256,4096]{1,0:T(8,128)(2,1)S(1)}, u32[]{:S(2)}, u32[]{:S(2)}) collective-permute-start(bf16[256,4096]{1,0:T(8,128)(2,1)S(1)} %slice.499), channel_id=1, source_target_pairs={{0,2},{1,3},{2,0},{3,1},{4,6},{5,7},{6,4},{7,5}} | collective-permute-start | bytes 6291464 | tf_op jit(solution)/shard_map/cond/branch_1_fun/ppermute | solution.py:203
  (52 other events, 1852.9 us)
Sparse Core Ops, SparseCore 0:
  54.9 234.6 all-gather.11
  291.5 295.3 all-gather.15
  588.8 246.2 all-gather.13
  836.7 235.6 all-gather.17
  1074.1 160.7 all-gather.23
  1236.6 299.9 all-gather.21
  1538.4 294.7 all-gather.19
  1835.0 238.9 all-gather.25

commit v2 on v1

v2 whole, which is shorter than its diff:
```python
import functools

import jax
import jax.numpy as jnp
from jax import lax
from jax.experimental import pallas as pl
from jax.experimental.pallas import tpu as pltpu
from jax.sharding import PartitionSpec as P


EPS = 1e-5
TM = 256
DC = 256
NG = 4
CAP = 256
SIDE_RANKS = {4: ((4, 7), (5, 6)), 2: ((2, 5, 7), (3, 4, 6))}
VMEM = 66 * 1000 * 1000


def pad16(n):
    return (n + 15) // 16 * 16


def prep_body(groups, n_exp, s_ref, *refs):
    srcs, outs, sel = refs[:3], refs[3:-1], refs[-1]
    n = sum(groups)
    wide = sel.shape[0] // n

    @pl.when(pl.program_id(0) == 0)
    def _():
        col = lax.broadcasted_iota(jnp.int32, (wide, sel.shape[1]), 1)
        line = lax.broadcasted_iota(jnp.int32, (wide, sel.shape[1]), 0)
        for k in range(n):
            sel[k * wide:(k + 1) * wide, :] = (col == line * n_exp + s_ref[k]).astype(jnp.bfloat16)

    for m in range(3):
        k = 0
        for out, size in zip(outs, groups):
            for j in range(size):
                out[j, m] = jnp.dot(sel[k * wide:(k + 1) * wide, :], srcs[m][0], preferred_element_type=jnp.float32).astype(jnp.bfloat16)
                k += 1


def prep(layer, experts, groups, w_gate, w_up, w_down):
    n_exp, width, inner = w_gate.shape[1:]
    wide = pad16(inner)
    lines = [jnp.transpose(w, order).reshape(w.shape[0], inner * n_exp, width) for w, order in ((w_gate, (0, 3, 1, 2)), (w_up, (0, 3, 1, 2)), (w_down, (0, 2, 1, 3)))]
    n = sum(groups)
    return pl.pallas_call(
        functools.partial(prep_body, groups, n_exp),
        out_shape=[jax.ShapeDtypeStruct((g, 3, wide, width), jnp.bfloat16) for g in groups],
        grid_spec=pltpu.PrefetchScalarGridSpec(
            num_scalar_prefetch=1,
            grid=(width // DC,),
            in_specs=[pl.BlockSpec((1, inner * n_exp, DC), lambda c, s: (layer, 0, c))] * 3,
            out_specs=[pl.BlockSpec((g, 3, wide, DC), lambda c, s: (0, 0, 0, c)) for g in groups],
            scratch_shapes=[pltpu.VMEM((n * wide, inner * n_exp), jnp.bfloat16)],
        ),
        compiler_params=pltpu.CompilerParams(vmem_limit_bytes=VMEM),
        cost_estimate=pl.CostEstimate(flops=n * 600_000_000, bytes_accessed=70_000_000 + n * 4_300_000, transcendentals=0),
        name="prep",
    )(experts, *lines)


def expert_body(pieces, n_w, aliased, added, s_ref, h_ref, *refs):
    w_refs = refs[:n_w]
    more = n_w + aliased + 2 * added
    o_ref = refs[more]
    w1, w3, w2, act, sems = refs[more + 1:]
    wide = w1.shape[0] // len(pieces)
    i = pl.program_id(0)

    def copies(m, dst):
        out = []
        for p, (r, lead) in enumerate(pieces):
            src = w_refs[r].at[lead + (m,)] if isinstance(lead, tuple) else w_refs[r].at[lead, m]
            out.append(pltpu.make_async_copy(src, dst.at[pl.ds(p * wide, wide)], sems.at[m, p]))
        return out

    @pl.when(i == 0)
    def _():
        for m, dst in enumerate((w1, w3, w2)):
            for c in copies(m, dst):
                c.start()
        for m, dst in enumerate((w1, w3)):
            for c in copies(m, dst):
                c.wait()

    nt = (((1,), (1,)), ((), ()))

    @pl.when(i < s_ref[1])
    def _():
        cols = w1.shape[0]
        steps = (cols + 255) // 256

        def up(c, carry):
            at = pl.multiple_of(jnp.minimum(c * 256, cols - 256), 128)
            h = h_ref[...]
            u = lax.dot_general(h, w1[pl.ds(at, 256), :], nt, preferred_element_type=jnp.float32)
            v = lax.dot_general(h, w3[pl.ds(at, 256), :], nt, preferred_element_type=jnp.float32)
            act[:, pl.ds(at, 256)] = (jax.nn.silu(u) * v).astype(jnp.bfloat16)
            return carry

        lax.fori_loop(0, steps, up, 0)

    @pl.when(i == 0)
    def _():
        for c in copies(2, w2):
            c.wait()

    @pl.when(i < s_ref[1])
    def _():
        def down(c, carry):
            at = pl.multiple_of(c * 512, 512)
            o = jnp.dot(act[...], w2[:, pl.ds(at, 512)], preferred_element_type=jnp.float32)
            if added:
                x_ref, gate_ref = refs[more - 2:more]
                o = x_ref[:, pl.ds(at, 512)].astype(jnp.float32) + gate_ref[...] * o
            o_ref[:, pl.ds(at, 512)] = o
            return carry

        lax.fori_loop(0, o_ref.shape[1] // 512, down, 0)


def expert(scalars, rows, weights, pieces, out, max_tiles, add=None):
    width = rows.shape[1]
    wide = weights[0].shape[-2]
    cols = wide * len(pieces)
    aliased = out is not None
    at = lambda i, s: (s[0] + jnp.minimum(i, s[1] - 1), 0)
    anywhere = pl.BlockSpec(memory_space=pl.ANY)
    return pl.pallas_call(
        functools.partial(expert_body, pieces, len(weights), aliased, add is not None),
        out_shape=jax.ShapeDtypeStruct(rows.shape, jnp.float32),
        grid_spec=pltpu.PrefetchScalarGridSpec(
            num_scalar_prefetch=1,
            grid=(max_tiles,),
            in_specs=[pl.BlockSpec((TM, width), at)] + [anywhere] * (len(weights) + aliased)
            + ([pl.BlockSpec((TM, width), at), pl.BlockSpec((TM, 1), at)] if add else []),
            out_specs=pl.BlockSpec((TM, width), at),
            scratch_shapes=[pltpu.VMEM((cols, width), jnp.bfloat16)] * 3
            + [pltpu.VMEM((TM, cols), jnp.bfloat16), pltpu.SemaphoreType.DMA((3, len(pieces)))],
        ),
        input_output_aliases={2 + len(weights): 0} if aliased else {},
        compiler_params=pltpu.CompilerParams(vmem_limit_bytes=VMEM),
        cost_estimate=pl.CostEstimate(flops=3_000_000_000, bytes_accessed=60_000_000, transcendentals=0),
        name="expert",
    )(scalars, rows, *weights, *((out,) if aliased else ()), *(add or ()))


def prefix(onehot):
    n, k = onehot.shape
    blocks = onehot.astype(jnp.float32).reshape(n // 128, 128, k)
    lower = (jnp.arange(128)[:, None] > jnp.arange(128)[None, :]).astype(jnp.float32)
    inside = jnp.einsum("ij,bjk->bik", lower, blocks)
    sums = blocks.sum(axis=1)
    nb = n // 128
    before = jnp.einsum("ij,jk->ik", (jnp.arange(nb)[:, None] > jnp.arange(nb)[None, :]).astype(jnp.float32), sums)
    return (inside + before[:, None, :]).reshape(n, k).astype(jnp.int32), sums.sum(axis=0).astype(jnp.int32)


def row_plan(slots, n_local):
    n = slots.shape[0]
    onehot = slots[:, None] == jnp.arange(n_local)[None, :]
    within, counts = prefix(onehot)
    tiles = jnp.maximum((counts + TM - 1) // TM, 1)
    lower = jnp.arange(n_local)[:, None] > jnp.arange(n_local)[None, :]
    first = jnp.sum(jnp.where(lower, tiles[None, :], 0), axis=1)
    pos = jnp.sum(jnp.where(onehot, within + first[None, :] * TM, 0), axis=1)
    spare = jnp.where(jnp.arange(TM)[None, :] < (tiles * TM - counts)[:, None], jnp.arange(n_local)[:, None], n_local)
    keys = jnp.concatenate([slots, spare.reshape(-1)])
    order = lax.sort(keys * 8192 + jnp.arange(keys.shape[0], dtype=jnp.int32)) & 8191
    scalars = jnp.stack([first, tiles], axis=1).astype(jnp.int32)
    return jnp.where(order < n, order, 0), pos, scalars


def pick(table, index, size):
    return jnp.sum(jnp.where(index[..., None] == jnp.arange(size), table, 0), axis=-1)


def norm_gates(x, norm_w, router_w, ids0, ids1):
    xf = x.astype(jnp.float32)
    inv = lax.rsqrt(jnp.mean(xf * xf, axis=-1, keepdims=True) + EPS)
    h = (xf * inv * norm_w).astype(jnp.bfloat16)
    r = jnp.dot(h, router_w, preferred_element_type=jnp.float32)
    n_exp = router_w.shape[1]
    r0 = jnp.sum(jnp.where(ids0[:, None] == jnp.arange(n_exp), r, 0.0), axis=-1)
    r1 = jnp.sum(jnp.where(ids1[:, None] == jnp.arange(n_exp), r, 0.0), axis=-1)
    g = jax.nn.softmax(jnp.stack([r0, r1], axis=-1), axis=-1)
    return h, g[:, :1], g[:, 1:]


def take(table, index):
    return table.at[index].get(mode="promise_in_bounds")


def solution(mesh):
    n_dev = mesh.shape["fsdp"]

    def hop(a, bit):
        return lax.ppermute(a, "fsdp", [(i, i ^ bit) for i in range(n_dev)])

    def general(x, norm_w, router_w, w_gate, w_up, w_down, ids):
        n_layers, n_exp = w_gate.shape[:2]
        n_tok = x.shape[0]
        for l in range(n_layers):
            slot, pos, scalars = row_plan(jnp.concatenate([ids[l, 0], ids[l, 1]]), n_exp)
            h, g0, g1 = norm_gates(x, norm_w[l], router_w[l], ids[l, 0], ids[l, 1])
            rows = take(h, slot % n_tok)

            def step(e, out, l=l, rows=rows, scalars=scalars):
                w = prep(l, e[None].astype(jnp.int32), (1,), w_gate, w_up, w_down)[0][0]
                full = lax.all_gather(w, "fsdp")
                s = lax.dynamic_index_in_dim(scalars, e, 0, keepdims=False)
                return expert(s, rows, [full], [(0, p) for p in range(n_dev)], out, n_tok // TM)

            out = lax.fori_loop(0, n_exp, step, jnp.zeros(rows.shape, jnp.float32))
            x = (x.astype(jnp.float32) + (g0 * take(out, pos[:n_tok]) + g1 * take(out, pos[n_tok:]))).astype(jnp.bfloat16)
        return x

    def local_fn(tokens, norm_w, router_w, w_gate, w_up, w_down, route_ids):
        n_layers, n_exp = w_gate.shape[:2]
        n_tok = tokens.shape[0]
        n_light = (n_exp - NG) // 2
        n_local = NG + n_light
        me = lax.axis_index("fsdp")
        ids = jnp.swapaxes(route_ids, 1, 2)
        every = lax.all_gather(ids, "fsdp")
        hits = every[..., None] == jnp.arange(n_exp)
        load = jnp.sum(hits.astype(jnp.int32), axis=(0, 2, 3))
        earlier = jnp.arange(n_exp)[None, :] < jnp.arange(n_exp)[:, None]
        ahead = (load[:, None, :] > load[:, :, None]) | ((load[:, None, :] == load[:, :, None]) & earlier[None])
        rank = jnp.sum(ahead.astype(jnp.int32), axis=2)
        by_rank = jnp.sum(jnp.where(rank[:, None, :] == jnp.arange(n_exp)[None, :, None], jnp.arange(n_exp), 0), axis=2).astype(jnp.int32)
        home_of = [-1] * NG + [0] * (n_exp - NG)
        local_of = list(range(n_exp))
        for side, ranks in enumerate(SIDE_RANKS[NG]):
            for j, k in enumerate(ranks):
                home_of[k], local_of[k] = side, NG + j
        home = pick(jnp.array(home_of), rank, n_exp)
        local = pick(jnp.array(local_of), rank, n_exp)
        at_home = jnp.sum(jnp.where(hits, home[None, :, None, None, :], 0), axis=-1)
        lend = [n_dev // 2 if l % 2 == 0 else n_dev // 4 for l in range(n_layers)]
        share = [n_dev // 4 if l % 2 == 0 else n_dev // 2 for l in range(n_layers)]
        side_of = jnp.stack([(jnp.arange(n_dev) // bit) % 2 for bit in lend], axis=1)
        mine_side = jnp.stack([(me // bit) % 2 for bit in lend])
        needs = [jnp.any(at_home == v, axis=2) for v in (0, 1)]
        top = jnp.sum(jnp.where(rank == 0, jnp.arange(n_exp), 0), axis=1)[None, :, None, None]
        shared = jnp.all(jnp.any(every == top, axis=2))
        lent = jnp.where(side_of[:, :, None] == 0, needs[1], needs[0])
        n_lent = jnp.sum(lent.astype(jnp.int32), axis=2)
        ok = jnp.all(n_lent <= CAP) & shared

        def adaptive(x, norm_w, router_w, w_gate, w_up, w_down, ids):
            mine = lax.dynamic_index_in_dim(every, me, 0, keepdims=False)
            my_lent = lax.dynamic_index_in_dim(lent, me, 0, keepdims=False)
            my_top = jnp.sum(jnp.where(rank == 0, jnp.arange(n_exp), 0), axis=1)
            mine = jnp.where(mine[:, 0] == my_top[:, None], mine[:, 1], mine[:, 0])
            my_local = pick(local[:, None, :], mine, n_exp)
            sides = [jnp.array(r) for r in SIDE_RANKS[NG]]
            chosen = [[jnp.where(mine_side[l] == v, by_rank[l][sides[0]], by_rank[l][sides[1]]) for v in (0, 1)] for l in range(n_layers)]

            picks = [(by_rank[l, :1], jnp.concatenate([by_rank[l, 1:NG], *chosen[l]])) for l in range(n_layers)]
            picks = lax.optimization_barrier(picks)

            def shards(l, top, others):
                first = prep(l, top, (1,), w_gate, w_up, w_down)
                rest = prep(l, others, (1,) * (NG - 1 + 2 * n_light), w_gate, w_up, w_down)
                rest = [w[0] for w in rest]
                return first[0][0], rest[:NG - 1], rest[NG - 1:NG - 1 + n_light], rest[NG - 1 + n_light:]

            def all_of(w):
                return lax.all_gather(w, "fsdp")

            def after(values, *waited):
                return lax.optimization_barrier((values, *waited))[0]

            top_w, heavy_w, own, other = shards(0, *picks[0])
            full = [all_of(top_w)] + [all_of(w) for w in heavy_w]
            lists = []
            for l in range(n_layers):
                key = jnp.where(my_lent[l], 0, 8192) + jnp.arange(n_tok, dtype=jnp.int32)
                key, code = lax.sort((key, jnp.where(my_lent[l], my_local[l] * 8 + mine[l], n_local * 8)), num_keys=1)
                place = jnp.minimum(prefix(my_lent[l][:, None])[0][:, 0], CAP - 1)
                code = hop(code[:CAP], lend[l])
                lists.append(((key & 8191)[:CAP], place, code))
            for l in range(n_layers):
                key, place, code = lists[l]
                guest = hop(take(x, key), lend[l])
                if l == 0:
                    own_x, sent = [hop(w, share[0]) for w in own], [hop(w, lend[0]) for w in other]
                both = jnp.concatenate([x, guest])
                ids1 = jnp.concatenate([mine[l], code % 8])
                slots = jnp.concatenate([jnp.where(my_lent[l], n_local, my_local[l]), code // 8]) - 1
                slots = jnp.where(slots < 0, n_local - 1, slots)
                token, pos, scalars = row_plan(slots, n_local - 1)
                h, g0, g1 = norm_gates(both, norm_w[l], router_w[l], jnp.broadcast_to(my_top[l], ids1.shape), ids1)
                rows = take(h, token)
                max_tiles = (n_tok + CAP) // TM
                whole = [(0, p) for p in range(n_dev)]
                gathered = lambda k, out, w: expert(scalars[k - 1], rows, [w], whole, out, max_tiles)
                if l:
                    far = [hop(w, share[l]) for w in sent]
                    beside = [[hop(w, 1) for w in ws] for ws in zip(own, own_x, sent)]
                acc = expert(jnp.array([0, max_tiles], jnp.int32), h, [full[0]], whole, None, max_tiles, add=(both, g0))
                rows = after(rows, acc)
                if l == 0:
                    own_x, sent = after((own_x, sent), acc)
                    far = [hop(w, share[l]) for w in sent]
                    beside = [[hop(w, 1) for w in ws] for ws in zip(own, own_x, sent)]
                if l + 1 < n_layers:
                    top_w, heavy_w, own2, other2 = shards(l + 1, *after(picks[l + 1], acc))
                    coming = [all_of(top_w)] + [all_of(w) for w in heavy_w]
                    own_x2, sent2 = [hop(w, share[l + 1]) for w in own2], [hop(w, lend[l + 1]) for w in other2]
                out = None
                for k in range(1, NG - 1):
                    out = gathered(k, out, full[k])
                far = after(far, acc if out is None else out)
                for j in range(n_light):
                    w8 = [own[j], own_x[j], sent[j], far[j]] + beside[j] + [hop(far[j], 1)]
                    out = expert(scalars[NG - 1 + j], rows, w8, [(p, ()) for p in range(n_dev)], out, max_tiles)
                seen = acc[n_tok:] + g1[n_tok:] * take(out, pos[n_tok:])
                guest = seen.astype(jnp.bfloat16)
                back = hop(guest, lend[l])
                home_again = lambda: take(back, place)
                if l + 1 < n_layers:
                    late = after(full[NG - 1], guest)
                else:
                    returned = home_again()
                    late = after(full[NG - 1], guest, returned)
                    home_again = lambda: returned
                out = gathered(NG - 1, out, late)
                mixed = (acc[:n_tok] + g1[:n_tok] * take(out, pos[:n_tok])).astype(jnp.bfloat16)
                x = jnp.where(my_lent[l][:, None], home_again(), mixed)
                if l + 1 < n_layers:
                    x, own_x, sent = lax.optimization_barrier((x, own_x2, sent2))
                    full, own = coming, own2
            return x

        return lax.cond(ok, adaptive, general, tokens, norm_w, router_w, w_gate, w_up, w_down, ids)

    row_spec = P(("rep", "fsdp"), None)
    col_spec = P(None, None, None, "fsdp")
    return jax.shard_map(
        local_fn,
        mesh=mesh,
        in_specs=(row_spec, P(), P(), col_spec, col_spec, P(None, None, "fsdp", None), P(None, ("rep", "fsdp"), None)),
        out_specs=row_spec,
        check_vma=False,
    )
```

time: 2550 us -> 2580 us (1.012)
  waiting for transfers between devices: 816 us -> 1120 us
  other arithmetic: 331 us -> 145 us
  local copies, waits for them, and re-layouts: 499 us -> 384 us
  starting transfers between devices: 25.7 us -> 53.6 us
    ppermute x20 -> x34, waiting for transfers between devices: 688 us -> 1110 us  [hop(): return lax.ppermute(a, 'fsdp', [(i, i ^ bit) for i in range(n_dev)])]
    gather x12 -> x10, local copies, waits for them, and re-layouts: 483 us -> 327 us  [take(): return table.at[index].get(mode='promise_in_bounds')]
    all_gather x8, waiting for transfers between devices: 126 us -> 3.85 us  [all_of(): return lax.all_gather(w, 'fsdp')]
    add x2 -> x0, other arithmetic: 100 us -> none  [adaptive(): both.astype(jnp.float32)]
    convert_element_type x2, other arithmetic: 56.1 us -> 10.1 us  [adaptive(): guest = seen.astype(jnp.bfloat16)]
    cond x176 -> x96, local copies, waits for them, and re-layouts: 2.64 us -> 35.6 us
    ppermute x20 -> x34, starting transfers between devices: 24.8 us -> 52.9 us  [hop(): return lax.ppermute(a, 'fsdp', [(i, i ^ bit) for i in range(n_dev)])]
    select_n x6 -> x12, other arithmetic: 61.2 us -> 62.4 us  [the longest x2 60.5 us: adaptive(): x = jnp.where(my_lent[l][:, None], home_again(), mixed)]
  transfers between devices with their start and end apart: 28 -> 42, of which waited for: 9 -> 12; matrix products, arithmetic and copies ran while one was open for 31% -> 17% of each run, Pallas kernels for 29% -> 30%
where the time goes in v2:
time: 2580 us; the launch traced here: 2570 us
  waiting for transfers between devices  1120 us (43%)
  Pallas kernels  819 us (32%)
  local copies, waits for them, and re-layouts  384 us (15%)
  other arithmetic  145 us (6%)
  starting transfers between devices  53.6 us (2%)
    ppermute x34, waiting for transfers between devices, hop(): return lax.ppermute(a, 'fsdp', [(i, i ^ bit) for i in range(n_dev)])  1110 us
    pallas_call x12, Pallas kernels, expert(): pl.pallas_call(functools.partial(expert_body, pieces, len(weights), alias...  667 us
    gather x10, local copies, waits for them, and re-layouts, take(): return table.at[index].get(mode='promise_in_bounds')  327 us
    pallas_call x4, Pallas kernels, prep(): pl.pallas_call(functools.partial(prep_body, groups, n_exp), out_shape=[ja...  151 us
    select_n x2, other arithmetic, adaptive(): x = jnp.where(my_lent[l][:, None], home_again(), mixed)  60.5 us
    ppermute x34, starting transfers between devices, hop(): return lax.ppermute(a, 'fsdp', [(i, i ^ bit) for i in range(n_dev)])  52.9 us
  transfers between devices with their start and end apart: 42, of which 12 were waited for; matrix products, arithmetic and copies ran while one was open for 17% of the time, Pallas kernels for 30%

profile of v2, /device:TPU:0, one launch (start us, length us, event | category | flops | bytes accessed | tf_op | source)
XLA Modules:
  0.0 2572.1 jit_solution(4907354475697416188)
XLA Ops:
  6.5 14.4 all-gather
  27.2 2531.6 %conditional.1 = (bf16[2048,4096]{1,0:T(8,128)(2,1)S(1)}) conditional(s32[]{:T(128)} %convert_element_type.241, (bf16[2048,4096]{1,0:T(8,128)(2,1)}, s32[2,2,2048]{2,1,0:T(2,128)}, f32[2,4096]{1,0:T(2,128)}, bf16[2,4096,8]{1,2,0:T(8,128)(2,1)}, bf16[2,8,4096,172]{2,1,3,0:T(8,128)(2,1)}, /*index=5*/bf16[2,8,4096,172]{2,1,3,0:T(8,128)(2,1)}, ...), branch_computations={%region_11.34_spmd, %region_34.61_spmd} | conditional | flops 46115446784 | bytes 3621014528 | solution.py:340
  42.0 21.3 prep.14
  63.4 54.2 %prep.15 = (bf16[1,3,176,4096]{3,2,1,0:T(8,128)(2,1)}, bf16[1,3,176,4096]{3,2,1,0:T(8,128)(2,1)}, bf16[1,3,176,4096]{3,2,1,0:T(8,128)(2,1)}, bf16[1,3,176,4096]{...) custom-call(s32[7]{0:T(128)} %get-tuple-element.402.s_ref, ...), custom_call_target="tpu_custom_call" | custom-call | flops 4200000000 | bytes 100100000 | tf_op jit(solution)/shard_map/cond/branch_1_fun/prep/pallas_call | solution.py:49
  120.3 5.1 sort.98
  125.5 16.6 gather_fusion
  142.1 2.0 collective-permute-start.1
  145.9 8.3 constant_dynamic-update-slice_fusion.1
  154.9 79.0 %collective-permute-done.1 = s32[256]{0:T(256)S(1)} collective-permute-done((s32[256]{0:T(256)S(1)}, s32[256]{0:T(256)S(1)}, u32[]{:S(2)}, u32[]{:S(2)}) %collective-permute-start.1) | collective-permute-done | bytes 1056 | tf_op jit(solution)/shard_map/cond/branch_1_fun/ppermute | solution.py:201
  234.1 4.4 fusion.45
  240.6 11.8 fusion.47.h_ref
  252.4 6.5 copy-done.2
  258.8 5.0 select_reduce_fusion.10
  265.8 3.8 all-gather.12.cloned.1.call-done.refs_0_
  269.5 128.8 %expert.22 = f32[2304,4096]{1,0:T(8,128)} custom-call(s32[2]{0:T(128)} %broadcast_multiply_fusion.2.s_ref, bf16[2304,4096]{1,0:T(8,128)(2,1)} %copy-done.2, bf16[8,3,176,4096]{3,2,1,0:T(8,128)(2,1)} %all-gather.12.cloned.1.call-done.refs_0_, bf16[2304,4096]{1,0:T(8,128)(2,1)} %copy-done.5, f32[2304,1]{1,0:T(8,128)} %bitcast.289), custom_call_target="tpu_custom_call" | custom-call | flops 3000000000 | bytes 60000000 | tf_op jit(solution)/shard_map/cond/branch_1_fun/expert/pallas_call | solution.py:132
  398.4 21.5 prep.17
  419.9 54.3 %prep.16 = (bf16[1,3,176,4096]{3,2,1,0:T(8,128)(2,1)}, bf16[1,3,176,4096]{3,2,1,0:T(8,128)(2,1)}, bf16[1,3,176,4096]{3,2,1,0:T(8,128)(2,1)}, bf16[1,3,176,4096]{...) custom-call(s32[7]{0:T(128)} %get-tuple-element.419.s_ref, ...), custom_call_target="tpu_custom_call" | custom-call | flops 4200000000 | bytes 100100000 | tf_op jit(solution)/shard_map/cond/branch_1_fun/prep/pallas_call | solution.py:49
  477.8 2.0 collective-permute-start.5
  479.8 178.4 %collective-permute-done.2.refs_1_ = bf16[3,176,4096]{2,1,0:T(8,128)(2,1)} collective-permute-done((bf16[3,176,4096]{2,1,0:T(8,128)(2,1)}, bf16[3,176,4096]{2,1,0:T(8,128)(2,1)}, u32[]{:S(2)}, u32[]{:S(2)}) %collective-permute-start.2) | collective-permute-done | bytes 4325408 | tf_op jit(solution)/shard_map/cond/branch_1_fun/ppermute | solution.py:201
  658.2 161.5 %collective-permute-done.3.refs_1_ = bf16[3,176,4096]{2,1,0:T(8,128)(2,1)} collective-permute-done((bf16[3,176,4096]{2,1,0:T(8,128)(2,1)}, bf16[3,176,4096]{2,1,0:T(8,128)(2,1)}, u32[]{:S(2)}, u32[]{:S(2)}) %collective-permute-start.3) | collective-permute-done | bytes 4325408 | tf_op jit(solution)/shard_map/cond/branch_1_fun/ppermute | solution.py:201
  822.7 5.1 sort.100
  829.7 342.3 %collective-permute-done.22 = s32[256]{0:T(256)S(1)} collective-permute-done((s32[256]{0:T(256)S(1)}, s32[256]{0:T(256)S(1)}, u32[]{:S(2)}, u32[]{:S(2)}) %collective-permute-start.22) | collective-permute-done | bytes 1056 | tf_op jit(solution)/shard_map/cond/branch_1_fun/ppermute | solution.py:201
  1173.5 5.8 sort.99
  1183.3 57.8 %gather_fusion.5 = bf16[3584,4096]{1,0:T(8,128)(2,1)} fusion(bf16[2304,4096]{1,0:T(8,128)(2,1)} %copy-done.2, s32[4096]{0:T(1024)S(1)} %pad_clamp_fusion.1), kind=kCustom, calls=%fused_computation.11 | custom fusion | bytes 58734592 | tf_op jit(solution)/shard_map/cond/branch_1_fun/gather | solution.py:194
  1241.1 53.9 %expert.23.refs_1_ = f32[3584,4096]{1,0:T(8,128)} custom-call(s32[2]{0:T(128)} %get-tuple-element.712.s_ref, bf16[3584,4096]{1,0:T(8,128)(2,1)} %gather_fusion.5, bf16[8,3,176,4096]{3,2,1,0:T(8,128)(2,1)} %all-gather.16.cloned.1.call-done.refs_0_), custom_call_target="tpu_custom_call" | custom-call | flops 3000000000 | bytes 60000000 | tf_op jit(solution)/shard_map/cond/branch_1_fun/expert/pallas_call | solution.py:132
  1295.2 54.0 %expert.24.refs_8_ = f32[3584,4096]{1,0:T(8,128)} custom-call(s32[2]{0:T(128)} %get-tuple-element.713.s_ref, bf16[3584,4096]{1,0:T(8,128)(2,1)} %gather_fusion.5, bf16[8,3,176,4096]{3,2,1,0:T(8,128)(2,1)} %all-gather.14.cloned.1.call-done.refs_0_, f32[3584,4096]{1,0:T(8,128)} %expert.23.refs_1_), custom_call_target="tpu_custom_call", output_to_operand_aliasing={{}: (3, {})} | custom-call | flops 3000000000 | bytes 60000000 | tf_op jit(solution)/shard_map/cond/branch_1_fun/expert/pallas_call | solution.py:132
  1357.0 2.6 collective-permute-done.15.refs_7_
  1359.6 37.9 %expert.25.refs_8_ = f32[3584,4096]{1,0:T(8,128)} custom-call(s32[2]{0:T(128)} %get-tuple-element.711.s_ref, bf16[3584,4096]{1,0:T(8,128)(2,1)} %gather_fusion.5, bf16[3,176,4096]{2,1,0:T(8,128)(2,1)} %bitcast.306, bf16[3,176,4096]{2,1,0:T(8,128)(2,1)} %collective-permute-done.2.refs_1_, ...), custom_call_target="tpu_custom_call", output_to_operand_aliasing={{}: (10, {})} | custom-call | flops 3000000000 | bytes 60000000 | tf_op jit(solution)/shard_map/cond/branch_1_fun/expert/pallas_call | solution.py:132
  1397.6 27.3 %expert.26.refs_1_ = f32[3584,4096]{1,0:T(8,128)} custom-call(s32[2]{0:T(128)} %get-tuple-element.714.s_ref, bf16[3584,4096]{1,0:T(8,128)(2,1)} %gather_fusion.5, bf16[3,176,4096]{2,1,0:T(8,128)(2,1)} %bitcast.303, bf16[3,176,4096]{2,1,0:T(8,128)(2,1)} %collective-permute-done.3.refs_1_, ...), custom_call_target="tpu_custom_call", output_to_operand_aliasing={{}: (10, {})} | custom-call | flops 3000000000 | bytes 60000000 | tf_op jit(solution)/shard_map/cond/branch_1_fun/expert/pallas_call | solution.py:132
  1425.0 23.6 gather_fusion.6
  1448.6 5.7 fusion.56
  1456.9 2.0 collective-permute-start.17
  1458.9 10.3 collective-permute-start.19
  1469.3 38.7 %expert.27 = f32[3584,4096]{1,0:T(8,128)} custom-call(s32[2]{0:T(128)} %get-tuple-element.710.s_ref, bf16[3584,4096]{1,0:T(8,128)(2,1)} %gather_fusion.5, bf16[8,3,176,4096]{3,2,1,0:T(8,128)(2,1)} %all-gather.18.cloned.1.call-done.refs_0_, f32[3584,4096]{1,0:T(8,128)} %expert.26.refs_1_), custom_call_target="tpu_custom_call", output_to_operand_aliasing={{}: (3, {})} | custom-call | flops 3000000000 | bytes 60000000 | tf_op jit(solution)/shard_map/cond/branch_1_fun/expert/pallas_call | solution.py:132
  1508.0 45.7 %gather_fusion.8 = f32[2048,4096]{1,0:T(8,128)} fusion(f32[3584,4096]{1,0:T(8,128)} %expert.27, s32[2048]{0:T(1024)S(1)} %broadcast_clamp_fusion.5), kind=kCustom, calls=%fused_computation.14 | custom fusion | bytes 67117056 | tf_op jit(solution)/shard_map/cond/branch_1_fun/gather | solution.py:194
  1553.7 30.5 %gather_fusion.7 = bf16[2048,4096]{1,0:T(8,128)(2,1)} fusion(bf16[256,4096]{1,0:T(8,128)(2,1)} %collective-permute-done.16, s32[2048]{0:T(1024)S(1)} %broadcast_clamp_fusion.7), kind=kCustom, calls=%fused_computation.13 | custom fusion | bytes 33562624 | tf_op jit(solution)/shard_map/cond/branch_1_fun/gather | solution.py:194
  1584.2 33.9 %fusion.53 = bf16[2048,4096]{1,0:T(8,128)(2,1)} fusion(bf16[2048,4096]{1,0:T(8,128)(2,1)} %gather_fusion.7, f32[2048,4096]{1,0:T(8,128)} %gather_fusion.8, f32[2304,4096]{1,0:T(8,128)} %expert.22, f32[2048]{0:T(1024)S(1)} %copy-done.33, pred[2048]{0:T(1024)(128)(4,1)S(1)} %copy-done.43), kind=kLoop, calls=%fused_computation.164 | loop fusion | flops 33554432 | bytes 100673536 | tf_op jit(solution)/shard_map/cond/branch_1_fun/jit(_where)/select_n | solution.py:334
  1618.1 92.5 %collective-permute-done.17.refs_1_ = bf16[3,176,4096]{2,1,0:T(8,128)(2,1)} collective-permute-done((bf16[3,176,4096]{2,1,0:T(8,128)(2,1)}, bf16[3,176,4096]{2,1,0:T(8,128)(2,1)}, u32[]{:S(2)}, u32[]{:S(2)}) %collective-permute-start.17) | collective-permute-done | bytes 4325408 | tf_op jit(solution)/shard_map/cond/branch_1_fun/ppermute | solution.py:201
  1710.6 180.2 %collective-permute-done.18.refs_1_ = bf16[3,176,4096]{2,1,0:T(8,128)(2,1)} collective-permute-done((bf16[3,176,4096]{2,1,0:T(8,128)(2,1)}, bf16[3,176,4096]{2,1,0:T(8,128)(2,1)}, u32[]{:S(2)}, u32[]{:S(2)}) %collective-permute-start.18) | collective-permute-done | bytes 4325408 | tf_op jit(solution)/shard_map/cond/branch_1_fun/ppermute | solution.py:201
  1890.8 11.9 gather_fusion.9
  1902.8 12.5 collective-permute-start.21
  1915.4 5.8 sort.101
  1924.2 8.2 constant_dynamic-update-slice_fusion.3
  1932.5 25.8 %collective-permute-done.21 = bf16[256,4096]{1,0:T(8,128)(2,1)} collective-permute-done((bf16[256,4096]{1,0:T(8,128)(2,1)S(1)}, bf16[256,4096]{1,0:T(8,128)(2,1)}, u32[]{:S(2)}, u32[]{:S(2)}) %collective-permute-start.21) | collective-permute-done | bytes 2097184 | tf_op jit(solution)/shard_map/cond/branch_1_fun/ppermute | solution.py:201
  1960.1 4.4 fusion.48
  1966.5 11.8 fusion.50.h_ref
  1978.4 6.4 copy-done.3
  1984.8 5.0 select_reduce_fusion.8
  1990.3 57.8 %gather_fusion.10 = bf16[3584,4096]{1,0:T(8,128)(2,1)} fusion(bf16[2304,4096]{1,0:T(8,128)(2,1)} %copy-done.3, s32[4096]{0:T(1024)S(1)} %pad_clamp_fusion), kind=kCustom, calls=%fused_computation.16 | custom fusion | bytes 58734592 | tf_op jit(solution)/shard_map/cond/branch_1_fun/gather | solution.py:194
  2049.5 125.6 %expert.28 = f32[2304,4096]{1,0:T(8,128)} custom-call(s32[2]{0:T(128)} %broadcast_multiply_fusion.2.s_ref, bf16[2304,4096]{1,0:T(8,128)(2,1)} %copy-done.3, bf16[8,3,176,4096]{3,2,1,0:T(8,128)(2,1)} %all-gather.20.cloned.1.call-done.refs_0_, bf16[2304,4096]{1,0:T(8,128)(2,1)} %copy-done.6, f32[2304,1]{1,0:T(8,128)} %bitcast.290), custom_call_target="tpu_custom_call" | custom-call | flops 3000000000 | bytes 60000000 | tf_op jit(solution)/shard_map/cond/branch_1_fun/expert/pallas_call | solution.py:132
  2175.1 50.1 %expert.29.refs_1_ = f32[3584,4096]{1,0:T(8,128)} custom-call(s32[2]{0:T(128)} %get-tuple-element.707.s_ref, bf16[3584,4096]{1,0:T(8,128)(2,1)} %gather_fusion.10, bf16[8,3,176,4096]{3,2,1,0:T(8,128)(2,1)} %all-gather.24.cloned.1.call-done.refs_0_), custom_call_target="tpu_custom_call" | custom-call | flops 3000000000 | bytes 60000000 | tf_op jit(solution)/shard_map/cond/branch_1_fun/expert/pallas_call | solution.py:132
  2225.3 50.1 %expert.30.refs_8_ = f32[3584,4096]{1,0:T(8,128)} custom-call(s32[2]{0:T(128)} %get-tuple-element.708.s_ref, bf16[3584,4096]{1,0:T(8,128)(2,1)} %gather_fusion.10, bf16[8,3,176,4096]{3,2,1,0:T(8,128)(2,1)} %all-gather.22.cloned.1.call-done.refs_0_, f32[3584,4096]{1,0:T(8,128)} %expert.29.refs_1_), custom_call_target="tpu_custom_call", output_to_operand_aliasing={{}: (3, {})} | custom-call | flops 3000000000 | bytes 60000000 | tf_op jit(solution)/shard_map/cond/branch_1_fun/expert/pallas_call | solution.py:132
  2275.4 12.9 collective-permute-start.32
  2290.4 5.2 collective-permute-done.32.refs_7_
  2295.6 37.7 %expert.31.refs_8_ = f32[3584,4096]{1,0:T(8,128)} custom-call(s32[2]{0:T(128)} %get-tuple-element.706.s_ref, bf16[3584,4096]{1,0:T(8,128)(2,1)} %gather_fusion.10, bf16[3,176,4096]{2,1,0:T(8,128)(2,1)} %bitcast.300, bf16[3,176,4096]{2,1,0:T(8,128)(2,1)} %collective-permute-done.17.refs_1_, ...), custom_call_target="tpu_custom_call", output_to_operand_aliasing={{}: (10, {})} | custom-call | flops 3000000000 | bytes 60000000 | tf_op jit(solution)/shard_map/cond/branch_1_fun/expert/pallas_call | solution.py:132
  2333.3 25.3 expert.32.refs_1_
  2358.6 23.6 gather_fusion.11
  2382.3 4.4 fusion.55
  2388.3 46.3 %collective-permute-done.33 = bf16[256,4096]{1,0:T(8,128)(2,1)S(1)} collective-permute-done((bf16[256,4096]{1,0:T(8,128)(2,1)S(1)}, bf16[256,4096]{1,0:T(8,128)(2,1)S(1)}, u32[]{:S(2)}, u32[]{:S(2)}) %collective-permute-start.33) | collective-permute-done | bytes 2097184 | tf_op jit(solution)/shard_map/cond/branch_1_fun/ppermute | solution.py:201
  2434.6 14.0 gather_fusion.12
  2448.6 37.9 %expert.33 = f32[3584,4096]{1,0:T(8,128)} custom-call(s32[2]{0:T(128)} %get-tuple-element.705.s_ref, bf16[3584,4096]{1,0:T(8,128)(2,1)} %gather_fusion.10, bf16[8,3,176,4096]{3,2,1,0:T(8,128)(2,1)} %all-gather.26.cloned.1.call-done.refs_0_, f32[3584,4096]{1,0:T(8,128)} %expert.32.refs_1_), custom_call_target="tpu_custom_call", output_to_operand_aliasing={{}: (3, {})} | custom-call | flops 3000000000 | bytes 60000000 | tf_op jit(solution)/shard_map/cond/branch_1_fun/expert/pallas_call | solution.py:132
  2486.6 45.4 %gather_fusion.13 = f32[2048,4096]{1,0:T(8,128)} fusion(f32[3584,4096]{1,0:T(8,128)} %expert.33, s32[2048]{0:T(1024)S(1)} %broadcast_clamp_fusion.4), kind=kCustom, calls=%fused_computation.19 | custom fusion | bytes 67117056 | tf_op jit(solution)/shard_map/cond/branch_1_fun/gather | solution.py:194
  2531.9 26.7 %fusion.54 = bf16[2048,4096]{1,0:T(8,128)(2,1)S(1)} fusion(bf16[2048,4096]{1,0:T(8,128)(2,1)} %gather_fusion.12, f32[2048,4096]{1,0:T(8,128)} %gather_fusion.13, f32[2304,4096]{1,0:T(8,128)} %expert.28, f32[2048]{0:T(1024)S(1)} %copy-done.34, pred[2048]{0:T(1024)(128)(4,1)S(1)} %copy-done.40), kind=kLoop, calls=%fused_computation.165 | loop fusion | flops 33554432 | bytes 100673536 | tf_op jit(solution)/shard_map/cond/branch_1_fun/jit(_where)/select_n | solution.py:334
  2558.9 6.2 copy-done.8
  (304 shorter events, 57.1 us)
Async XLA Ops:
  35.9 233.6 %all-gather.12.cloned.1.call-start = ((), (), s32[]{:S(2)}) async-start(), calls=%async_computation | async-start | bytes 38928384 | tf_op jit(solution)/shard_map/cond/branch_1_fun/all_gather | solution.py:273
  63.3 55.8 %copy-start.52 = (s32[2,8]{1,0:T(2,128)S(1)}, s32[2,8]{1,0:T(2,128)}, u32[]{:S(2)}) copy-start(s32[2,8]{1,0:T(2,128)} %copy-done.51) | copy-start | bytes 196 | tf_op jit(solution)/shard_map/cond
  63.3 1177.8 %all-gather.16.cloned.1.call-start = ((), (), s32[]{:S(2)}) async-start(), calls=%async_computation.2 | async-start | bytes 38928384 | tf_op jit(solution)/shard_map/cond/branch_1_fun/all_gather | solution.py:273
  117.6 1177.5 %all-gather.14.cloned.1.call-start = ((), (), s32[]{:S(2)}) async-start(), calls=%async_computation.1 | async-start | bytes 38928384 | tf_op jit(solution)/shard_map/cond/branch_1_fun/all_gather | solution.py:273
  118.3 1350.9 %all-gather.18.cloned.1.call-start = ((), (), s32[]{:S(2)}) async-start(), calls=%async_computation.3 | async-start | bytes 38928384 | tf_op jit(solution)/shard_map/cond/branch_1_fun/all_gather | solution.py:273
  118.9 1930.6 %all-gather.20.cloned.1.call-start = ((), (), s32[]{:S(2)}) async-start(), calls=%async_computation.4 | async-start | bytes 38928384 | tf_op jit(solution)/shard_map/cond/branch_1_fun/all_gather | solution.py:273
  119.1 35.1 %copy-start.41 = (pred[2048]{0:T(1024)(128)(4,1)}, pred[2048]{0:T(1024)(128)(4,1)S(1)}, u32[]{:S(2)}) copy-start(pred[2048]{0:T(1024)(128)(4,1)S(1)} %get-tuple-element.698) | copy-start | bytes 6148 | tf_op jit(solution)/shard_map/cond
  119.1 702.9 %copy-start.37 = (pred[2048]{0:T(1024)(128)(4,1)}, pred[2048]{0:T(1024)(128)(4,1)S(1)}, u32[]{:S(2)}) copy-start(pred[2048]{0:T(1024)(128)(4,1)S(1)} %get-tuple-element.697) | copy-start | bytes 6148 | tf_op jit(solution)/shard_map/cond
  120.3 701.8 %copy-start.20 = (s32[1,2048]{1,0:T(1,128)}, s32[1,2048]{1,0:T(1,128)S(1)}, u32[]{:S(2)}) copy-start(s32[1,2048]{1,0:T(1,128)S(1)} %get-tuple-element.783) | copy-start | bytes 24580 | tf_op jit(solution)/shard_map/cond
  142.1 91.8 %collective-permute-start = (bf16[256,4096]{1,0:T(8,128)(2,1)S(1)}, bf16[256,4096]{1,0:T(8,128)(2,1)S(1)}, u32[]{:S(2)}, u32[]{:S(2)}) collective-permute-start(bf16[256,4096]{1,0:T(8,128)(2,1)S(1)} %gather_fusion), channel_id=1, source_target_pairs={{0,4},{1,5},{2,6},{3,7},{4,0},{5,1},{6,2},{7,3}} | collective-permute-start | bytes 6291464 | tf_op jit(solution)/shard_map/cond/branch_1_fun/ppermute | solution.py:201
  142.1 91.8 %collective-permute-start.1 = (s32[256]{0:T(256)S(1)}, s32[256]{0:T(256)S(1)}, u32[]{:S(2)}, u32[]{:S(2)}) collective-permute-start(s32[256]{0:T(256)S(1)} %slice.211), channel_id=1, source_target_pairs={{0,4},{1,5},{2,6},{3,7},{4,0},{5,1},{6,2},{7,3}} | collective-permute-start | bytes 3080 | tf_op jit(solution)/shard_map/cond/branch_1_fun/ppermute | solution.py:201
  419.9 1755.2 %all-gather.24.cloned.1.call-start = ((), (), s32[]{:S(2)}) async-start(), calls=%async_computation.6 | async-start | bytes 38928384 | tf_op jit(solution)/shard_map/cond/branch_1_fun/all_gather | solution.py:273
  474.3 1751.0 %all-gather.22.cloned.1.call-start = ((), (), s32[]{:S(2)}) async-start(), calls=%async_computation.5 | async-start | bytes 38928384 | tf_op jit(solution)/shard_map/cond/branch_1_fun/all_gather | solution.py:273
  475.0 1973.6 %all-gather.26.cloned.1.call-start = ((), (), s32[]{:S(2)}) async-start(), calls=%async_computation.7 | async-start | bytes 38928384 | tf_op jit(solution)/shard_map/cond/branch_1_fun/all_gather | solution.py:273
  475.8 182.5 %collective-permute-start.2 = (bf16[3,176,4096]{2,1,0:T(8,128)(2,1)}, bf16[3,176,4096]{2,1,0:T(8,128)(2,1)}, u32[]{:S(2)}, u32[]{:S(2)}) collective-permute-start(bf16[3,176,4096]{2,1,0:T(8,128)(2,1)} %bitcast.304), channel_id=1, source_target_pairs={{0,2},{1,3},{2,0},{3,1},{4,6},{5,7},{6,4},{7,5}} | collective-permute-start | bytes 12976136 | tf_op jit(solution)/shard_map/cond/branch_1_fun/ppermute | solution.py:201
  476.8 342.9 %collective-permute-start.3 = (bf16[3,176,4096]{2,1,0:T(8,128)(2,1)}, bf16[3,176,4096]{2,1,0:T(8,128)(2,1)}, u32[]{:S(2)}, u32[]{:S(2)}) collective-permute-start(bf16[3,176,4096]{2,1,0:T(8,128)(2,1)} %bitcast.301), channel_id=1, source_target_pairs={{0,2},{1,3},{2,0},{3,1},{4,6},{5,7},{6,4},{7,5}} | collective-permute-start | bytes 12976136 | tf_op jit(solution)/shard_map/cond/branch_1_fun/ppermute | solution.py:201
  477.8 341.9 %collective-permute-start.4 = (bf16[3,176,4096]{2,1,0:T(8,128)(2,1)}, bf16[3,176,4096]{2,1,0:T(8,128)(2,1)}, u32[]{:S(2)}, u32[]{:S(2)}) collective-permute-start(bf16[3,176,4096]{2,1,0:T(8,128)(2,1)} %bitcast.374), channel_id=1, source_target_pairs={{0,4},{1,5},{2,6},{3,7},{4,0},{5,1},{6,2},{7,3}} | collective-permute-start | bytes 12976136 | tf_op jit(solution)/shard_map/cond/branch_1_fun/ppermute | solution.py:201
  477.8 342.2 %collective-permute-start.5 = (bf16[3,176,4096]{2,1,0:T(8,128)(2,1)}, bf16[3,176,4096]{2,1,0:T(8,128)(2,1)}, u32[]{:S(2)}, u32[]{:S(2)}) collective-permute-start(bf16[3,176,4096]{2,1,0:T(8,128)(2,1)} %bitcast.373), channel_id=1, source_target_pairs={{0,4},{1,5},{2,6},{3,7},{4,0},{5,1},{6,2},{7,3}} | collective-permute-start | bytes 12976136 | tf_op jit(solution)/shard_map/cond/branch_1_fun/ppermute | solution.py:201
  820.0 529.2 %collective-permute-start.6 = (bf16[3,176,4096]{2,1,0:T(8,128)(2,1)}, bf16[3,176,4096]{2,1,0:T(8,128)(2,1)}, u32[]{:S(2)}, u32[]{:S(2)}) collective-permute-start(bf16[3,176,4096]{2,1,0:T(8,128)(2,1)} %collective-permute-done.4.refs_2_), channel_id=1, source_target_pairs={{0,2},{1,3},{2,0},{3,1},{4,6},{5,7},{6,4},{7,5}} | collective-permute-start | bytes 12976136 | tf_op jit(solution)/shard_map/cond/branch_1_fun/ppermute | solution.py:201
  821.4 527.8 %collective-permute-start.7 = (bf16[3,176,4096]{2,1,0:T(8,128)(2,1)}, bf16[3,176,4096]{2,1,0:T(8,128)(2,1)}, u32[]{:S(2)}, u32[]{:S(2)}) collective-permute-start(bf16[3,176,4096]{2,1,0:T(8,128)(2,1)} %collective-permute-done.5.refs_2_), channel_id=1, source_target_pairs={{0,2},{1,3},{2,0},{3,1},{4,6},{5,7},{6,4},{7,5}} | collective-permute-start | bytes 12976136 | tf_op jit(solution)/shard_map/cond/branch_1_fun/ppermute | solution.py:201
  827.8 344.2 %collective-permute-start.22 = (s32[256]{0:T(256)S(1)}, s32[256]{0:T(256)S(1)}, u32[]{:S(2)}, u32[]{:S(2)}) collective-permute-start(s32[256]{0:T(256)S(1)} %slice.232), channel_id=1, source_target_pairs={{0,2},{1,3},{2,0},{3,1},{4,6},{5,7},{6,4},{7,5}} | collective-permute-start | bytes 3080 | tf_op jit(solution)/shard_map/cond/branch_1_fun/ppermute | solution.py:201
  829.2 520.8 %collective-permute-start.12 = (bf16[3,176,4096]{2,1,0:T(8,128)(2,1)}, bf16[3,176,4096]{2,1,0:T(8,128)(2,1)}, u32[]{:S(2)}, u32[]{:S(2)}) collective-permute-start(bf16[3,176,4096]{2,1,0:T(8,128)(2,1)} %bitcast.305), channel_id=1, source_target_pairs={{0,1},{1,0},{2,3},{3,2},{4,5},{5,4},{6,7},{7,6}} | collective-permute-start | bytes 12976136 | tf_op jit(solution)/shard_map/cond/branch_1_fun/ppermute | solution.py:201
  829.2 521.3 %collective-permute-start.13 = (bf16[3,176,4096]{2,1,0:T(8,128)(2,1)}, bf16[3,176,4096]{2,1,0:T(8,128)(2,1)}, u32[]{:S(2)}, u32[]{:S(2)}) collective-permute-start(bf16[3,176,4096]{2,1,0:T(8,128)(2,1)} %collective-permute-done.2.refs_1_), channel_id=1, source_target_pairs={{0,1},{1,0},{2,3},{3,2},{4,5},{5,4},{6,7},{7,6}} | collective-permute-start | bytes 12976136 | tf_op jit(solution)/shard_map/cond/branch_1_fun/ppermute | solution.py:201
  1172.0 178.5 %collective-permute-start.14 = (bf16[3,176,4096]{2,1,0:T(8,128)(2,1)}, bf16[3,176,4096]{2,1,0:T(8,128)(2,1)}, u32[]{:S(2)}, u32[]{:S(2)}) collective-permute-start(bf16[3,176,4096]{2,1,0:T(8,128)(2,1)} %collective-permute-done.4.refs_2_), channel_id=1, source_target_pairs={{0,1},{1,0},{2,3},{3,2},{4,5},{5,4},{6,7},{7,6}} | collective-permute-start | bytes 12976136 | tf_op jit(solution)/shard_map/cond/branch_1_fun/ppermute | solution.py:201
  1295.1 56.9 %copy-start.38 = (pred[2048]{0:T(1024)(128)(4,1)S(1)}, pred[2048]{0:T(1024)(128)(4,1)}, u32[]{:S(2)}) copy-start(pred[2048]{0:T(1024)(128)(4,1)} %copy-done.37) | copy-start | bytes 6148 | tf_op jit(solution)/shard_map/cond
  1295.1 56.9 %copy-start.42 = (pred[2048]{0:T(1024)(128)(4,1)S(1)}, pred[2048]{0:T(1024)(128)(4,1)}, u32[]{:S(2)}) copy-start(pred[2048]{0:T(1024)(128)(4,1)} %copy-done.41) | copy-start | bytes 6148 | tf_op jit(solution)/shard_map/cond
  1295.1 59.1 %copy-start.62 = (f32[5]{0:T(128)S(1)}, f32[5]{0:T(128)}, u32[]{:S(2)}) copy-start(f32[5]{0:T(128)} %copy-done.61) | copy-start | bytes 64 | tf_op jit(solution)/shard_map/cond
  1295.1 59.3 %copy-start.56 = (bf16[18,5]{0,1:T(8,128)(2,1)S(1)}, bf16[18,5]{0,1:T(8,128)(2,1)}, u32[]{:S(2)}) copy-start(bf16[18,5]{0,1:T(8,128)(2,1)} %get-tuple-element.699) | copy-start | bytes 544 | tf_op jit(solution)/shard_map/cond
  1295.2 59.4 %copy-start.31 = (s32[18,128]{1,0:T(8,128)S(1)}, s32[18,128]{1,0:T(8,128)}, u32[]{:S(2)}) copy-start(s32[18,128]{1,0:T(8,128)} %copy-done.30) | copy-start | bytes 27652 | tf_op jit(solution)/shard_map/cond
  1295.2 59.6 %copy-start.67 = (s32[5]{0:T(128)S(1)}, s32[5]{0:T(128)}, u32[]{:S(2)}) copy-start(s32[5]{0:T(128)} %copy-done.66) | copy-start | bytes 64 | tf_op jit(solution)/shard_map/cond
  1295.2 59.6 %copy-start.55 = (bf16[18,5]{0,1:T(8,128)(2,1)S(1)}, bf16[18,5]{0,1:T(8,128)(2,1)}, u32[]{:S(2)}) copy-start(bf16[18,5]{0,1:T(8,128)(2,1)} %get-tuple-element.701) | copy-start | bytes 544 | tf_op jit(solution)/shard_map/cond
  1295.2 59.8 %copy-start.29 = (s32[18,128]{1,0:T(8,128)S(1)}, s32[18,128]{1,0:T(8,128)}, u32[]{:S(2)}) copy-start(s32[18,128]{1,0:T(8,128)} %copy-done.28) | copy-start | bytes 27652 | tf_op jit(solution)/shard_map/cond
  1349.2 10.4 collective-permute-start.15
  1350.0 47.6 %collective-permute-start.8 = (bf16[3,176,4096]{2,1,0:T(8,128)(2,1)}, bf16[3,176,4096]{2,1,0:T(8,128)(2,1)}, u32[]{:S(2)}, u32[]{:S(2)}) collective-permute-start(bf16[3,176,4096]{2,1,0:T(8,128)(2,1)} %bitcast.302), channel_id=1, source_target_pairs={{0,1},{1,0},{2,3},{3,2},{4,5},{5,4},{6,7},{7,6}} | collective-permute-start | bytes 12976136 | tf_op jit(solution)/shard_map/cond/branch_1_fun/ppermute | solution.py:201
  1350.0 47.6 %collective-permute-start.10 = (bf16[3,176,4096]{2,1,0:T(8,128)(2,1)}, bf16[3,176,4096]{2,1,0:T(8,128)(2,1)}, u32[]{:S(2)}, u32[]{:S(2)}) collective-permute-start(bf16[3,176,4096]{2,1,0:T(8,128)(2,1)} %collective-permute-done.5.refs_2_), channel_id=1, source_target_pairs={{0,1},{1,0},{2,3},{3,2},{4,5},{5,4},{6,7},{7,6}} | collective-permute-start | bytes 12976136 | tf_op jit(solution)/shard_map/cond/branch_1_fun/ppermute | solution.py:201
  1350.5 47.1 %collective-permute-start.9 = (bf16[3,176,4096]{2,1,0:T(8,128)(2,1)}, bf16[3,176,4096]{2,1,0:T(8,128)(2,1)}, u32[]{:S(2)}, u32[]{:S(2)}) collective-permute-start(bf16[3,176,4096]{2,1,0:T(8,128)(2,1)} %collective-permute-done.3.refs_1_), channel_id=1, source_target_pairs={{0,1},{1,0},{2,3},{3,2},{4,5},{5,4},{6,7},{7,6}} | collective-permute-start | bytes 12976136 | tf_op jit(solution)/shard_map/cond/branch_1_fun/ppermute | solution.py:201
  1350.5 47.1 %collective-permute-start.11 = (bf16[3,176,4096]{2,1,0:T(8,128)(2,1)}, bf16[3,176,4096]{2,1,0:T(8,128)(2,1)}, u32[]{:S(2)}, u32[]{:S(2)}) collective-permute-start(bf16[3,176,4096]{2,1,0:T(8,128)(2,1)} %collective-permute-done.7.refs_3_), channel_id=1, source_target_pairs={{0,1},{1,0},{2,3},{3,2},{4,5},{5,4},{6,7},{7,6}} | collective-permute-start | bytes 12976136 | tf_op jit(solution)/shard_map/cond/branch_1_fun/ppermute | solution.py:201
  1354.4 43.1 %copy-start.64 = (s32[5]{0:T(128)}, s32[5]{0:T(128)S(1)}, u32[]{:S(2)}) copy-start(s32[5]{0:T(128)S(1)} %select_reduce_fusion.13) | copy-start | bytes 64 | tf_op jit(solution)/shard_map/cond
  1454.3 99.4 %collective-permute-start.16 = (bf16[256,4096]{1,0:T(8,128)(2,1)}, bf16[256,4096]{1,0:T(8,128)(2,1)}, u32[]{:S(2)}, u32[]{:S(2)}) collective-permute-start(bf16[256,4096]{1,0:T(8,128)(2,1)} %fusion.56), channel_id=1, source_target_pairs={{0,4},{1,5},{2,6},{3,7},{4,0},{5,1},{6,2},{7,3}} | collective-permute-start | bytes 6291464 | tf_op jit(solution)/shard_map/cond/branch_1_fun/ppermute | solution.py:201
  1456.9 253.7 %collective-permute-start.17 = (bf16[3,176,4096]{2,1,0:T(8,128)(2,1)}, bf16[3,176,4096]{2,1,0:T(8,128)(2,1)}, u32[]{:S(2)}, u32[]{:S(2)}) collective-permute-start(bf16[3,176,4096]{2,1,0:T(8,128)(2,1)} %bitcast.298), channel_id=1, source_target_pairs={{0,4},{1,5},{2,6},{3,7},{4,0},{5,1},{6,2},{7,3}} | collective-permute-start | bytes 12976136 | tf_op jit(solution)/shard_map/cond/branch_1_fun/ppermute | solution.py:201
  1458.9 431.9 %collective-permute-start.18 = (bf16[3,176,4096]{2,1,0:T(8,128)(2,1)}, bf16[3,176,4096]{2,1,0:T(8,128)(2,1)}, u32[]{:S(2)}, u32[]{:S(2)}) collective-permute-start(bf16[3,176,4096]{2,1,0:T(8,128)(2,1)} %bitcast.295), channel_id=1, source_target_pairs={{0,4},{1,5},{2,6},{3,7},{4,0},{5,1},{6,2},{7,3}} | collective-permute-start | bytes 12976136 | tf_op jit(solution)/shard_map/cond/branch_1_fun/ppermute | solution.py:201
  1458.9 431.9 %collective-permute-start.19 = (bf16[3,176,4096]{2,1,0:T(8,128)(2,1)}, bf16[3,176,4096]{2,1,0:T(8,128)(2,1)}, u32[]{:S(2)}, u32[]{:S(2)}) collective-permute-start(bf16[3,176,4096]{2,1,0:T(8,128)(2,1)} %bitcast.372), channel_id=1, source_target_pairs={{0,2},{1,3},{2,0},{3,1},{4,6},{5,7},{6,4},{7,5}} | collective-permute-start | bytes 12976136 | tf_op jit(solution)/shard_map/cond/branch_1_fun/ppermute | solution.py:201
  1469.2 421.6 %collective-permute-start.20 = (bf16[3,176,4096]{2,1,0:T(8,128)(2,1)}, bf16[3,176,4096]{2,1,0:T(8,128)(2,1)}, u32[]{:S(2)}, u32[]{:S(2)}) collective-permute-start(bf16[3,176,4096]{2,1,0:T(8,128)(2,1)} %bitcast.371), channel_id=1, source_target_pairs={{0,2},{1,3},{2,0},{3,1},{4,6},{5,7},{6,4},{7,5}} | collective-permute-start | bytes 12976136 | tf_op jit(solution)/shard_map/cond/branch_1_fun/ppermute | solution.py:201
  1618.1 297.3 %copy-start.32 = (s32[2304]{0:T(1024)S(1)}, s32[2304]{0:T(1024)}, u32[]{:S(2)}) copy-start(s32[2304]{0:T(1024)} %compare_select_fusion.29) | copy-start | bytes 27652 | tf_op jit(solution)/shard_map/cond
  1618.1 297.3 %copy-start.48 = (s32[1280]{0:T(1024)S(1)}, s32[1280]{0:T(1024)}, u32[]{:S(2)}) copy-start(s32[1280]{0:T(1024)} %select_n.522) | copy-start | bytes 15364 | tf_op jit(solution)/shard_map/cond
  1618.1 303.0 %copy-start.60 = (s32[5,1]{0,1:T(1,128)S(1)}, s32[5,1]{0,1:T(1,128)}, u32[]{:S(2)}) copy-start(s32[5,1]{0,1:T(1,128)} %get-tuple-element.811) | copy-start | bytes 64 | tf_op jit(solution)/shard_map/cond
  1618.1 303.0 %copy-start.65 = (s32[5]{0:T(128)S(1)}, s32[5]{0:T(128)}, u32[]{:S(2)}) copy-start(s32[5]{0:T(128)} %copy-done.64) | copy-start | bytes 64 | tf_op jit(solution)/shard_map/cond
  1618.1 303.8 %copy-start.21 = (s32[1,2048]{1,0:T(1,128)S(1)}, s32[1,2048]{1,0:T(1,128)}, u32[]{:S(2)}) copy-start(s32[1,2048]{1,0:T(1,128)} %copy-done.20) | copy-start | bytes 24580 | tf_op jit(solution)/shard_map/cond
  1618.1 303.8 %copy-start.59 = (s32[256]{0:T(256)S(1)}, s32[256]{0:T(256)}, u32[]{:S(2)}) copy-start(s32[256]{0:T(256)} %get-tuple-element.792) | copy-start | bytes 3076 | tf_op jit(solution)/shard_map/cond
  1902.8 55.5 %collective-permute-start.21 = (bf16[256,4096]{1,0:T(8,128)(2,1)S(1)}, bf16[256,4096]{1,0:T(8,128)(2,1)}, u32[]{:S(2)}, u32[]{:S(2)}) collective-permute-start(bf16[256,4096]{1,0:T(8,128)(2,1)S(1)} %gather_fusion.9), channel_id=1, source_target_pairs={{0,2},{1,3},{2,0},{3,1},{4,6},{5,7},{6,4},{7,5}} | collective-permute-start | bytes 6291464 | tf_op jit(solution)/shard_map/cond/branch_1_fun/ppermute | solution.py:201
  1922.0 366.3 %collective-permute-start.29 = (bf16[3,176,4096]{2,1,0:T(8,128)(2,1)}, bf16[3,176,4096]{2,1,0:T(8,128)(2,1)}, u32[]{:S(2)}, u32[]{:S(2)}) collective-permute-start(bf16[3,176,4096]{2,1,0:T(8,128)(2,1)} %bitcast.299), channel_id=1, source_target_pairs={{0,1},{1,0},{2,3},{3,2},{4,5},{5,4},{6,7},{7,6}} | collective-permute-start | bytes 12976136 | tf_op jit(solution)/shard_map/cond/branch_1_fun/ppermute | solution.py:201
  1922.0 353.4 %collective-permute-start.23 = (bf16[3,176,4096]{2,1,0:T(8,128)(2,1)}, bf16[3,176,4096]{2,1,0:T(8,128)(2,1)}, u32[]{:S(2)}, u32[]{:S(2)}) collective-permute-start(bf16[3,176,4096]{2,1,0:T(8,128)(2,1)} %collective-permute-done.19.refs_2_), channel_id=1, source_target_pairs={{0,4},{1,5},{2,6},{3,7},{4,0},{5,1},{6,2},{7,3}} | collective-permute-start | bytes 12976136 | tf_op jit(solution)/shard_map/cond/branch_1_fun/ppermute | solution.py:201
  1922.0 366.8 %collective-permute-start.31 = (bf16[3,176,4096]{2,1,0:T(8,128)(2,1)}, bf16[3,176,4096]{2,1,0:T(8,128)(2,1)}, u32[]{:S(2)}, u32[]{:S(2)}) collective-permute-start(bf16[3,176,4096]{2,1,0:T(8,128)(2,1)} %collective-permute-done.19.refs_2_), channel_id=1, source_target_pairs={{0,1},{1,0},{2,3},{3,2},{4,5},{5,4},{6,7},{7,6}} | collective-permute-start | bytes 12976136 | tf_op jit(solution)/shard_map/cond/branch_1_fun/ppermute | solution.py:201
  1922.5 352.9 %collective-permute-start.24 = (bf16[3,176,4096]{2,1,0:T(8,128)(2,1)}, bf16[3,176,4096]{2,1,0:T(8,128)(2,1)}, u32[]{:S(2)}, u32[]{:S(2)}) collective-permute-start(bf16[3,176,4096]{2,1,0:T(8,128)(2,1)} %collective-permute-done.20.refs_2_), channel_id=1, source_target_pairs={{0,4},{1,5},{2,6},{3,7},{4,0},{5,1},{6,2},{7,3}} | collective-permute-start | bytes 12976136 | tf_op jit(solution)/shard_map/cond/branch_1_fun/ppermute | solution.py:201
  1958.3 330.4 %collective-permute-start.30 = (bf16[3,176,4096]{2,1,0:T(8,128)(2,1)}, bf16[3,176,4096]{2,1,0:T(8,128)(2,1)}, u32[]{:S(2)}, u32[]{:S(2)}) collective-permute-start(bf16[3,176,4096]{2,1,0:T(8,128)(2,1)} %collective-permute-done.17.refs_1_), channel_id=1, source_target_pairs={{0,1},{1,0},{2,3},{3,2},{4,5},{5,4},{6,7},{7,6}} | collective-permute-start | bytes 12976136 | tf_op jit(solution)/shard_map/cond/branch_1_fun/ppermute | solution.py:201
  2225.3 64.0 %copy-start.58 = (s32[256,1]{0,1:T(1,128)S(1)}, s32[256,1]{0,1:T(1,128)}, u32[]{:S(2)}) copy-start(s32[256,1]{0,1:T(1,128)} %get-tuple-element.807) | copy-start | bytes 3076 | tf_op jit(solution)/shard_map/cond
  2275.4 20.2 collective-permute-start.32
  2288.2 45.1 %collective-permute-start.25 = (bf16[3,176,4096]{2,1,0:T(8,128)(2,1)}, bf16[3,176,4096]{2,1,0:T(8,128)(2,1)}, u32[]{:S(2)}, u32[]{:S(2)}) collective-permute-start(bf16[3,176,4096]{2,1,0:T(8,128)(2,1)} %bitcast.296), channel_id=1, source_target_pairs={{0,1},{1,0},{2,3},{3,2},{4,5},{5,4},{6,7},{7,6}} | collective-permute-start | bytes 12976136 | tf_op jit(solution)/shard_map/cond/branch_1_fun/ppermute | solution.py:201
  2288.3 45.0 %collective-permute-start.27 = (bf16[3,176,4096]{2,1,0:T(8,128)(2,1)}, bf16[3,176,4096]{2,1,0:T(8,128)(2,1)}, u32[]{:S(2)}, u32[]{:S(2)}) collective-permute-start(bf16[3,176,4096]{2,1,0:T(8,128)(2,1)} %collective-permute-done.20.refs_2_), channel_id=1, source_target_pairs={{0,1},{1,0},{2,3},{3,2},{4,5},{5,4},{6,7},{7,6}} | collective-permute-start | bytes 12976136 | tf_op jit(solution)/shard_map/cond/branch_1_fun/ppermute | solution.py:201
  2288.8 44.6 %collective-permute-start.26 = (bf16[3,176,4096]{2,1,0:T(8,128)(2,1)}, bf16[3,176,4096]{2,1,0:T(8,128)(2,1)}, u32[]{:S(2)}, u32[]{:S(2)}) collective-permute-start(bf16[3,176,4096]{2,1,0:T(8,128)(2,1)} %collective-permute-done.18.refs_1_), channel_id=1, source_target_pairs={{0,1},{1,0},{2,3},{3,2},{4,5},{5,4},{6,7},{7,6}} | collective-permute-start | bytes 12976136 | tf_op jit(solution)/shard_map/cond/branch_1_fun/ppermute | solution.py:201
  2288.8 44.5 %collective-permute-start.28 = (bf16[3,176,4096]{2,1,0:T(8,128)(2,1)}, bf16[3,176,4096]{2,1,0:T(8,128)(2,1)}, u32[]{:S(2)}, u32[]{:S(2)}) collective-permute-start(bf16[3,176,4096]{2,1,0:T(8,128)(2,1)} %collective-permute-done.24.refs_3_), channel_id=1, source_target_pairs={{0,1},{1,0},{2,3},{3,2},{4,5},{5,4},{6,7},{7,6}} | collective-permute-start | bytes 12976136 | tf_op jit(solution)/shard_map/cond/branch_1_fun/ppermute | solution.py:201
  2386.7 47.9 %collective-permute-start.33 = (bf16[256,4096]{1,0:T(8,128)(2,1)S(1)}, bf16[256,4096]{1,0:T(8,128)(2,1)S(1)}, u32[]{:S(2)}, u32[]{:S(2)}) collective-permute-start(bf16[256,4096]{1,0:T(8,128)(2,1)S(1)} %fusion.55), channel_id=1, source_target_pairs={{0,2},{1,3},{2,0},{3,1},{4,6},{5,7},{6,4},{7,5}} | collective-permute-start | bytes 6291464 | tf_op jit(solution)/shard_map/cond/branch_1_fun/ppermute | solution.py:201
  2486.5 45.4 %copy-start.34 = (f32[2048]{0:T(1024)S(1)}, f32[2048]{0:T(1024)}, u32[]{:S(2)}) copy-start(f32[2048]{0:T(1024)} %slice_reduce_fusion) | copy-start | bytes 24580 | tf_op jit(solution)/shard_map/cond
  2486.6 45.4 %copy-start.40 = (pred[2048]{0:T(1024)(128)(4,1)S(1)}, pred[2048]{0:T(1024)(128)(4,1)}, u32[]{:S(2)}) copy-start(pred[2048]{0:T(1024)(128)(4,1)} %copy-done.37) | copy-start | bytes 6148 | tf_op jit(solution)/shard_map/cond
  (27 other events, 445.7 us)
Sparse Core Ops, SparseCore 0:
  63.4 206.0 all-gather.11
  271.4 160.8 all-gather.15
  434.1 269.8 all-gather.13
  705.7 295.2 all-gather.17
  1002.7 234.5 all-gather.19
  1238.9 160.7 all-gather.23
  1401.6 256.1 all-gather.21
  1659.6 269.5 all-gather.25

commit v3 on v2

--- a/solution.py
+++ b/solution.py
@@ -313,7 +313,8 @@
                     coming = [all_of(top_w)] + [all_of(w) for w in heavy_w]
                     own_x2, sent2 = [hop(w, share[l + 1]) for w in own2], [hop(w, lend[l + 1]) for w in other2]
                 out = None
-                for k in range(1, NG - 1):
+                early = NG - 1 if l + 1 < n_layers else min(2, NG - 1)
+                for k in range(1, early):
                     out = gathered(k, out, full[k])
                 far = after(far, acc if out is None else out)
                 for j in range(n_light):
@@ -322,12 +323,14 @@
                 seen = acc[n_tok:] + g1[n_tok:] * take(out, pos[n_tok:])
                 guest = seen.astype(jnp.bfloat16)
                 back = hop(guest, lend[l])
+                for k in range(early, NG - 1):
+                    out = gathered(k, out, after(full[k], guest))
                 home_again = lambda: take(back, place)
                 if l + 1 < n_layers:
                     late = after(full[NG - 1], guest)
                 else:
                     returned = home_again()
-                    late = after(full[NG - 1], guest, returned)
+                    late = after(full[NG - 1], out, returned)
                     home_again = lambda: returned
                 out = gathered(NG - 1, out, late)
                 mixed = (acc[:n_tok] + g1[:n_tok] * take(out, pos[:n_tok])).astype(jnp.bfloat16)

time: 2580 us -> 2550 us (0.988)
  waiting for transfers between devices: 1120 us -> 1070 us
    ppermute x34, waiting for transfers between devices: 1110 us -> 1070 us  [hop(): return lax.ppermute(a, 'fsdp', [(i, i ^ bit) for i in range(n_dev)])]
  transfers between devices with their start and end apart: 42 -> 42, of which waited for: 12 -> 11; matrix products, arithmetic and copies ran while one was open for 17% -> 18% of each run, Pallas kernels for 30% -> 30%
where the time goes in v3:
time: 2550 us; the launch traced here: 2540 us
  waiting for transfers between devices  1070 us (42%)
  Pallas kernels  819 us (32%)
  local copies, waits for them, and re-layouts  401 us (16%)
  other arithmetic  147 us (6%)
  starting transfers between devices  53.6 us (2%)
    ppermute x34, waiting for transfers between devices, hop(): return lax.ppermute(a, 'fsdp', [(i, i ^ bit) for i in range(n_dev)])  1070 us
    pallas_call x12, Pallas kernels, expert(): pl.pallas_call(functools.partial(expert_body, pieces, len(weights), alias...  667 us
    gather x10, local copies, waits for them, and re-layouts, take(): return table.at[index].get(mode='promise_in_bounds')  344 us
    pallas_call x4, Pallas kernels, prep(): pl.pallas_call(functools.partial(prep_body, groups, n_exp), out_shape=[ja...  151 us
    select_n x2, other arithmetic, adaptive(): x = jnp.where(my_lent[l][:, None], home_again(), mixed)  60.5 us
    ppermute x34, starting transfers between devices, hop(): return lax.ppermute(a, 'fsdp', [(i, i ^ bit) for i in range(n_dev)])  52.8 us
  transfers between devices with their start and end apart: 42, of which 11 were waited for; matrix products, arithmetic and copies ran while one was open for 18% of the time, Pallas kernels for 30%

profile of v3, /device:TPU:0, one launch (start us, length us, event | category | flops | bytes accessed | tf_op | source)
XLA Modules:
  0.0 2543.4 jit_solution(2903807974838075889)
XLA Ops:
  6.5 14.4 all-gather
  27.2 2502.9 %conditional.1 = (bf16[2048,4096]{1,0:T(8,128)(2,1)S(1)}) conditional(s32[]{:T(128)} %convert_element_type.241, (bf16[2048,4096]{1,0:T(8,128)(2,1)}, s32[2,2,2048]{2,1,0:T(2,128)}, f32[2,4096]{1,0:T(2,128)}, bf16[2,4096,8]{1,2,0:T(8,128)(2,1)}, bf16[2,8,4096,172]{2,1,3,0:T(8,128)(2,1)}, /*index=5*/bf16[2,8,4096,172]{2,1,3,0:T(8,128)(2,1)}, ...), branch_computations={%region_11.34_spmd, %region_34.61_spmd} | conditional | flops 46115446784 | bytes 3621014528 | solution.py:343
  42.0 21.3 prep.14
  63.4 54.2 %prep.15 = (bf16[1,3,176,4096]{3,2,1,0:T(8,128)(2,1)}, bf16[1,3,176,4096]{3,2,1,0:T(8,128)(2,1)}, bf16[1,3,176,4096]{3,2,1,0:T(8,128)(2,1)}, bf16[1,3,176,4096]{...) custom-call(s32[7]{0:T(128)} %get-tuple-element.402.s_ref, ...), custom_call_target="tpu_custom_call" | custom-call | flops 4200000000 | bytes 100100000 | tf_op jit(solution)/shard_map/cond/branch_1_fun/prep/pallas_call | solution.py:49
  120.3 5.1 sort.98
  125.5 16.6 gather_fusion
  142.1 2.0 collective-permute-start.1
  145.9 8.3 constant_dynamic-update-slice_fusion.1
  154.9 79.0 %collective-permute-done.1 = s32[256]{0:T(256)S(1)} collective-permute-done((s32[256]{0:T(256)S(1)}, s32[256]{0:T(256)S(1)}, u32[]{:S(2)}, u32[]{:S(2)}) %collective-permute-start.1) | collective-permute-done | bytes 1056 | tf_op jit(solution)/shard_map/cond/branch_1_fun/ppermute | solution.py:201
  234.1 4.4 fusion.45
  240.6 11.8 fusion.47.h_ref
  252.4 6.5 copy-done.2
  258.8 5.0 select_reduce_fusion.10
  265.8 3.8 all-gather.12.cloned.1.call-done.refs_0_
  269.5 128.8 %expert.22 = f32[2304,4096]{1,0:T(8,128)} custom-call(s32[2]{0:T(128)} %broadcast_multiply_fusion.2.s_ref, bf16[2304,4096]{1,0:T(8,128)(2,1)} %copy-done.2, bf16[8,3,176,4096]{3,2,1,0:T(8,128)(2,1)} %all-gather.12.cloned.1.call-done.refs_0_, bf16[2304,4096]{1,0:T(8,128)(2,1)} %copy-done.5, f32[2304,1]{1,0:T(8,128)} %bitcast.289), custom_call_target="tpu_custom_call" | custom-call | flops 3000000000 | bytes 60000000 | tf_op jit(solution)/shard_map/cond/branch_1_fun/expert/pallas_call | solution.py:132
  398.4 21.5 prep.17
  419.9 54.3 %prep.16 = (bf16[1,3,176,4096]{3,2,1,0:T(8,128)(2,1)}, bf16[1,3,176,4096]{3,2,1,0:T(8,128)(2,1)}, bf16[1,3,176,4096]{3,2,1,0:T(8,128)(2,1)}, bf16[1,3,176,4096]{...) custom-call(s32[7]{0:T(128)} %get-tuple-element.419.s_ref, ...), custom_call_target="tpu_custom_call" | custom-call | flops 4200000000 | bytes 100100000 | tf_op jit(solution)/shard_map/cond/branch_1_fun/prep/pallas_call | solution.py:49
  477.8 2.0 collective-permute-start.5
  479.8 178.4 %collective-permute-done.2.refs_1_ = bf16[3,176,4096]{2,1,0:T(8,128)(2,1)} collective-permute-done((bf16[3,176,4096]{2,1,0:T(8,128)(2,1)}, bf16[3,176,4096]{2,1,0:T(8,128)(2,1)}, u32[]{:S(2)}, u32[]{:S(2)}) %collective-permute-start.2) | collective-permute-done | bytes 4325408 | tf_op jit(solution)/shard_map/cond/branch_1_fun/ppermute | solution.py:201
  658.2 161.5 %collective-permute-done.3.refs_1_ = bf16[3,176,4096]{2,1,0:T(8,128)(2,1)} collective-permute-done((bf16[3,176,4096]{2,1,0:T(8,128)(2,1)}, bf16[3,176,4096]{2,1,0:T(8,128)(2,1)}, u32[]{:S(2)}, u32[]{:S(2)}) %collective-permute-start.3) | collective-permute-done | bytes 4325408 | tf_op jit(solution)/shard_map/cond/branch_1_fun/ppermute | solution.py:201
  822.6 5.1 sort.100
  829.7 342.3 %collective-permute-done.22 = s32[256]{0:T(256)S(1)} collective-permute-done((s32[256]{0:T(256)S(1)}, s32[256]{0:T(256)S(1)}, u32[]{:S(2)}, u32[]{:S(2)}) %collective-permute-start.22) | collective-permute-done | bytes 1056 | tf_op jit(solution)/shard_map/cond/branch_1_fun/ppermute | solution.py:201
  1173.5 5.8 sort.99
  1183.3 57.8 %gather_fusion.5 = bf16[3584,4096]{1,0:T(8,128)(2,1)} fusion(bf16[2304,4096]{1,0:T(8,128)(2,1)} %copy-done.2, s32[4096]{0:T(1024)S(1)} %pad_clamp_fusion.1), kind=kCustom, calls=%fused_computation.11 | custom fusion | bytes 58734592 | tf_op jit(solution)/shard_map/cond/branch_1_fun/gather | solution.py:194
  1241.1 53.9 %expert.23.refs_1_ = f32[3584,4096]{1,0:T(8,128)} custom-call(s32[2]{0:T(128)} %get-tuple-element.713.s_ref, bf16[3584,4096]{1,0:T(8,128)(2,1)} %gather_fusion.5, bf16[8,3,176,4096]{3,2,1,0:T(8,128)(2,1)} %all-gather.16.cloned.1.call-done.refs_0_), custom_call_target="tpu_custom_call" | custom-call | flops 3000000000 | bytes 60000000 | tf_op jit(solution)/shard_map/cond/branch_1_fun/expert/pallas_call | solution.py:132
  1295.2 54.0 %expert.24.refs_8_ = f32[3584,4096]{1,0:T(8,128)} custom-call(s32[2]{0:T(128)} %get-tuple-element.714.s_ref, bf16[3584,4096]{1,0:T(8,128)(2,1)} %gather_fusion.5, bf16[8,3,176,4096]{3,2,1,0:T(8,128)(2,1)} %all-gather.14.cloned.1.call-done.refs_0_, f32[3584,4096]{1,0:T(8,128)} %expert.23.refs_1_), custom_call_target="tpu_custom_call", output_to_operand_aliasing={{}: (3, {})} | custom-call | flops 3000000000 | bytes 60000000 | tf_op jit(solution)/shard_map/cond/branch_1_fun/expert/pallas_call | solution.py:132
  1357.0 2.6 collective-permute-done.15.refs_7_
  1359.6 37.9 %expert.25.refs_8_ = f32[3584,4096]{1,0:T(8,128)} custom-call(s32[2]{0:T(128)} %get-tuple-element.712.s_ref, bf16[3584,4096]{1,0:T(8,128)(2,1)} %gather_fusion.5, bf16[3,176,4096]{2,1,0:T(8,128)(2,1)} %bitcast.306, bf16[3,176,4096]{2,1,0:T(8,128)(2,1)} %collective-permute-done.2.refs_1_, ...), custom_call_target="tpu_custom_call", output_to_operand_aliasing={{}: (10, {})} | custom-call | flops 3000000000 | bytes 60000000 | tf_op jit(solution)/shard_map/cond/branch_1_fun/expert/pallas_call | solution.py:132
  1397.5 27.3 %expert.26.refs_1_ = f32[3584,4096]{1,0:T(8,128)} custom-call(s32[2]{0:T(128)} %get-tuple-element.715.s_ref, bf16[3584,4096]{1,0:T(8,128)(2,1)} %gather_fusion.5, bf16[3,176,4096]{2,1,0:T(8,128)(2,1)} %bitcast.303, bf16[3,176,4096]{2,1,0:T(8,128)(2,1)} %collective-permute-done.3.refs_1_, ...), custom_call_target="tpu_custom_call", output_to_operand_aliasing={{}: (10, {})} | custom-call | flops 3000000000 | bytes 60000000 | tf_op jit(solution)/shard_map/cond/branch_1_fun/expert/pallas_call | solution.py:132
  1424.9 23.6 gather_fusion.6
  1448.5 5.7 fusion.56
  1456.7 2.0 collective-permute-start.17
  1458.8 10.5 collective-permute-start.19
  1469.3 39.0 %expert.27 = f32[3584,4096]{1,0:T(8,128)} custom-call(s32[2]{0:T(128)} %get-tuple-element.711.s_ref, bf16[3584,4096]{1,0:T(8,128)(2,1)} %gather_fusion.5, bf16[8,3,176,4096]{3,2,1,0:T(8,128)(2,1)} %all-gather.18.cloned.1.call-done.refs_0_, f32[3584,4096]{1,0:T(8,128)} %expert.26.refs_1_), custom_call_target="tpu_custom_call", output_to_operand_aliasing={{}: (3, {})} | custom-call | flops 3000000000 | bytes 60000000 | tf_op jit(solution)/shard_map/cond/branch_1_fun/expert/pallas_call | solution.py:132
  1508.3 45.7 %gather_fusion.8 = f32[2048,4096]{1,0:T(8,128)} fusion(f32[3584,4096]{1,0:T(8,128)} %expert.27, s32[2048]{0:T(1024)S(1)} %broadcast_clamp_fusion.5), kind=kCustom, calls=%fused_computation.14 | custom fusion | bytes 67117056 | tf_op jit(solution)/shard_map/cond/branch_1_fun/gather | solution.py:194
  1554.0 30.5 %gather_fusion.7 = bf16[2048,4096]{1,0:T(8,128)(2,1)} fusion(bf16[256,4096]{1,0:T(8,128)(2,1)} %collective-permute-done.16, s32[2048]{0:T(1024)S(1)} %broadcast_clamp_fusion.7), kind=kCustom, calls=%fused_computation.13 | custom fusion | bytes 33562624 | tf_op jit(solution)/shard_map/cond/branch_1_fun/gather | solution.py:194
  1584.5 33.9 %fusion.53 = bf16[2048,4096]{1,0:T(8,128)(2,1)} fusion(bf16[2048,4096]{1,0:T(8,128)(2,1)} %gather_fusion.7, f32[2048,4096]{1,0:T(8,128)} %gather_fusion.8, f32[2304,4096]{1,0:T(8,128)} %expert.22, f32[2048]{0:T(1024)S(1)} %copy-done.33, pred[2048]{0:T(1024)(128)(4,1)S(1)} %copy-done.43), kind=kLoop, calls=%fused_computation.164 | loop fusion | flops 33554432 | bytes 100673536 | tf_op jit(solution)/shard_map/cond/branch_1_fun/jit(_where)/select_n | solution.py:337
  1618.4 92.1 %collective-permute-done.17.refs_1_ = bf16[3,176,4096]{2,1,0:T(8,128)(2,1)} collective-permute-done((bf16[3,176,4096]{2,1,0:T(8,128)(2,1)}, bf16[3,176,4096]{2,1,0:T(8,128)(2,1)}, u32[]{:S(2)}, u32[]{:S(2)}) %collective-permute-start.17) | collective-permute-done | bytes 4325408 | tf_op jit(solution)/shard_map/cond/branch_1_fun/ppermute | solution.py:201
  1710.5 180.2 %collective-permute-done.18.refs_1_ = bf16[3,176,4096]{2,1,0:T(8,128)(2,1)} collective-permute-done((bf16[3,176,4096]{2,1,0:T(8,128)(2,1)}, bf16[3,176,4096]{2,1,0:T(8,128)(2,1)}, u32[]{:S(2)}, u32[]{:S(2)}) %collective-permute-start.18) | collective-permute-done | bytes 4325408 | tf_op jit(solution)/shard_map/cond/branch_1_fun/ppermute | solution.py:201
  1890.7 11.9 gather_fusion.9
  1902.7 12.4 collective-permute-start.21
  1915.1 5.8 sort.101
  1924.0 8.4 constant_dynamic-update-slice_fusion.3
  1932.5 25.6 %collective-permute-done.21 = bf16[256,4096]{1,0:T(8,128)(2,1)} collective-permute-done((bf16[256,4096]{1,0:T(8,128)(2,1)S(1)}, bf16[256,4096]{1,0:T(8,128)(2,1)}, u32[]{:S(2)}, u32[]{:S(2)}) %collective-permute-start.21) | collective-permute-done | bytes 2097184 | tf_op jit(solution)/shard_map/cond/branch_1_fun/ppermute | solution.py:201
  1959.9 4.4 fusion.48
  1964.3 2.0 copy-done.6
  1966.3 11.8 fusion.50.h_ref
  1978.2 6.4 copy-done.3
  1984.6 5.0 select_reduce_fusion.8
  1990.1 57.8 %gather_fusion.10 = bf16[3584,4096]{1,0:T(8,128)(2,1)} fusion(bf16[2304,4096]{1,0:T(8,128)(2,1)} %copy-done.3, s32[4096]{0:T(1024)S(1)} %pad_clamp_fusion), kind=kCustom, calls=%fused_computation.16 | custom fusion | bytes 58734592 | tf_op jit(solution)/shard_map/cond/branch_1_fun/gather | solution.py:194
  2049.3 125.6 %expert.28 = f32[2304,4096]{1,0:T(8,128)} custom-call(s32[2]{0:T(128)} %broadcast_multiply_fusion.2.s_ref, bf16[2304,4096]{1,0:T(8,128)(2,1)} %copy-done.3, bf16[8,3,176,4096]{3,2,1,0:T(8,128)(2,1)} %all-gather.20.cloned.1.call-done.refs_0_, bf16[2304,4096]{1,0:T(8,128)(2,1)} %copy-done.6, f32[2304,1]{1,0:T(8,128)} %bitcast.290), custom_call_target="tpu_custom_call" | custom-call | flops 3000000000 | bytes 60000000 | tf_op jit(solution)/shard_map/cond/branch_1_fun/expert/pallas_call | solution.py:132
  2175.0 50.1 %expert.29.refs_8_ = f32[3584,4096]{1,0:T(8,128)} custom-call(s32[2]{0:T(128)} %get-tuple-element.709.s_ref, bf16[3584,4096]{1,0:T(8,128)(2,1)} %gather_fusion.10, bf16[8,3,176,4096]{3,2,1,0:T(8,128)(2,1)} %all-gather.22.cloned.1.call-done.refs_0_), custom_call_target="tpu_custom_call" | custom-call | flops 3000000000 | bytes 60000000 | tf_op jit(solution)/shard_map/cond/branch_1_fun/expert/pallas_call | solution.py:132
  2225.1 12.9 collective-permute-start.32
  2240.1 5.2 collective-permute-done.32.refs_7_
  2245.2 37.7 %expert.30.refs_8_ = f32[3584,4096]{1,0:T(8,128)} custom-call(s32[2]{0:T(128)} %get-tuple-element.708.s_ref, bf16[3584,4096]{1,0:T(8,128)(2,1)} %gather_fusion.10, bf16[3,176,4096]{2,1,0:T(8,128)(2,1)} %bitcast.300, bf16[3,176,4096]{2,1,0:T(8,128)(2,1)} %collective-permute-done.17.refs_1_, ...), custom_call_target="tpu_custom_call", output_to_operand_aliasing={{}: (10, {})} | custom-call | flops 3000000000 | bytes 60000000 | tf_op jit(solution)/shard_map/cond/branch_1_fun/expert/pallas_call | solution.py:132
  2283.0 25.3 expert.31.refs_1_
  2308.3 23.6 gather_fusion.11
  2332.0 5.7 fusion.55
  2339.3 50.1 %expert.32.refs_1_ = f32[3584,4096]{1,0:T(8,128)} custom-call(s32[2]{0:T(128)} %get-tuple-element.706.s_ref, bf16[3584,4096]{1,0:T(8,128)(2,1)} %gather_fusion.10, bf16[8,3,176,4096]{3,2,1,0:T(8,128)(2,1)} %all-gather.26.cloned.1.call-done.refs_0_, f32[3584,4096]{1,0:T(8,128)} %expert.31.refs_1_), custom_call_target="tpu_custom_call", output_to_operand_aliasing={{}: (3, {})} | custom-call | flops 3000000000 | bytes 60000000 | tf_op jit(solution)/shard_map/cond/branch_1_fun/expert/pallas_call | solution.py:132
  2389.4 30.7 %gather_fusion.12 = bf16[2048,4096]{1,0:T(8,128)(2,1)} fusion(bf16[256,4096]{1,0:T(8,128)(2,1)} %collective-permute-done.33, s32[2048]{0:T(1024)S(1)} %broadcast_clamp_fusion.6), kind=kCustom, calls=%fused_computation.18 | custom fusion | bytes 33562624 | tf_op jit(solution)/shard_map/cond/branch_1_fun/gather | solution.py:194
  2420.1 37.7 %expert.33 = f32[3584,4096]{1,0:T(8,128)} custom-call(s32[2]{0:T(128)} %get-tuple-element.707.s_ref, bf16[3584,4096]{1,0:T(8,128)(2,1)} %gather_fusion.10, bf16[8,3,176,4096]{3,2,1,0:T(8,128)(2,1)} %all-gather.24.cloned.1.call-done.refs_0_, f32[3584,4096]{1,0:T(8,128)} %expert.32.refs_1_), custom_call_target="tpu_custom_call", output_to_operand_aliasing={{}: (3, {})} | custom-call | flops 3000000000 | bytes 60000000 | tf_op jit(solution)/shard_map/cond/branch_1_fun/expert/pallas_call | solution.py:132
  2457.8 45.4 %gather_fusion.13 = f32[2048,4096]{1,0:T(8,128)} fusion(f32[3584,4096]{1,0:T(8,128)} %expert.33, s32[2048]{0:T(1024)S(1)} %broadcast_clamp_fusion.4), kind=kCustom, calls=%fused_computation.19 | custom fusion | bytes 67117056 | tf_op jit(solution)/shard_map/cond/branch_1_fun/gather | solution.py:194
  2503.2 26.7 %fusion.54 = bf16[2048,4096]{1,0:T(8,128)(2,1)S(1)} fusion(bf16[2048,4096]{1,0:T(8,128)(2,1)} %gather_fusion.12, f32[2048,4096]{1,0:T(8,128)} %gather_fusion.13, f32[2304,4096]{1,0:T(8,128)} %expert.28, f32[2048]{0:T(1024)S(1)} %copy-done.34, pred[2048]{0:T(1024)(128)(4,1)S(1)} %copy-done.40), kind=kLoop, calls=%fused_computation.165 | loop fusion | flops 33554432 | bytes 100673536 | tf_op jit(solution)/shard_map/cond/branch_1_fun/jit(_where)/select_n | solution.py:337
  2530.1 6.2 copy-done.8
  (304 shorter events, 55.1 us)
Async XLA Ops:
  35.9 233.6 %all-gather.12.cloned.1.call-start = ((), (), s32[]{:S(2)}) async-start(), calls=%async_computation | async-start | bytes 38928384 | tf_op jit(solution)/shard_map/cond/branch_1_fun/all_gather | solution.py:273
  63.3 55.8 %copy-start.52 = (s32[2,8]{1,0:T(2,128)S(1)}, s32[2,8]{1,0:T(2,128)}, u32[]{:S(2)}) copy-start(s32[2,8]{1,0:T(2,128)} %copy-done.51) | copy-start | bytes 196 | tf_op jit(solution)/shard_map/cond
  63.3 1177.8 %all-gather.16.cloned.1.call-start = ((), (), s32[]{:S(2)}) async-start(), calls=%async_computation.2 | async-start | bytes 38928384 | tf_op jit(solution)/shard_map/cond/branch_1_fun/all_gather | solution.py:273
  117.6 1177.5 %all-gather.14.cloned.1.call-start = ((), (), s32[]{:S(2)}) async-start(), calls=%async_computation.1 | async-start | bytes 38928384 | tf_op jit(solution)/shard_map/cond/branch_1_fun/all_gather | solution.py:273
  118.3 1350.9 %all-gather.18.cloned.1.call-start = ((), (), s32[]{:S(2)}) async-start(), calls=%async_computation.3 | async-start | bytes 38928384 | tf_op jit(solution)/shard_map/cond/branch_1_fun/all_gather | solution.py:273
  118.9 1930.4 %all-gather.20.cloned.1.call-start = ((), (), s32[]{:S(2)}) async-start(), calls=%async_computation.4 | async-start | bytes 38928384 | tf_op jit(solution)/shard_map/cond/branch_1_fun/all_gather | solution.py:273
  119.1 35.1 %copy-start.41 = (pred[2048]{0:T(1024)(128)(4,1)}, pred[2048]{0:T(1024)(128)(4,1)S(1)}, u32[]{:S(2)}) copy-start(pred[2048]{0:T(1024)(128)(4,1)S(1)} %get-tuple-element.699) | copy-start | bytes 6148 | tf_op jit(solution)/shard_map/cond
  119.1 702.9 %copy-start.37 = (pred[2048]{0:T(1024)(128)(4,1)}, pred[2048]{0:T(1024)(128)(4,1)S(1)}, u32[]{:S(2)}) copy-start(pred[2048]{0:T(1024)(128)(4,1)S(1)} %get-tuple-element.698) | copy-start | bytes 6148 | tf_op jit(solution)/shard_map/cond
  120.3 701.8 %copy-start.20 = (s32[1,2048]{1,0:T(1,128)}, s32[1,2048]{1,0:T(1,128)S(1)}, u32[]{:S(2)}) copy-start(s32[1,2048]{1,0:T(1,128)S(1)} %get-tuple-element.784) | copy-start | bytes 24580 | tf_op jit(solution)/shard_map/cond
  142.1 91.8 %collective-permute-start = (bf16[256,4096]{1,0:T(8,128)(2,1)S(1)}, bf16[256,4096]{1,0:T(8,128)(2,1)S(1)}, u32[]{:S(2)}, u32[]{:S(2)}) collective-permute-start(bf16[256,4096]{1,0:T(8,128)(2,1)S(1)} %gather_fusion), channel_id=1, source_target_pairs={{0,4},{1,5},{2,6},{3,7},{4,0},{5,1},{6,2},{7,3}} | collective-permute-start | bytes 6291464 | tf_op jit(solution)/shard_map/cond/branch_1_fun/ppermute | solution.py:201
  142.1 91.8 %collective-permute-start.1 = (s32[256]{0:T(256)S(1)}, s32[256]{0:T(256)S(1)}, u32[]{:S(2)}, u32[]{:S(2)}) collective-permute-start(s32[256]{0:T(256)S(1)} %slice.211), channel_id=1, source_target_pairs={{0,4},{1,5},{2,6},{3,7},{4,0},{5,1},{6,2},{7,3}} | collective-permute-start | bytes 3080 | tf_op jit(solution)/shard_map/cond/branch_1_fun/ppermute | solution.py:201
  419.9 1755.0 %all-gather.22.cloned.1.call-start = ((), (), s32[]{:S(2)}) async-start(), calls=%async_computation.5 | async-start | bytes 38928384 | tf_op jit(solution)/shard_map/cond/branch_1_fun/all_gather | solution.py:273
  474.2 1865.0 %all-gather.26.cloned.1.call-start = ((), (), s32[]{:S(2)}) async-start(), calls=%async_computation.7 | async-start | bytes 38928384 | tf_op jit(solution)/shard_map/cond/branch_1_fun/all_gather | solution.py:273
  475.0 1945.1 %all-gather.24.cloned.1.call-start = ((), (), s32[]{:S(2)}) async-start(), calls=%async_computation.6 | async-start | bytes 38928384 | tf_op jit(solution)/shard_map/cond/branch_1_fun/all_gather | solution.py:273
  475.7 182.5 %collective-permute-start.2 = (bf16[3,176,4096]{2,1,0:T(8,128)(2,1)}, bf16[3,176,4096]{2,1,0:T(8,128)(2,1)}, u32[]{:S(2)}, u32[]{:S(2)}) collective-permute-start(bf16[3,176,4096]{2,1,0:T(8,128)(2,1)} %bitcast.304), channel_id=1, source_target_pairs={{0,2},{1,3},{2,0},{3,1},{4,6},{5,7},{6,4},{7,5}} | collective-permute-start | bytes 12976136 | tf_op jit(solution)/shard_map/cond/branch_1_fun/ppermute | solution.py:201
  476.8 342.9 %collective-permute-start.3 = (bf16[3,176,4096]{2,1,0:T(8,128)(2,1)}, bf16[3,176,4096]{2,1,0:T(8,128)(2,1)}, u32[]{:S(2)}, u32[]{:S(2)}) collective-permute-start(bf16[3,176,4096]{2,1,0:T(8,128)(2,1)} %bitcast.301), channel_id=1, source_target_pairs={{0,2},{1,3},{2,0},{3,1},{4,6},{5,7},{6,4},{7,5}} | collective-permute-start | bytes 12976136 | tf_op jit(solution)/shard_map/cond/branch_1_fun/ppermute | solution.py:201
  477.8 341.9 %collective-permute-start.4 = (bf16[3,176,4096]{2,1,0:T(8,128)(2,1)}, bf16[3,176,4096]{2,1,0:T(8,128)(2,1)}, u32[]{:S(2)}, u32[]{:S(2)}) collective-permute-start(bf16[3,176,4096]{2,1,0:T(8,128)(2,1)} %bitcast.374), channel_id=1, source_target_pairs={{0,4},{1,5},{2,6},{3,7},{4,0},{5,1},{6,2},{7,3}} | collective-permute-start | bytes 12976136 | tf_op jit(solution)/shard_map/cond/branch_1_fun/ppermute | solution.py:201
  477.8 342.2 %collective-permute-start.5 = (bf16[3,176,4096]{2,1,0:T(8,128)(2,1)}, bf16[3,176,4096]{2,1,0:T(8,128)(2,1)}, u32[]{:S(2)}, u32[]{:S(2)}) collective-permute-start(bf16[3,176,4096]{2,1,0:T(8,128)(2,1)} %bitcast.373), channel_id=1, source_target_pairs={{0,4},{1,5},{2,6},{3,7},{4,0},{5,1},{6,2},{7,3}} | collective-permute-start | bytes 12976136 | tf_op jit(solution)/shard_map/cond/branch_1_fun/ppermute | solution.py:201
  820.0 529.2 %collective-permute-start.6 = (bf16[3,176,4096]{2,1,0:T(8,128)(2,1)}, bf16[3,176,4096]{2,1,0:T(8,128)(2,1)}, u32[]{:S(2)}, u32[]{:S(2)}) collective-permute-start(bf16[3,176,4096]{2,1,0:T(8,128)(2,1)} %collective-permute-done.4.refs_2_), channel_id=1, source_target_pairs={{0,2},{1,3},{2,0},{3,1},{4,6},{5,7},{6,4},{7,5}} | collective-permute-start | bytes 12976136 | tf_op jit(solution)/shard_map/cond/branch_1_fun/ppermute | solution.py:201
  821.4 527.8 %collective-permute-start.7 = (bf16[3,176,4096]{2,1,0:T(8,128)(2,1)}, bf16[3,176,4096]{2,1,0:T(8,128)(2,1)}, u32[]{:S(2)}, u32[]{:S(2)}) collective-permute-start(bf16[3,176,4096]{2,1,0:T(8,128)(2,1)} %collective-permute-done.5.refs_2_), channel_id=1, source_target_pairs={{0,2},{1,3},{2,0},{3,1},{4,6},{5,7},{6,4},{7,5}} | collective-permute-start | bytes 12976136 | tf_op jit(solution)/shard_map/cond/branch_1_fun/ppermute | solution.py:201
  827.8 344.2 %collective-permute-start.22 = (s32[256]{0:T(256)S(1)}, s32[256]{0:T(256)S(1)}, u32[]{:S(2)}, u32[]{:S(2)}) collective-permute-start(s32[256]{0:T(256)S(1)} %slice.232), channel_id=1, source_target_pairs={{0,2},{1,3},{2,0},{3,1},{4,6},{5,7},{6,4},{7,5}} | collective-permute-start | bytes 3080 | tf_op jit(solution)/shard_map/cond/branch_1_fun/ppermute | solution.py:201
  829.2 520.8 %collective-permute-start.12 = (bf16[3,176,4096]{2,1,0:T(8,128)(2,1)}, bf16[3,176,4096]{2,1,0:T(8,128)(2,1)}, u32[]{:S(2)}, u32[]{:S(2)}) collective-permute-start(bf16[3,176,4096]{2,1,0:T(8,128)(2,1)} %bitcast.305), channel_id=1, source_target_pairs={{0,1},{1,0},{2,3},{3,2},{4,5},{5,4},{6,7},{7,6}} | collective-permute-start | bytes 12976136 | tf_op jit(solution)/shard_map/cond/branch_1_fun/ppermute | solution.py:201
  829.2 521.2 %collective-permute-start.13 = (bf16[3,176,4096]{2,1,0:T(8,128)(2,1)}, bf16[3,176,4096]{2,1,0:T(8,128)(2,1)}, u32[]{:S(2)}, u32[]{:S(2)}) collective-permute-start(bf16[3,176,4096]{2,1,0:T(8,128)(2,1)} %collective-permute-done.2.refs_1_), channel_id=1, source_target_pairs={{0,1},{1,0},{2,3},{3,2},{4,5},{5,4},{6,7},{7,6}} | collective-permute-start | bytes 12976136 | tf_op jit(solution)/shard_map/cond/branch_1_fun/ppermute | solution.py:201
  1172.0 178.5 %collective-permute-start.14 = (bf16[3,176,4096]{2,1,0:T(8,128)(2,1)}, bf16[3,176,4096]{2,1,0:T(8,128)(2,1)}, u32[]{:S(2)}, u32[]{:S(2)}) collective-permute-start(bf16[3,176,4096]{2,1,0:T(8,128)(2,1)} %collective-permute-done.4.refs_2_), channel_id=1, source_target_pairs={{0,1},{1,0},{2,3},{3,2},{4,5},{5,4},{6,7},{7,6}} | collective-permute-start | bytes 12976136 | tf_op jit(solution)/shard_map/cond/branch_1_fun/ppermute | solution.py:201
  1295.1 56.9 %copy-start.38 = (pred[2048]{0:T(1024)(128)(4,1)S(1)}, pred[2048]{0:T(1024)(128)(4,1)}, u32[]{:S(2)}) copy-start(pred[2048]{0:T(1024)(128)(4,1)} %copy-done.37) | copy-start | bytes 6148 | tf_op jit(solution)/shard_map/cond
  1295.1 56.9 %copy-start.42 = (pred[2048]{0:T(1024)(128)(4,1)S(1)}, pred[2048]{0:T(1024)(128)(4,1)}, u32[]{:S(2)}) copy-start(pred[2048]{0:T(1024)(128)(4,1)} %copy-done.41) | copy-start | bytes 6148 | tf_op jit(solution)/shard_map/cond
  1295.1 59.1 %copy-start.62 = (f32[5]{0:T(128)S(1)}, f32[5]{0:T(128)}, u32[]{:S(2)}) copy-start(f32[5]{0:T(128)} %copy-done.61) | copy-start | bytes 64 | tf_op jit(solution)/shard_map/cond
  1295.1 59.3 %copy-start.56 = (bf16[18,5]{0,1:T(8,128)(2,1)S(1)}, bf16[18,5]{0,1:T(8,128)(2,1)}, u32[]{:S(2)}) copy-start(bf16[18,5]{0,1:T(8,128)(2,1)} %get-tuple-element.700) | copy-start | bytes 544 | tf_op jit(solution)/shard_map/cond
  1295.1 59.4 %copy-start.31 = (s32[18,128]{1,0:T(8,128)S(1)}, s32[18,128]{1,0:T(8,128)}, u32[]{:S(2)}) copy-start(s32[18,128]{1,0:T(8,128)} %copy-done.30) | copy-start | bytes 27652 | tf_op jit(solution)/shard_map/cond
  1295.2 59.6 %copy-start.67 = (s32[5]{0:T(128)S(1)}, s32[5]{0:T(128)}, u32[]{:S(2)}) copy-start(s32[5]{0:T(128)} %copy-done.66) | copy-start | bytes 64 | tf_op jit(solution)/shard_map/cond
  1295.2 59.6 %copy-start.55 = (bf16[18,5]{0,1:T(8,128)(2,1)S(1)}, bf16[18,5]{0,1:T(8,128)(2,1)}, u32[]{:S(2)}) copy-start(bf16[18,5]{0,1:T(8,128)(2,1)} %get-tuple-element.702) | copy-start | bytes 544 | tf_op jit(solution)/shard_map/cond
  1295.2 59.7 %copy-start.29 = (s32[18,128]{1,0:T(8,128)S(1)}, s32[18,128]{1,0:T(8,128)}, u32[]{:S(2)}) copy-start(s32[18,128]{1,0:T(8,128)} %copy-done.28) | copy-start | bytes 27652 | tf_op jit(solution)/shard_map/cond
  1349.2 10.3 collective-permute-start.15
  1349.9 47.6 %collective-permute-start.8 = (bf16[3,176,4096]{2,1,0:T(8,128)(2,1)}, bf16[3,176,4096]{2,1,0:T(8,128)(2,1)}, u32[]{:S(2)}, u32[]{:S(2)}) collective-permute-start(bf16[3,176,4096]{2,1,0:T(8,128)(2,1)} %bitcast.302), channel_id=1, source_target_pairs={{0,1},{1,0},{2,3},{3,2},{4,5},{5,4},{6,7},{7,6}} | collective-permute-start | bytes 12976136 | tf_op jit(solution)/shard_map/cond/branch_1_fun/ppermute | solution.py:201
  1350.0 47.6 %collective-permute-start.10 = (bf16[3,176,4096]{2,1,0:T(8,128)(2,1)}, bf16[3,176,4096]{2,1,0:T(8,128)(2,1)}, u32[]{:S(2)}, u32[]{:S(2)}) collective-permute-start(bf16[3,176,4096]{2,1,0:T(8,128)(2,1)} %collective-permute-done.5.refs_2_), channel_id=1, source_target_pairs={{0,1},{1,0},{2,3},{3,2},{4,5},{5,4},{6,7},{7,6}} | collective-permute-start | bytes 12976136 | tf_op jit(solution)/shard_map/cond/branch_1_fun/ppermute | solution.py:201
  1350.4 47.1 %collective-permute-start.9 = (bf16[3,176,4096]{2,1,0:T(8,128)(2,1)}, bf16[3,176,4096]{2,1,0:T(8,128)(2,1)}, u32[]{:S(2)}, u32[]{:S(2)}) collective-permute-start(bf16[3,176,4096]{2,1,0:T(8,128)(2,1)} %collective-permute-done.3.refs_1_), channel_id=1, source_target_pairs={{0,1},{1,0},{2,3},{3,2},{4,5},{5,4},{6,7},{7,6}} | collective-permute-start | bytes 12976136 | tf_op jit(solution)/shard_map/cond/branch_1_fun/ppermute | solution.py:201
  1350.5 47.1 %collective-permute-start.11 = (bf16[3,176,4096]{2,1,0:T(8,128)(2,1)}, bf16[3,176,4096]{2,1,0:T(8,128)(2,1)}, u32[]{:S(2)}, u32[]{:S(2)}) collective-permute-start(bf16[3,176,4096]{2,1,0:T(8,128)(2,1)} %collective-permute-done.7.refs_3_), channel_id=1, source_target_pairs={{0,1},{1,0},{2,3},{3,2},{4,5},{5,4},{6,7},{7,6}} | collective-permute-start | bytes 12976136 | tf_op jit(solution)/shard_map/cond/branch_1_fun/ppermute | solution.py:201
  1354.4 43.1 %copy-start.64 = (s32[5]{0:T(128)}, s32[5]{0:T(128)S(1)}, u32[]{:S(2)}) copy-start(s32[5]{0:T(128)S(1)} %select_reduce_fusion.13) | copy-start | bytes 64 | tf_op jit(solution)/shard_map/cond
  1454.2 99.8 %collective-permute-start.16 = (bf16[256,4096]{1,0:T(8,128)(2,1)}, bf16[256,4096]{1,0:T(8,128)(2,1)}, u32[]{:S(2)}, u32[]{:S(2)}) collective-permute-start(bf16[256,4096]{1,0:T(8,128)(2,1)} %fusion.56), channel_id=1, source_target_pairs={{0,4},{1,5},{2,6},{3,7},{4,0},{5,1},{6,2},{7,3}} | collective-permute-start | bytes 6291464 | tf_op jit(solution)/shard_map/cond/branch_1_fun/ppermute | solution.py:201
  1456.7 253.7 %collective-permute-start.17 = (bf16[3,176,4096]{2,1,0:T(8,128)(2,1)}, bf16[3,176,4096]{2,1,0:T(8,128)(2,1)}, u32[]{:S(2)}, u32[]{:S(2)}) collective-permute-start(bf16[3,176,4096]{2,1,0:T(8,128)(2,1)} %bitcast.298), channel_id=1, source_target_pairs={{0,4},{1,5},{2,6},{3,7},{4,0},{5,1},{6,2},{7,3}} | collective-permute-start | bytes 12976136 | tf_op jit(solution)/shard_map/cond/branch_1_fun/ppermute | solution.py:201
  1458.8 432.0 %collective-permute-start.18 = (bf16[3,176,4096]{2,1,0:T(8,128)(2,1)}, bf16[3,176,4096]{2,1,0:T(8,128)(2,1)}, u32[]{:S(2)}, u32[]{:S(2)}) collective-permute-start(bf16[3,176,4096]{2,1,0:T(8,128)(2,1)} %bitcast.295), channel_id=1, source_target_pairs={{0,4},{1,5},{2,6},{3,7},{4,0},{5,1},{6,2},{7,3}} | collective-permute-start | bytes 12976136 | tf_op jit(solution)/shard_map/cond/branch_1_fun/ppermute | solution.py:201
  1458.8 431.9 %collective-permute-start.19 = (bf16[3,176,4096]{2,1,0:T(8,128)(2,1)}, bf16[3,176,4096]{2,1,0:T(8,128)(2,1)}, u32[]{:S(2)}, u32[]{:S(2)}) collective-permute-start(bf16[3,176,4096]{2,1,0:T(8,128)(2,1)} %bitcast.372), channel_id=1, source_target_pairs={{0,2},{1,3},{2,0},{3,1},{4,6},{5,7},{6,4},{7,5}} | collective-permute-start | bytes 12976136 | tf_op jit(solution)/shard_map/cond/branch_1_fun/ppermute | solution.py:201
  1469.3 421.5 %collective-permute-start.20 = (bf16[3,176,4096]{2,1,0:T(8,128)(2,1)}, bf16[3,176,4096]{2,1,0:T(8,128)(2,1)}, u32[]{:S(2)}, u32[]{:S(2)}) collective-permute-start(bf16[3,176,4096]{2,1,0:T(8,128)(2,1)} %bitcast.371), channel_id=1, source_target_pairs={{0,2},{1,3},{2,0},{3,1},{4,6},{5,7},{6,4},{7,5}} | collective-permute-start | bytes 12976136 | tf_op jit(solution)/shard_map/cond/branch_1_fun/ppermute | solution.py:201
  1618.3 296.7 %copy-start.32 = (s32[2304]{0:T(1024)S(1)}, s32[2304]{0:T(1024)}, u32[]{:S(2)}) copy-start(s32[2304]{0:T(1024)} %compare_select_fusion.29) | copy-start | bytes 27652 | tf_op jit(solution)/shard_map/cond
  1618.3 296.7 %copy-start.48 = (s32[1280]{0:T(1024)S(1)}, s32[1280]{0:T(1024)}, u32[]{:S(2)}) copy-start(s32[1280]{0:T(1024)} %select_n.522) | copy-start | bytes 15364 | tf_op jit(solution)/shard_map/cond
  1618.4 302.5 %copy-start.60 = (s32[5,1]{0,1:T(1,128)S(1)}, s32[5,1]{0,1:T(1,128)}, u32[]{:S(2)}) copy-start(s32[5,1]{0,1:T(1,128)} %get-tuple-element.812) | copy-start | bytes 64 | tf_op jit(solution)/shard_map/cond
  1618.4 302.5 %copy-start.65 = (s32[5]{0:T(128)S(1)}, s32[5]{0:T(128)}, u32[]{:S(2)}) copy-start(s32[5]{0:T(128)} %copy-done.64) | copy-start | bytes 64 | tf_op jit(solution)/shard_map/cond
  1618.4 303.4 %copy-start.21 = (s32[1,2048]{1,0:T(1,128)S(1)}, s32[1,2048]{1,0:T(1,128)}, u32[]{:S(2)}) copy-start(s32[1,2048]{1,0:T(1,128)} %copy-done.20) | copy-start | bytes 24580 | tf_op jit(solution)/shard_map/cond
  1618.4 303.3 %copy-start.59 = (s32[256]{0:T(256)S(1)}, s32[256]{0:T(256)}, u32[]{:S(2)}) copy-start(s32[256]{0:T(256)} %get-tuple-element.793) | copy-start | bytes 3076 | tf_op jit(solution)/shard_map/cond
  1902.7 55.4 %collective-permute-start.21 = (bf16[256,4096]{1,0:T(8,128)(2,1)S(1)}, bf16[256,4096]{1,0:T(8,128)(2,1)}, u32[]{:S(2)}, u32[]{:S(2)}) collective-permute-start(bf16[256,4096]{1,0:T(8,128)(2,1)S(1)} %gather_fusion.9), channel_id=1, source_target_pairs={{0,2},{1,3},{2,0},{3,1},{4,6},{5,7},{6,4},{7,5}} | collective-permute-start | bytes 6291464 | tf_op jit(solution)/shard_map/cond/branch_1_fun/ppermute | solution.py:201
  1921.8 316.2 %collective-permute-start.29 = (bf16[3,176,4096]{2,1,0:T(8,128)(2,1)}, bf16[3,176,4096]{2,1,0:T(8,128)(2,1)}, u32[]{:S(2)}, u32[]{:S(2)}) collective-permute-start(bf16[3,176,4096]{2,1,0:T(8,128)(2,1)} %bitcast.299), channel_id=1, source_target_pairs={{0,1},{1,0},{2,3},{3,2},{4,5},{5,4},{6,7},{7,6}} | collective-permute-start | bytes 12976136 | tf_op jit(solution)/shard_map/cond/branch_1_fun/ppermute | solution.py:201
  1921.8 303.3 %collective-permute-start.23 = (bf16[3,176,4096]{2,1,0:T(8,128)(2,1)}, bf16[3,176,4096]{2,1,0:T(8,128)(2,1)}, u32[]{:S(2)}, u32[]{:S(2)}) collective-permute-start(bf16[3,176,4096]{2,1,0:T(8,128)(2,1)} %collective-permute-done.19.refs_2_), channel_id=1, source_target_pairs={{0,4},{1,5},{2,6},{3,7},{4,0},{5,1},{6,2},{7,3}} | collective-permute-start | bytes 12976136 | tf_op jit(solution)/shard_map/cond/branch_1_fun/ppermute | solution.py:201
  1921.8 316.6 %collective-permute-start.31 = (bf16[3,176,4096]{2,1,0:T(8,128)(2,1)}, bf16[3,176,4096]{2,1,0:T(8,128)(2,1)}, u32[]{:S(2)}, u32[]{:S(2)}) collective-permute-start(bf16[3,176,4096]{2,1,0:T(8,128)(2,1)} %collective-permute-done.19.refs_2_), channel_id=1, source_target_pairs={{0,1},{1,0},{2,3},{3,2},{4,5},{5,4},{6,7},{7,6}} | collective-permute-start | bytes 12976136 | tf_op jit(solution)/shard_map/cond/branch_1_fun/ppermute | solution.py:201
  1922.3 302.8 %collective-permute-start.24 = (bf16[3,176,4096]{2,1,0:T(8,128)(2,1)}, bf16[3,176,4096]{2,1,0:T(8,128)(2,1)}, u32[]{:S(2)}, u32[]{:S(2)}) collective-permute-start(bf16[3,176,4096]{2,1,0:T(8,128)(2,1)} %collective-permute-done.20.refs_2_), channel_id=1, source_target_pairs={{0,4},{1,5},{2,6},{3,7},{4,0},{5,1},{6,2},{7,3}} | collective-permute-start | bytes 12976136 | tf_op jit(solution)/shard_map/cond/branch_1_fun/ppermute | solution.py:201
  1958.1 280.3 %collective-permute-start.30 = (bf16[3,176,4096]{2,1,0:T(8,128)(2,1)}, bf16[3,176,4096]{2,1,0:T(8,128)(2,1)}, u32[]{:S(2)}, u32[]{:S(2)}) collective-permute-start(bf16[3,176,4096]{2,1,0:T(8,128)(2,1)} %collective-permute-done.17.refs_1_), channel_id=1, source_target_pairs={{0,1},{1,0},{2,3},{3,2},{4,5},{5,4},{6,7},{7,6}} | collective-permute-start | bytes 12976136 | tf_op jit(solution)/shard_map/cond/branch_1_fun/ppermute | solution.py:201
  2174.9 64.0 %copy-start.58 = (s32[256,1]{0,1:T(1,128)S(1)}, s32[256,1]{0,1:T(1,128)}, u32[]{:S(2)}) copy-start(s32[256,1]{0,1:T(1,128)} %get-tuple-element.808) | copy-start | bytes 3076 | tf_op jit(solution)/shard_map/cond
  2225.1 20.2 collective-permute-start.32
  2237.9 45.1 %collective-permute-start.25 = (bf16[3,176,4096]{2,1,0:T(8,128)(2,1)}, bf16[3,176,4096]{2,1,0:T(8,128)(2,1)}, u32[]{:S(2)}, u32[]{:S(2)}) collective-permute-start(bf16[3,176,4096]{2,1,0:T(8,128)(2,1)} %bitcast.296), channel_id=1, source_target_pairs={{0,1},{1,0},{2,3},{3,2},{4,5},{5,4},{6,7},{7,6}} | collective-permute-start | bytes 12976136 | tf_op jit(solution)/shard_map/cond/branch_1_fun/ppermute | solution.py:201
  2238.0 45.1 %collective-permute-start.27 = (bf16[3,176,4096]{2,1,0:T(8,128)(2,1)}, bf16[3,176,4096]{2,1,0:T(8,128)(2,1)}, u32[]{:S(2)}, u32[]{:S(2)}) collective-permute-start(bf16[3,176,4096]{2,1,0:T(8,128)(2,1)} %collective-permute-done.20.refs_2_), channel_id=1, source_target_pairs={{0,1},{1,0},{2,3},{3,2},{4,5},{5,4},{6,7},{7,6}} | collective-permute-start | bytes 12976136 | tf_op jit(solution)/shard_map/cond/branch_1_fun/ppermute | solution.py:201
  2238.4 44.6 %collective-permute-start.26 = (bf16[3,176,4096]{2,1,0:T(8,128)(2,1)}, bf16[3,176,4096]{2,1,0:T(8,128)(2,1)}, u32[]{:S(2)}, u32[]{:S(2)}) collective-permute-start(bf16[3,176,4096]{2,1,0:T(8,128)(2,1)} %collective-permute-done.18.refs_1_), channel_id=1, source_target_pairs={{0,1},{1,0},{2,3},{3,2},{4,5},{5,4},{6,7},{7,6}} | collective-permute-start | bytes 12976136 | tf_op jit(solution)/shard_map/cond/branch_1_fun/ppermute | solution.py:201
  2238.5 44.5 %collective-permute-start.28 = (bf16[3,176,4096]{2,1,0:T(8,128)(2,1)}, bf16[3,176,4096]{2,1,0:T(8,128)(2,1)}, u32[]{:S(2)}, u32[]{:S(2)}) collective-permute-start(bf16[3,176,4096]{2,1,0:T(8,128)(2,1)} %collective-permute-done.24.refs_3_), channel_id=1, source_target_pairs={{0,1},{1,0},{2,3},{3,2},{4,5},{5,4},{6,7},{7,6}} | collective-permute-start | bytes 12976136 | tf_op jit(solution)/shard_map/cond/branch_1_fun/ppermute | solution.py:201
  2337.7 51.7 %collective-permute-start.33 = (bf16[256,4096]{1,0:T(8,128)(2,1)}, bf16[256,4096]{1,0:T(8,128)(2,1)}, u32[]{:S(2)}, u32[]{:S(2)}) collective-permute-start(bf16[256,4096]{1,0:T(8,128)(2,1)} %fusion.55), channel_id=1, source_target_pairs={{0,2},{1,3},{2,0},{3,1},{4,6},{5,7},{6,4},{7,5}} | collective-permute-start | bytes 6291464 | tf_op jit(solution)/shard_map/cond/branch_1_fun/ppermute | solution.py:201
  2457.8 45.4 %copy-start.34 = (f32[2048]{0:T(1024)S(1)}, f32[2048]{0:T(1024)}, u32[]{:S(2)}) copy-start(f32[2048]{0:T(1024)} %slice_reduce_fusion) | copy-start | bytes 24580 | tf_op jit(solution)/shard_map/cond
  2457.8 45.4 %copy-start.40 = (pred[2048]{0:T(1024)(128)(4,1)S(1)}, pred[2048]{0:T(1024)(128)(4,1)}, u32[]{:S(2)}) copy-start(pred[2048]{0:T(1024)(128)(4,1)} %copy-done.37) | copy-start | bytes 6148 | tf_op jit(solution)/shard_map/cond
  (27 other events, 450.6 us)
Sparse Core Ops, SparseCore 0:
  63.4 206.0 all-gather.11
  271.4 160.8 all-gather.15
  434.1 269.9 all-gather.13
  705.7 295.2 all-gather.17
  1002.7 234.4 all-gather.19
  1238.9 160.7 all-gather.21
  1401.6 256.4 all-gather.25
  1659.9 269.3 all-gather.23

commit v4 on v3

--- a/solution.py
+++ b/solution.py
@@ -12,7 +12,7 @@
 TM = 256
 DC = 256
 NG = 4
-CAP = 256
+CAP = 320
 SIDE_RANKS = {4: ((4, 7), (5, 6)), 2: ((2, 5, 7), (3, 4, 6))}
 VMEM = 66 * 1000 * 1000
 
@@ -161,6 +161,7 @@
 
 def row_plan(slots, n_local):
     n = slots.shape[0]
+    slots = jnp.concatenate([slots, jnp.full(-n % 128, n_local, slots.dtype)])
     onehot = slots[:, None] == jnp.arange(n_local)[None, :]
     within, counts = prefix(onehot)
     tiles = jnp.maximum((counts + TM - 1) // TM, 1)
@@ -171,7 +172,7 @@
     keys = jnp.concatenate([slots, spare.reshape(-1)])
     order = lax.sort(keys * 8192 + jnp.arange(keys.shape[0], dtype=jnp.int32)) & 8191
     scalars = jnp.stack([first, tiles], axis=1).astype(jnp.int32)
-    return jnp.where(order < n, order, 0), pos, scalars
+    return jnp.where(order < n, order, 0), pos[:n], scalars
 
 
 def pick(table, index, size):
@@ -296,7 +297,7 @@
                 token, pos, scalars = row_plan(slots, n_local - 1)
                 h, g0, g1 = norm_gates(both, norm_w[l], router_w[l], jnp.broadcast_to(my_top[l], ids1.shape), ids1)
                 rows = take(h, token)
-                max_tiles = (n_tok + CAP) // TM
+                max_tiles = pl.cdiv(n_tok + CAP, TM)
                 whole = [(0, p) for p in range(n_dev)]
                 gathered = lambda k, out, w: expert(scalars[k - 1], rows, [w], whole, out, max_tiles)
                 if l:

time: 2550 us -> 2680 us (1.051)
  local copies, waits for them, and re-layouts: 401 us -> 462 us
  waiting for transfers between devices: 1070 us -> 1130 us
    ppermute x34, waiting for transfers between devices: 1070 us -> 1130 us  [hop(): return lax.ppermute(a, 'fsdp', [(i, i ^ bit) for i in range(n_dev)])]
    gather x10, local copies, waits for them, and re-layouts: 344 us -> 401 us  [take(): return table.at[index].get(mode='promise_in_bounds')]
  transfers between devices with their start and end apart: 42 -> 42, of which waited for: 11 -> 11; matrix products, arithmetic and copies ran while one was open for 18% -> 18% of each run, Pallas kernels for 30% -> 29%
where the time goes in v4:
time: 2680 us; the launch traced here: 2660 us
  waiting for transfers between devices  1130 us (42%)
  Pallas kernels  832 us (31%)
  local copies, waits for them, and re-layouts  462 us (17%)
  other arithmetic  153 us (6%)
  starting transfers between devices  41.3 us (2%)
    ppermute x34, waiting for transfers between devices, hop(): return lax.ppermute(a, 'fsdp', [(i, i ^ bit) for i in range(n_dev)])  1130 us
    pallas_call x12, Pallas kernels, expert(): pl.pallas_call(functools.partial(expert_body, pieces, len(weights), alias...  679 us
    gather x10, local copies, waits for them, and re-layouts, take(): return table.at[index].get(mode='promise_in_bounds')  401 us
    pallas_call x4, Pallas kernels, prep(): pl.pallas_call(functools.partial(prep_body, groups, n_exp), out_shape=[ja...  153 us
    select_n x2, other arithmetic, adaptive(): x = jnp.where(my_lent[l][:, None], home_again(), mixed)  64 us
  transfers between devices with their start and end apart: 42, of which 11 were waited for; matrix products, arithmetic and copies ran while one was open for 18% of the time, Pallas kernels for 29%

profile of v4, /device:TPU:0, one launch (start us, length us, event | category | flops | bytes accessed | tf_op | source)
XLA Modules:
  0.0 2664.9 jit_solution(3149749691993571984)
XLA Ops:
  6.5 14.4 all-gather
  27.2 2624.4 %conditional.1 = (bf16[2048,4096]{1,0:T(8,128)(2,1)S(1)}) conditional(s32[]{:T(128)} %convert_element_type.241, (bf16[2048,4096]{1,0:T(8,128)(2,1)}, s32[2,2,2048]{2,1,0:T(2,128)}, f32[2,4096]{1,0:T(2,128)}, bf16[2,4096,8]{1,2,0:T(8,128)(2,1)}, bf16[2,8,4096,172]{2,1,3,0:T(8,128)(2,1)}, /*index=5*/bf16[2,8,4096,172]{2,1,3,0:T(8,128)(2,1)}, ...), branch_computations={%region_11.34_spmd, %region_34.61_spmd} | conditional | flops 46129414144 | bytes 3659796224 | solution.py:344
  40.6 21.2 prep.14
  61.8 54.2 %prep.15 = (bf16[1,3,176,4096]{3,2,1,0:T(8,128)(2,1)}, bf16[1,3,176,4096]{3,2,1,0:T(8,128)(2,1)}, bf16[1,3,176,4096]{3,2,1,0:T(8,128)(2,1)}, bf16[1,3,176,4096]{...) custom-call(s32[7]{0:T(128)} %get-tuple-element.402.s_ref, ...), custom_call_target="tpu_custom_call" | custom-call | flops 4200000000 | bytes 100100000 | tf_op jit(solution)/shard_map/cond/branch_1_fun/prep/pallas_call | solution.py:49
  119.3 5.1 sort.100
  124.5 5.1 sort.98
  130.2 15.6 gather_fusion
  149.7 8.9 constant_dynamic-update-slice_fusion.1
  159.3 102.3 %collective-permute-done.1 = s32[320]{0:T(512)S(1)} collective-permute-done((s32[320]{0:T(512)S(1)}, s32[320]{0:T(512)S(1)}, u32[]{:S(2)}, u32[]{:S(2)}) %collective-permute-start.1) | collective-permute-done | bytes 1312 | tf_op jit(solution)/shard_map/cond/branch_1_fun/ppermute | solution.py:202
  261.9 4.6 fusion.45
  266.5 2.0 copy-done.5
  268.5 11.7 fusion.47.h_ref
  280.2 8.6 copy-done.2
  288.9 5.1 select_reduce_fusion.10
  295.9 137.4 %expert.22 = f32[2368,4096]{1,0:T(8,128)} custom-call(s32[2]{0:T(128)} %broadcast_multiply_fusion.2.s_ref, bf16[2368,4096]{1,0:T(8,128)(2,1)} %copy-done.2, bf16[8,3,176,4096]{3,2,1,0:T(8,128)(2,1)} %all-gather.12.cloned.1.call-done.refs_0_, bf16[2368,4096]{1,0:T(8,128)(2,1)} %copy-done.5, f32[2368,1]{1,0:T(8,128)} %bitcast.277), custom_call_target="tpu_custom_call" | custom-call | flops 3000000000 | bytes 60000000 | tf_op jit(solution)/shard_map/cond/branch_1_fun/expert/pallas_call | solution.py:132
  433.3 23.0 prep.17
  456.4 54.5 %prep.16 = (bf16[1,3,176,4096]{3,2,1,0:T(8,128)(2,1)}, bf16[1,3,176,4096]{3,2,1,0:T(8,128)(2,1)}, bf16[1,3,176,4096]{3,2,1,0:T(8,128)(2,1)}, bf16[1,3,176,4096]{...) custom-call(s32[7]{0:T(128)} %get-tuple-element.419.s_ref, ...), custom_call_target="tpu_custom_call" | custom-call | flops 4200000000 | bytes 100100000 | tf_op jit(solution)/shard_map/cond/branch_1_fun/prep/pallas_call | solution.py:49
  516.5 178.0 %collective-permute-done.2.refs_1_ = bf16[3,176,4096]{2,1,0:T(8,128)(2,1)} collective-permute-done((bf16[3,176,4096]{2,1,0:T(8,128)(2,1)}, bf16[3,176,4096]{2,1,0:T(8,128)(2,1)}, u32[]{:S(2)}, u32[]{:S(2)}) %collective-permute-start.2) | collective-permute-done | bytes 4325408 | tf_op jit(solution)/shard_map/cond/branch_1_fun/ppermute | solution.py:202
  694.5 169.5 %collective-permute-done.3.refs_1_ = bf16[3,176,4096]{2,1,0:T(8,128)(2,1)} collective-permute-done((bf16[3,176,4096]{2,1,0:T(8,128)(2,1)}, bf16[3,176,4096]{2,1,0:T(8,128)(2,1)}, u32[]{:S(2)}, u32[]{:S(2)}) %collective-permute-start.3) | collective-permute-done | bytes 4325408 | tf_op jit(solution)/shard_map/cond/branch_1_fun/ppermute | solution.py:202
  868.0 348.0 %collective-permute-done.22 = s32[320]{0:T(512)S(1)} collective-permute-done((s32[320]{0:T(512)S(1)}, s32[320]{0:T(512)S(1)}, u32[]{:S(2)}, u32[]{:S(2)}) %collective-permute-start.22) | collective-permute-done | bytes 1312 | tf_op jit(solution)/shard_map/cond/branch_1_fun/ppermute | solution.py:202
  1220.4 5.8 sort.99
  1227.6 61.8 %gather_fusion.5 = bf16[3712,4096]{1,0:T(8,128)(2,1)} fusion(bf16[2368,4096]{1,0:T(8,128)(2,1)} %copy-done.2, s32[4096]{0:T(1024)S(1)} %pad_clamp_fusion.1), kind=kCustom, calls=%fused_computation.11 | custom fusion | bytes 60832256 | tf_op jit(solution)/shard_map/cond/branch_1_fun/gather | solution.py:195
  1289.4 50.2 %expert.23.refs_1_ = f32[3712,4096]{1,0:T(8,128)} custom-call(s32[2]{0:T(128)} %get-tuple-element.713.s_ref, bf16[3712,4096]{1,0:T(8,128)(2,1)} %gather_fusion.5, bf16[8,3,176,4096]{3,2,1,0:T(8,128)(2,1)} %all-gather.16.cloned.1.call-done.refs_0_), custom_call_target="tpu_custom_call" | custom-call | flops 3000000000 | bytes 60000000 | tf_op jit(solution)/shard_map/cond/branch_1_fun/expert/pallas_call | solution.py:132
  1339.7 50.9 %expert.24.refs_8_ = f32[3712,4096]{1,0:T(8,128)} custom-call(s32[2]{0:T(128)} %get-tuple-element.714.s_ref, bf16[3712,4096]{1,0:T(8,128)(2,1)} %gather_fusion.5, bf16[8,3,176,4096]{3,2,1,0:T(8,128)(2,1)} %all-gather.14.cloned.1.call-done.refs_0_, f32[3712,4096]{1,0:T(8,128)} %expert.23.refs_1_), custom_call_target="tpu_custom_call", output_to_operand_aliasing={{}: (3, {})} | custom-call | flops 3000000000 | bytes 60000000 | tf_op jit(solution)/shard_map/cond/branch_1_fun/expert/pallas_call | solution.py:132
  1393.1 5.1 collective-permute-done.15.refs_7_
  1398.3 37.9 %expert.25.refs_8_ = f32[3712,4096]{1,0:T(8,128)} custom-call(s32[2]{0:T(128)} %get-tuple-element.712.s_ref, bf16[3712,4096]{1,0:T(8,128)(2,1)} %gather_fusion.5, bf16[3,176,4096]{2,1,0:T(8,128)(2,1)} %bitcast.294, bf16[3,176,4096]{2,1,0:T(8,128)(2,1)} %collective-permute-done.2.refs_1_, ...), custom_call_target="tpu_custom_call", output_to_operand_aliasing={{}: (10, {})} | custom-call | flops 3000000000 | bytes 60000000 | tf_op jit(solution)/shard_map/cond/branch_1_fun/expert/pallas_call | solution.py:132
  1436.2 25.4 expert.26.refs_1_
  1461.6 20.3 gather_fusion.6
  1481.9 9.8 fusion.56
  1494.1 2.0 collective-permute-start.17
  1496.1 10.1 collective-permute-start.19
  1506.2 37.8 %expert.27 = f32[3712,4096]{1,0:T(8,128)} custom-call(s32[2]{0:T(128)} %get-tuple-element.711.s_ref, bf16[3712,4096]{1,0:T(8,128)(2,1)} %gather_fusion.5, bf16[8,3,176,4096]{3,2,1,0:T(8,128)(2,1)} %all-gather.18.cloned.1.call-done.refs_0_, f32[3712,4096]{1,0:T(8,128)} %expert.26.refs_1_), custom_call_target="tpu_custom_call", output_to_operand_aliasing={{}: (3, {})} | custom-call | flops 3000000000 | bytes 60000000 | tf_op jit(solution)/shard_map/cond/branch_1_fun/expert/pallas_call | solution.py:132
  1544.0 72.4 %gather_fusion.8 = f32[2048,4096]{1,0:T(8,128)} fusion(f32[3712,4096]{1,0:T(8,128)} %expert.27, s32[2048]{0:T(1024)S(1)} %broadcast_clamp_fusion.5), kind=kCustom, calls=%fused_computation.14 | custom fusion | bytes 67117056 | tf_op jit(solution)/shard_map/cond/branch_1_fun/gather | solution.py:195
  1616.4 30.7 %gather_fusion.7 = bf16[2048,4096]{1,0:T(8,128)(2,1)} fusion(bf16[320,4096]{1,0:T(8,128)(2,1)} %collective-permute-done.16, s32[2048]{0:T(1024)S(1)} %broadcast_clamp_fusion.7), kind=kCustom, calls=%fused_computation.13 | custom fusion | bytes 33562624 | tf_op jit(solution)/shard_map/cond/branch_1_fun/gather | solution.py:195
  1647.1 37.3 %fusion.53 = bf16[2048,4096]{1,0:T(8,128)(2,1)} fusion(bf16[2048,4096]{1,0:T(8,128)(2,1)} %gather_fusion.7, f32[2048,4096]{1,0:T(8,128)} %gather_fusion.8, f32[2368,4096]{1,0:T(8,128)} %expert.22, f32[2048]{0:T(1024)S(1)} %copy-done.34, pred[2048]{0:T(1024)(128)(4,1)S(1)} %copy-done.44), kind=kLoop, calls=%fused_computation.164 | loop fusion | flops 33554432 | bytes 100673536 | tf_op jit(solution)/shard_map/cond/branch_1_fun/jit(_where)/select_n | solution.py:338
  1684.5 87.0 %collective-permute-done.17.refs_1_ = bf16[3,176,4096]{2,1,0:T(8,128)(2,1)} collective-permute-done((bf16[3,176,4096]{2,1,0:T(8,128)(2,1)}, bf16[3,176,4096]{2,1,0:T(8,128)(2,1)}, u32[]{:S(2)}, u32[]{:S(2)}) %collective-permute-start.17) | collective-permute-done | bytes 4325408 | tf_op jit(solution)/shard_map/cond/branch_1_fun/ppermute | solution.py:202
  1771.4 184.3 %collective-permute-done.18.refs_1_ = bf16[3,176,4096]{2,1,0:T(8,128)(2,1)} collective-permute-done((bf16[3,176,4096]{2,1,0:T(8,128)(2,1)}, bf16[3,176,4096]{2,1,0:T(8,128)(2,1)}, u32[]{:S(2)}, u32[]{:S(2)}) %collective-permute-start.18) | collective-permute-done | bytes 4325408 | tf_op jit(solution)/shard_map/cond/branch_1_fun/ppermute | solution.py:202
  1955.7 15.9 gather_fusion.9
  1971.7 1.6 collective-permute-start.21
  1974.1 5.8 sort.101
  1983.2 8.4 constant_dynamic-update-slice_fusion.3
  1991.7 38.4 %collective-permute-done.21 = bf16[320,4096]{1,0:T(8,128)(2,1)} collective-permute-done((bf16[320,4096]{1,0:T(8,128)(2,1)S(1)}, bf16[320,4096]{1,0:T(8,128)(2,1)}, u32[]{:S(2)}, u32[]{:S(2)}) %collective-permute-start.21) | collective-permute-done | bytes 2621472 | tf_op jit(solution)/shard_map/cond/branch_1_fun/ppermute | solution.py:202
  2030.0 2.0 constant_dynamic-update-slice_fusion.2.refs_1_
  2032.1 4.6 fusion.48
  2036.7 2.0 copy-done.6
  2038.7 12.0 fusion.50.h_ref
  2050.7 6.6 copy-done.3
  2057.4 5.1 select_reduce_fusion.8
  2063.0 61.1 %gather_fusion.10 = bf16[3712,4096]{1,0:T(8,128)(2,1)} fusion(bf16[2368,4096]{1,0:T(8,128)(2,1)} %copy-done.3, s32[4096]{0:T(1024)S(1)} %pad_clamp_fusion), kind=kCustom, calls=%fused_computation.16 | custom fusion | bytes 60832256 | tf_op jit(solution)/shard_map/cond/branch_1_fun/gather | solution.py:195
  2125.5 137.6 %expert.28 = f32[2368,4096]{1,0:T(8,128)} custom-call(s32[2]{0:T(128)} %broadcast_multiply_fusion.2.s_ref, bf16[2368,4096]{1,0:T(8,128)(2,1)} %copy-done.3, bf16[8,3,176,4096]{3,2,1,0:T(8,128)(2,1)} %all-gather.20.cloned.1.call-done.refs_0_, bf16[2368,4096]{1,0:T(8,128)(2,1)} %copy-done.6, f32[2368,1]{1,0:T(8,128)} %bitcast.278), custom_call_target="tpu_custom_call" | custom-call | flops 3000000000 | bytes 60000000 | tf_op jit(solution)/shard_map/cond/branch_1_fun/expert/pallas_call | solution.py:132
  2263.1 50.3 %expert.29.refs_8_ = f32[3712,4096]{1,0:T(8,128)} custom-call(s32[2]{0:T(128)} %get-tuple-element.709.s_ref, bf16[3712,4096]{1,0:T(8,128)(2,1)} %gather_fusion.10, bf16[8,3,176,4096]{3,2,1,0:T(8,128)(2,1)} %all-gather.22.cloned.1.call-done.refs_0_), custom_call_target="tpu_custom_call" | custom-call | flops 3000000000 | bytes 60000000 | tf_op jit(solution)/shard_map/cond/branch_1_fun/expert/pallas_call | solution.py:132
  2313.5 12.9 collective-permute-start.32
  2328.9 4.8 collective-permute-done.32.refs_7_
  2333.7 37.9 %expert.30.refs_8_ = f32[3712,4096]{1,0:T(8,128)} custom-call(s32[2]{0:T(128)} %get-tuple-element.708.s_ref, bf16[3712,4096]{1,0:T(8,128)(2,1)} %gather_fusion.10, bf16[3,176,4096]{2,1,0:T(8,128)(2,1)} %bitcast.288, bf16[3,176,4096]{2,1,0:T(8,128)(2,1)} %collective-permute-done.17.refs_1_, ...), custom_call_target="tpu_custom_call", output_to_operand_aliasing={{}: (10, {})} | custom-call | flops 3000000000 | bytes 60000000 | tf_op jit(solution)/shard_map/cond/branch_1_fun/expert/pallas_call | solution.py:132
  2371.6 25.4 expert.31.refs_1_
  2397.0 20.3 gather_fusion.11
  2417.3 6.8 fusion.55
  2425.7 50.2 %expert.32.refs_1_ = f32[3712,4096]{1,0:T(8,128)} custom-call(s32[2]{0:T(128)} %get-tuple-element.706.s_ref, bf16[3712,4096]{1,0:T(8,128)(2,1)} %gather_fusion.10, bf16[8,3,176,4096]{3,2,1,0:T(8,128)(2,1)} %all-gather.26.cloned.1.call-done.refs_0_, f32[3712,4096]{1,0:T(8,128)} %expert.31.refs_1_), custom_call_target="tpu_custom_call", output_to_operand_aliasing={{}: (3, {})} | custom-call | flops 3000000000 | bytes 60000000 | tf_op jit(solution)/shard_map/cond/branch_1_fun/expert/pallas_call | solution.py:132
  2475.9 7.7 collective-permute-done.33
  2483.6 30.7 %gather_fusion.12 = bf16[2048,4096]{1,0:T(8,128)(2,1)} fusion(bf16[320,4096]{1,0:T(8,128)(2,1)} %collective-permute-done.33, s32[2048]{0:T(1024)S(1)} %broadcast_clamp_fusion.6), kind=kCustom, calls=%fused_computation.18 | custom fusion | bytes 33562624 | tf_op jit(solution)/shard_map/cond/branch_1_fun/gather | solution.py:195
  2514.3 37.8 %expert.33 = f32[3712,4096]{1,0:T(8,128)} custom-call(s32[2]{0:T(128)} %get-tuple-element.707.s_ref, bf16[3712,4096]{1,0:T(8,128)(2,1)} %gather_fusion.10, bf16[8,3,176,4096]{3,2,1,0:T(8,128)(2,1)} %all-gather.24.cloned.1.call-done.refs_0_, f32[3712,4096]{1,0:T(8,128)} %expert.32.refs_1_), custom_call_target="tpu_custom_call", output_to_operand_aliasing={{}: (3, {})} | custom-call | flops 3000000000 | bytes 60000000 | tf_op jit(solution)/shard_map/cond/branch_1_fun/expert/pallas_call | solution.py:132
  2552.2 72.5 %gather_fusion.13 = f32[2048,4096]{1,0:T(8,128)} fusion(f32[3712,4096]{1,0:T(8,128)} %expert.33, s32[2048]{0:T(1024)S(1)} %broadcast_clamp_fusion.4), kind=kCustom, calls=%fused_computation.19 | custom fusion | bytes 67117056 | tf_op jit(solution)/shard_map/cond/branch_1_fun/gather | solution.py:195
  2624.7 26.7 %fusion.54 = bf16[2048,4096]{1,0:T(8,128)(2,1)S(1)} fusion(bf16[2048,4096]{1,0:T(8,128)(2,1)} %gather_fusion.12, f32[2048,4096]{1,0:T(8,128)} %gather_fusion.13, f32[2368,4096]{1,0:T(8,128)} %expert.28, f32[2048]{0:T(1024)S(1)} %copy-done.35, pred[2048]{0:T(1024)(128)(4,1)S(1)} %copy-done.41), kind=kLoop, calls=%fused_computation.165 | loop fusion | flops 33554432 | bytes 100673536 | tf_op jit(solution)/shard_map/cond/branch_1_fun/jit(_where)/select_n | solution.py:338
  2651.6 6.2 copy-done.8
  (294 shorter events, 52.2 us)
Async XLA Ops:
  34.4 261.5 %all-gather.12.cloned.1.call-start = ((), (), s32[]{:S(2)}) async-start(), calls=%async_computation | async-start | bytes 38928384 | tf_op jit(solution)/shard_map/cond/branch_1_fun/all_gather | solution.py:274
  61.8 55.8 %copy-start.50 = (s32[2,8]{1,0:T(2,128)S(1)}, s32[2,8]{1,0:T(2,128)}, u32[]{:S(2)}) copy-start(s32[2,8]{1,0:T(2,128)} %copy-done.49) | copy-start | bytes 196 | tf_op jit(solution)/shard_map/cond
  61.8 1227.6 %all-gather.16.cloned.1.call-start = ((), (), s32[]{:S(2)}) async-start(), calls=%async_computation.2 | async-start | bytes 38928384 | tf_op jit(solution)/shard_map/cond/branch_1_fun/all_gather | solution.py:274
  116.0 33.0 %copy-start.19 = (f32[2,4096]{1,0:T(2,128)S(1)}, f32[2,4096]{1,0:T(2,128)}, u32[]{:S(2)}) copy-start(f32[2,4096]{1,0:T(2,128)} %get-tuple-element.387) | copy-start | bytes 98308 | tf_op jit(solution)/shard_map/cond
  116.1 1223.6 %all-gather.14.cloned.1.call-start = ((), (), s32[]{:S(2)}) async-start(), calls=%async_computation.1 | async-start | bytes 38928384 | tf_op jit(solution)/shard_map/cond/branch_1_fun/all_gather | solution.py:274
  116.8 1389.4 %all-gather.18.cloned.1.call-start = ((), (), s32[]{:S(2)}) async-start(), calls=%async_computation.3 | async-start | bytes 38928384 | tf_op jit(solution)/shard_map/cond/branch_1_fun/all_gather | solution.py:274
  117.4 2008.1 %all-gather.20.cloned.1.call-start = ((), (), s32[]{:S(2)}) async-start(), calls=%async_computation.4 | async-start | bytes 38928384 | tf_op jit(solution)/shard_map/cond/branch_1_fun/all_gather | solution.py:274
  145.8 115.8 %collective-permute-start = (bf16[320,4096]{1,0:T(8,128)(2,1)S(1)}, bf16[320,4096]{1,0:T(8,128)(2,1)S(1)}, u32[]{:S(2)}, u32[]{:S(2)}) collective-permute-start(bf16[320,4096]{1,0:T(8,128)(2,1)S(1)} %gather_fusion), channel_id=1, source_target_pairs={{0,4},{1,5},{2,6},{3,7},{4,0},{5,1},{6,2},{7,3}} | collective-permute-start | bytes 7864328 | tf_op jit(solution)/shard_map/cond/branch_1_fun/ppermute | solution.py:202
  147.1 114.6 %collective-permute-start.1 = (s32[320]{0:T(512)S(1)}, s32[320]{0:T(512)S(1)}, u32[]{:S(2)}, u32[]{:S(2)}) collective-permute-start(s32[320]{0:T(512)S(1)} %slice.213), channel_id=1, source_target_pairs={{0,4},{1,5},{2,6},{3,7},{4,0},{5,1},{6,2},{7,3}} | collective-permute-start | bytes 3848 | tf_op jit(solution)/shard_map/cond/branch_1_fun/ppermute | solution.py:202
  456.3 1806.8 %all-gather.22.cloned.1.call-start = ((), (), s32[]{:S(2)}) async-start(), calls=%async_computation.5 | async-start | bytes 38928384 | tf_op jit(solution)/shard_map/cond/branch_1_fun/all_gather | solution.py:274
  510.9 1914.8 %all-gather.26.cloned.1.call-start = ((), (), s32[]{:S(2)}) async-start(), calls=%async_computation.7 | async-start | bytes 38928384 | tf_op jit(solution)/shard_map/cond/branch_1_fun/all_gather | solution.py:274
  511.7 2002.7 %all-gather.24.cloned.1.call-start = ((), (), s32[]{:S(2)}) async-start(), calls=%async_computation.6 | async-start | bytes 38928384 | tf_op jit(solution)/shard_map/cond/branch_1_fun/all_gather | solution.py:274
  512.4 182.0 %collective-permute-start.2 = (bf16[3,176,4096]{2,1,0:T(8,128)(2,1)}, bf16[3,176,4096]{2,1,0:T(8,128)(2,1)}, u32[]{:S(2)}, u32[]{:S(2)}) collective-permute-start(bf16[3,176,4096]{2,1,0:T(8,128)(2,1)} %bitcast.292), channel_id=1, source_target_pairs={{0,2},{1,3},{2,0},{3,1},{4,6},{5,7},{6,4},{7,5}} | collective-permute-start | bytes 12976136 | tf_op jit(solution)/shard_map/cond/branch_1_fun/ppermute | solution.py:202
  513.3 350.6 %collective-permute-start.3 = (bf16[3,176,4096]{2,1,0:T(8,128)(2,1)}, bf16[3,176,4096]{2,1,0:T(8,128)(2,1)}, u32[]{:S(2)}, u32[]{:S(2)}) collective-permute-start(bf16[3,176,4096]{2,1,0:T(8,128)(2,1)} %bitcast.289), channel_id=1, source_target_pairs={{0,2},{1,3},{2,0},{3,1},{4,6},{5,7},{6,4},{7,5}} | collective-permute-start | bytes 12976136 | tf_op jit(solution)/shard_map/cond/branch_1_fun/ppermute | solution.py:202
  514.5 349.5 %collective-permute-start.4 = (bf16[3,176,4096]{2,1,0:T(8,128)(2,1)}, bf16[3,176,4096]{2,1,0:T(8,128)(2,1)}, u32[]{:S(2)}, u32[]{:S(2)}) collective-permute-start(bf16[3,176,4096]{2,1,0:T(8,128)(2,1)} %bitcast.358), channel_id=1, source_target_pairs={{0,4},{1,5},{2,6},{3,7},{4,0},{5,1},{6,2},{7,3}} | collective-permute-start | bytes 12976136 | tf_op jit(solution)/shard_map/cond/branch_1_fun/ppermute | solution.py:202
  515.5 348.6 %collective-permute-start.5 = (bf16[3,176,4096]{2,1,0:T(8,128)(2,1)}, bf16[3,176,4096]{2,1,0:T(8,128)(2,1)}, u32[]{:S(2)}, u32[]{:S(2)}) collective-permute-start(bf16[3,176,4096]{2,1,0:T(8,128)(2,1)} %bitcast.357), channel_id=1, source_target_pairs={{0,4},{1,5},{2,6},{3,7},{4,0},{5,1},{6,2},{7,3}} | collective-permute-start | bytes 12976136 | tf_op jit(solution)/shard_map/cond/branch_1_fun/ppermute | solution.py:202
  864.1 526.5 %collective-permute-start.6 = (bf16[3,176,4096]{2,1,0:T(8,128)(2,1)}, bf16[3,176,4096]{2,1,0:T(8,128)(2,1)}, u32[]{:S(2)}, u32[]{:S(2)}) collective-permute-start(bf16[3,176,4096]{2,1,0:T(8,128)(2,1)} %collective-permute-done.4.refs_2_), channel_id=1, source_target_pairs={{0,2},{1,3},{2,0},{3,1},{4,6},{5,7},{6,4},{7,5}} | collective-permute-start | bytes 12976136 | tf_op jit(solution)/shard_map/cond/branch_1_fun/ppermute | solution.py:202
  865.4 525.1 %collective-permute-start.7 = (bf16[3,176,4096]{2,1,0:T(8,128)(2,1)}, bf16[3,176,4096]{2,1,0:T(8,128)(2,1)}, u32[]{:S(2)}, u32[]{:S(2)}) collective-permute-start(bf16[3,176,4096]{2,1,0:T(8,128)(2,1)} %collective-permute-done.5.refs_2_), channel_id=1, source_target_pairs={{0,2},{1,3},{2,0},{3,1},{4,6},{5,7},{6,4},{7,5}} | collective-permute-start | bytes 12976136 | tf_op jit(solution)/shard_map/cond/branch_1_fun/ppermute | solution.py:202
  866.1 349.8 %collective-permute-start.22 = (s32[320]{0:T(512)S(1)}, s32[320]{0:T(512)S(1)}, u32[]{:S(2)}, u32[]{:S(2)}) collective-permute-start(s32[320]{0:T(512)S(1)} %slice.233), channel_id=1, source_target_pairs={{0,2},{1,3},{2,0},{3,1},{4,6},{5,7},{6,4},{7,5}} | collective-permute-start | bytes 3848 | tf_op jit(solution)/shard_map/cond/branch_1_fun/ppermute | solution.py:202
  867.5 523.6 %collective-permute-start.12 = (bf16[3,176,4096]{2,1,0:T(8,128)(2,1)}, bf16[3,176,4096]{2,1,0:T(8,128)(2,1)}, u32[]{:S(2)}, u32[]{:S(2)}) collective-permute-start(bf16[3,176,4096]{2,1,0:T(8,128)(2,1)} %bitcast.293), channel_id=1, source_target_pairs={{0,1},{1,0},{2,3},{3,2},{4,5},{5,4},{6,7},{7,6}} | collective-permute-start | bytes 12976136 | tf_op jit(solution)/shard_map/cond/branch_1_fun/ppermute | solution.py:202
  867.5 523.7 %collective-permute-start.13 = (bf16[3,176,4096]{2,1,0:T(8,128)(2,1)}, bf16[3,176,4096]{2,1,0:T(8,128)(2,1)}, u32[]{:S(2)}, u32[]{:S(2)}) collective-permute-start(bf16[3,176,4096]{2,1,0:T(8,128)(2,1)} %collective-permute-done.2.refs_1_), channel_id=1, source_target_pairs={{0,1},{1,0},{2,3},{3,2},{4,5},{5,4},{6,7},{7,6}} | collective-permute-start | bytes 12976136 | tf_op jit(solution)/shard_map/cond/branch_1_fun/ppermute | solution.py:202
  1215.9 175.7 %collective-permute-start.14 = (bf16[3,176,4096]{2,1,0:T(8,128)(2,1)}, bf16[3,176,4096]{2,1,0:T(8,128)(2,1)}, u32[]{:S(2)}, u32[]{:S(2)}) collective-permute-start(bf16[3,176,4096]{2,1,0:T(8,128)(2,1)} %collective-permute-done.4.refs_2_), channel_id=1, source_target_pairs={{0,1},{1,0},{2,3},{3,2},{4,5},{5,4},{6,7},{7,6}} | collective-permute-start | bytes 12976136 | tf_op jit(solution)/shard_map/cond/branch_1_fun/ppermute | solution.py:202
  1339.6 52.0 %copy-start.64 = (s32[5]{0:T(128)S(1)}, s32[5]{0:T(128)}, u32[]{:S(2)}) copy-start(s32[5]{0:T(128)} %copy-done.63) | copy-start | bytes 64 | tf_op jit(solution)/shard_map/cond
  1339.7 52.0 %copy-start.54 = (bf16[19,5]{0,1:T(8,128)(2,1)S(1)}, bf16[19,5]{0,1:T(8,128)(2,1)}, u32[]{:S(2)}) copy-start(bf16[19,5]{0,1:T(8,128)(2,1)} %get-tuple-element.702) | copy-start | bytes 574 | tf_op jit(solution)/shard_map/cond
  1339.7 52.1 %copy-start.33 = (s32[19,128]{1,0:T(8,128)S(1)}, s32[19,128]{1,0:T(8,128)}, u32[]{:S(2)}) copy-start(s32[19,128]{1,0:T(8,128)} %copy-done.32) | copy-start | bytes 29188 | tf_op jit(solution)/shard_map/cond
  1390.6 7.7 collective-permute-start.15
  1390.6 45.6 %collective-permute-start.8 = (bf16[3,176,4096]{2,1,0:T(8,128)(2,1)}, bf16[3,176,4096]{2,1,0:T(8,128)(2,1)}, u32[]{:S(2)}, u32[]{:S(2)}) collective-permute-start(bf16[3,176,4096]{2,1,0:T(8,128)(2,1)} %bitcast.290), channel_id=1, source_target_pairs={{0,1},{1,0},{2,3},{3,2},{4,5},{5,4},{6,7},{7,6}} | collective-permute-start | bytes 12976136 | tf_op jit(solution)/shard_map/cond/branch_1_fun/ppermute | solution.py:202
  1391.1 45.1 %collective-permute-start.10 = (bf16[3,176,4096]{2,1,0:T(8,128)(2,1)}, bf16[3,176,4096]{2,1,0:T(8,128)(2,1)}, u32[]{:S(2)}, u32[]{:S(2)}) collective-permute-start(bf16[3,176,4096]{2,1,0:T(8,128)(2,1)} %collective-permute-done.5.refs_2_), channel_id=1, source_target_pairs={{0,1},{1,0},{2,3},{3,2},{4,5},{5,4},{6,7},{7,6}} | collective-permute-start | bytes 12976136 | tf_op jit(solution)/shard_map/cond/branch_1_fun/ppermute | solution.py:202
  1391.1 45.1 %collective-permute-start.9 = (bf16[3,176,4096]{2,1,0:T(8,128)(2,1)}, bf16[3,176,4096]{2,1,0:T(8,128)(2,1)}, u32[]{:S(2)}, u32[]{:S(2)}) collective-permute-start(bf16[3,176,4096]{2,1,0:T(8,128)(2,1)} %collective-permute-done.3.refs_1_), channel_id=1, source_target_pairs={{0,1},{1,0},{2,3},{3,2},{4,5},{5,4},{6,7},{7,6}} | collective-permute-start | bytes 12976136 | tf_op jit(solution)/shard_map/cond/branch_1_fun/ppermute | solution.py:202
  1391.6 44.6 %collective-permute-start.11 = (bf16[3,176,4096]{2,1,0:T(8,128)(2,1)}, bf16[3,176,4096]{2,1,0:T(8,128)(2,1)}, u32[]{:S(2)}, u32[]{:S(2)}) collective-permute-start(bf16[3,176,4096]{2,1,0:T(8,128)(2,1)} %collective-permute-done.7.refs_3_), channel_id=1, source_target_pairs={{0,1},{1,0},{2,3},{3,2},{4,5},{5,4},{6,7},{7,6}} | collective-permute-start | bytes 12976136 | tf_op jit(solution)/shard_map/cond/branch_1_fun/ppermute | solution.py:202
  1461.6 31.2 %copy-start.9 = (f32[2368,2]{1,0:T(8,128)S(1)}, f32[2368,2]{1,0:T(8,128)}, u32[]{:S(2)}) copy-start(f32[2368,2]{1,0:T(8,128)} %broadcast_divide_fusion.3) | copy-start | bytes 56836 | tf_op jit(solution)/shard_map/cond
  1491.8 124.6 %collective-permute-start.16 = (bf16[320,4096]{1,0:T(8,128)(2,1)}, bf16[320,4096]{1,0:T(8,128)(2,1)}, u32[]{:S(2)}, u32[]{:S(2)}) collective-permute-start(bf16[320,4096]{1,0:T(8,128)(2,1)} %fusion.56), channel_id=1, source_target_pairs={{0,4},{1,5},{2,6},{3,7},{4,0},{5,1},{6,2},{7,3}} | collective-permute-start | bytes 7864328 | tf_op jit(solution)/shard_map/cond/branch_1_fun/ppermute | solution.py:202
  1494.1 277.4 %collective-permute-start.17 = (bf16[3,176,4096]{2,1,0:T(8,128)(2,1)}, bf16[3,176,4096]{2,1,0:T(8,128)(2,1)}, u32[]{:S(2)}, u32[]{:S(2)}) collective-permute-start(bf16[3,176,4096]{2,1,0:T(8,128)(2,1)} %bitcast.286), channel_id=1, source_target_pairs={{0,4},{1,5},{2,6},{3,7},{4,0},{5,1},{6,2},{7,3}} | collective-permute-start | bytes 12976136 | tf_op jit(solution)/shard_map/cond/branch_1_fun/ppermute | solution.py:202
  1496.1 459.6 %collective-permute-start.18 = (bf16[3,176,4096]{2,1,0:T(8,128)(2,1)}, bf16[3,176,4096]{2,1,0:T(8,128)(2,1)}, u32[]{:S(2)}, u32[]{:S(2)}) collective-permute-start(bf16[3,176,4096]{2,1,0:T(8,128)(2,1)} %bitcast.283), channel_id=1, source_target_pairs={{0,4},{1,5},{2,6},{3,7},{4,0},{5,1},{6,2},{7,3}} | collective-permute-start | bytes 12976136 | tf_op jit(solution)/shard_map/cond/branch_1_fun/ppermute | solution.py:202
  1496.1 459.6 %collective-permute-start.19 = (bf16[3,176,4096]{2,1,0:T(8,128)(2,1)}, bf16[3,176,4096]{2,1,0:T(8,128)(2,1)}, u32[]{:S(2)}, u32[]{:S(2)}) collective-permute-start(bf16[3,176,4096]{2,1,0:T(8,128)(2,1)} %bitcast.356), channel_id=1, source_target_pairs={{0,2},{1,3},{2,0},{3,1},{4,6},{5,7},{6,4},{7,5}} | collective-permute-start | bytes 12976136 | tf_op jit(solution)/shard_map/cond/branch_1_fun/ppermute | solution.py:202
  1506.2 449.5 %collective-permute-start.20 = (bf16[3,176,4096]{2,1,0:T(8,128)(2,1)}, bf16[3,176,4096]{2,1,0:T(8,128)(2,1)}, u32[]{:S(2)}, u32[]{:S(2)}) collective-permute-start(bf16[3,176,4096]{2,1,0:T(8,128)(2,1)} %bitcast.355), channel_id=1, source_target_pairs={{0,2},{1,3},{2,0},{3,1},{4,6},{5,7},{6,4},{7,5}} | collective-permute-start | bytes 12976136 | tf_op jit(solution)/shard_map/cond/branch_1_fun/ppermute | solution.py:202
  1616.4 30.7 %copy-start.34 = (f32[2048]{0:T(1024)S(1)}, f32[2048]{0:T(1024)}, u32[]{:S(2)}) copy-start(f32[2048]{0:T(1024)} %slice_reduce_fusion.1) | copy-start | bytes 24580 | tf_op jit(solution)/shard_map/cond
  1616.4 30.7 %copy-start.44 = (pred[2048]{0:T(1024)(128)(4,1)S(1)}, pred[2048]{0:T(1024)(128)(4,1)}, u32[]{:S(2)}) copy-start(pred[2048]{0:T(1024)(128)(4,1)} %copy-done.42) | copy-start | bytes 6148 | tf_op jit(solution)/shard_map/cond
  1647.1 308.6 %copy-start.51 = (s32[1024]{0:T(1024)S(1)}, s32[1024]{0:T(1024)}, u32[]{:S(2)}) copy-start(s32[1024]{0:T(1024)} %get-tuple-element.814) | copy-start | bytes 12292 | tf_op jit(solution)/shard_map/cond
  1684.4 289.5 %copy-start.57 = (s32[5]{0:T(128)S(1)}, s32[5]{0:T(128)}, u32[]{:S(2)}) copy-start(s32[5]{0:T(128)} %get-tuple-element.752) | copy-start | bytes 64 | tf_op jit(solution)/shard_map/cond
  1684.4 289.6 %copy-start.21 = (s32[2368]{0:T(1024)S(1)}, s32[2368]{0:T(1024)}, u32[]{:S(2)}) copy-start(s32[2368]{0:T(1024)} %copy-done.20) | copy-start | bytes 28420 | tf_op jit(solution)/shard_map/cond
  1684.4 289.6 %copy-start.56 = (s32[64]{0:T(128)S(1)}, s32[64]{0:T(128)}, u32[]{:S(2)}) copy-start(s32[64]{0:T(128)} %copy-done.55) | copy-start | bytes 772 | tf_op jit(solution)/shard_map/cond
  1684.4 295.5 %copy-start.60 = (s32[5]{0:T(128)S(1)}, s32[5]{0:T(128)}, u32[]{:S(2)}) copy-start(s32[5]{0:T(128)} %get-tuple-element.753) | copy-start | bytes 64 | tf_op jit(solution)/shard_map/cond
  1684.4 295.6 %copy-start.58 = (s32[5,1]{0,1:T(1,128)S(1)}, s32[5,1]{0,1:T(1,128)}, u32[]{:S(2)}) copy-start(s32[5,1]{0,1:T(1,128)} %get-tuple-element.810) | copy-start | bytes 64 | tf_op jit(solution)/shard_map/cond
  1684.5 296.4 %copy-start.23 = (s32[1,2048]{1,0:T(1,128)S(1)}, s32[1,2048]{1,0:T(1,128)}, u32[]{:S(2)}) copy-start(s32[1,2048]{1,0:T(1,128)} %copy-done.22) | copy-start | bytes 24580 | tf_op jit(solution)/shard_map/cond
  1684.5 296.4 %copy-start.53 = (s32[320]{0:T(512)S(1)}, s32[320]{0:T(512)}, u32[]{:S(2)}) copy-start(s32[320]{0:T(512)} %get-tuple-element.790) | copy-start | bytes 3844 | tf_op jit(solution)/shard_map/cond
  1971.7 58.4 %collective-permute-start.21 = (bf16[320,4096]{1,0:T(8,128)(2,1)S(1)}, bf16[320,4096]{1,0:T(8,128)(2,1)}, u32[]{:S(2)}, u32[]{:S(2)}) collective-permute-start(bf16[320,4096]{1,0:T(8,128)(2,1)S(1)} %gather_fusion.9), channel_id=1, source_target_pairs={{0,2},{1,3},{2,0},{3,1},{4,6},{5,7},{6,4},{7,5}} | collective-permute-start | bytes 7864328 | tf_op jit(solution)/shard_map/cond/branch_1_fun/ppermute | solution.py:202
  1980.9 345.5 %collective-permute-start.29 = (bf16[3,176,4096]{2,1,0:T(8,128)(2,1)}, bf16[3,176,4096]{2,1,0:T(8,128)(2,1)}, u32[]{:S(2)}, u32[]{:S(2)}) collective-permute-start(bf16[3,176,4096]{2,1,0:T(8,128)(2,1)} %bitcast.287), channel_id=1, source_target_pairs={{0,1},{1,0},{2,3},{3,2},{4,5},{5,4},{6,7},{7,6}} | collective-permute-start | bytes 12976136 | tf_op jit(solution)/shard_map/cond/branch_1_fun/ppermute | solution.py:202
  1981.0 332.5 %collective-permute-start.23 = (bf16[3,176,4096]{2,1,0:T(8,128)(2,1)}, bf16[3,176,4096]{2,1,0:T(8,128)(2,1)}, u32[]{:S(2)}, u32[]{:S(2)}) collective-permute-start(bf16[3,176,4096]{2,1,0:T(8,128)(2,1)} %collective-permute-done.19.refs_2_), channel_id=1, source_target_pairs={{0,4},{1,5},{2,6},{3,7},{4,0},{5,1},{6,2},{7,3}} | collective-permute-start | bytes 12976136 | tf_op jit(solution)/shard_map/cond/branch_1_fun/ppermute | solution.py:202
  1981.4 345.5 %collective-permute-start.31 = (bf16[3,176,4096]{2,1,0:T(8,128)(2,1)}, bf16[3,176,4096]{2,1,0:T(8,128)(2,1)}, u32[]{:S(2)}, u32[]{:S(2)}) collective-permute-start(bf16[3,176,4096]{2,1,0:T(8,128)(2,1)} %collective-permute-done.19.refs_2_), channel_id=1, source_target_pairs={{0,1},{1,0},{2,3},{3,2},{4,5},{5,4},{6,7},{7,6}} | collective-permute-start | bytes 12976136 | tf_op jit(solution)/shard_map/cond/branch_1_fun/ppermute | solution.py:202
  1981.6 331.9 %collective-permute-start.24 = (bf16[3,176,4096]{2,1,0:T(8,128)(2,1)}, bf16[3,176,4096]{2,1,0:T(8,128)(2,1)}, u32[]{:S(2)}, u32[]{:S(2)}) collective-permute-start(bf16[3,176,4096]{2,1,0:T(8,128)(2,1)} %collective-permute-done.20.refs_2_), channel_id=1, source_target_pairs={{0,4},{1,5},{2,6},{3,7},{4,0},{5,1},{6,2},{7,3}} | collective-permute-start | bytes 12976136 | tf_op jit(solution)/shard_map/cond/branch_1_fun/ppermute | solution.py:202
  1991.7 47.0 %copy-start.24 = (f32[1,4096]{1,0:T(1,128)S(1)}, f32[1,4096]{1,0:T(1,128)}, u32[]{:S(2)}) copy-start(f32[1,4096]{1,0:T(1,128)} %get-tuple-element.776) | copy-start | bytes 49156 | tf_op jit(solution)/shard_map/cond
  2030.0 296.8 %collective-permute-start.30 = (bf16[3,176,4096]{2,1,0:T(8,128)(2,1)}, bf16[3,176,4096]{2,1,0:T(8,128)(2,1)}, u32[]{:S(2)}, u32[]{:S(2)}) collective-permute-start(bf16[3,176,4096]{2,1,0:T(8,128)(2,1)} %collective-permute-done.17.refs_1_), channel_id=1, source_target_pairs={{0,1},{1,0},{2,3},{3,2},{4,5},{5,4},{6,7},{7,6}} | collective-permute-start | bytes 12976136 | tf_op jit(solution)/shard_map/cond/branch_1_fun/ppermute | solution.py:202
  2263.1 64.3 %copy-start.62 = (s32[5]{0:T(128)S(1)}, s32[5]{0:T(128)}, u32[]{:S(2)}) copy-start(s32[5]{0:T(128)} %copy-done.61) | copy-start | bytes 64 | tf_op jit(solution)/shard_map/cond
  2263.1 64.3 %copy-start.52 = (bf16[19,5]{0,1:T(8,128)(2,1)S(1)}, bf16[19,5]{0,1:T(8,128)(2,1)}, u32[]{:S(2)}) copy-start(bf16[19,5]{0,1:T(8,128)(2,1)} %get-tuple-element.700) | copy-start | bytes 574 | tf_op jit(solution)/shard_map/cond
  2263.1 64.4 %copy-start.31 = (s32[19,128]{1,0:T(8,128)S(1)}, s32[19,128]{1,0:T(8,128)}, u32[]{:S(2)}) copy-start(s32[19,128]{1,0:T(8,128)} %copy-done.30) | copy-start | bytes 29188 | tf_op jit(solution)/shard_map/cond
  2313.5 20.2 collective-permute-start.32
  2326.4 45.2 %collective-permute-start.25 = (bf16[3,176,4096]{2,1,0:T(8,128)(2,1)}, bf16[3,176,4096]{2,1,0:T(8,128)(2,1)}, u32[]{:S(2)}, u32[]{:S(2)}) collective-permute-start(bf16[3,176,4096]{2,1,0:T(8,128)(2,1)} %bitcast.284), channel_id=1, source_target_pairs={{0,1},{1,0},{2,3},{3,2},{4,5},{5,4},{6,7},{7,6}} | collective-permute-start | bytes 12976136 | tf_op jit(solution)/shard_map/cond/branch_1_fun/ppermute | solution.py:202
  2326.4 45.2 %collective-permute-start.27 = (bf16[3,176,4096]{2,1,0:T(8,128)(2,1)}, bf16[3,176,4096]{2,1,0:T(8,128)(2,1)}, u32[]{:S(2)}, u32[]{:S(2)}) collective-permute-start(bf16[3,176,4096]{2,1,0:T(8,128)(2,1)} %collective-permute-done.20.refs_2_), channel_id=1, source_target_pairs={{0,1},{1,0},{2,3},{3,2},{4,5},{5,4},{6,7},{7,6}} | collective-permute-start | bytes 12976136 | tf_op jit(solution)/shard_map/cond/branch_1_fun/ppermute | solution.py:202
  2326.9 44.7 %collective-permute-start.26 = (bf16[3,176,4096]{2,1,0:T(8,128)(2,1)}, bf16[3,176,4096]{2,1,0:T(8,128)(2,1)}, u32[]{:S(2)}, u32[]{:S(2)}) collective-permute-start(bf16[3,176,4096]{2,1,0:T(8,128)(2,1)} %collective-permute-done.18.refs_1_), channel_id=1, source_target_pairs={{0,1},{1,0},{2,3},{3,2},{4,5},{5,4},{6,7},{7,6}} | collective-permute-start | bytes 12976136 | tf_op jit(solution)/shard_map/cond/branch_1_fun/ppermute | solution.py:202
  2326.9 44.7 %collective-permute-start.28 = (bf16[3,176,4096]{2,1,0:T(8,128)(2,1)}, bf16[3,176,4096]{2,1,0:T(8,128)(2,1)}, u32[]{:S(2)}, u32[]{:S(2)}) collective-permute-start(bf16[3,176,4096]{2,1,0:T(8,128)(2,1)} %collective-permute-done.24.refs_3_), channel_id=1, source_target_pairs={{0,1},{1,0},{2,3},{3,2},{4,5},{5,4},{6,7},{7,6}} | collective-permute-start | bytes 12976136 | tf_op jit(solution)/shard_map/cond/branch_1_fun/ppermute | solution.py:202
  2424.1 59.5 %collective-permute-start.33 = (bf16[320,4096]{1,0:T(8,128)(2,1)}, bf16[320,4096]{1,0:T(8,128)(2,1)}, u32[]{:S(2)}, u32[]{:S(2)}) collective-permute-start(bf16[320,4096]{1,0:T(8,128)(2,1)} %fusion.55), channel_id=1, source_target_pairs={{0,2},{1,3},{2,0},{3,1},{4,6},{5,7},{6,4},{7,5}} | collective-permute-start | bytes 7864328 | tf_op jit(solution)/shard_map/cond/branch_1_fun/ppermute | solution.py:202
  2552.2 72.6 %copy-start.35 = (f32[2048]{0:T(1024)S(1)}, f32[2048]{0:T(1024)}, u32[]{:S(2)}) copy-start(f32[2048]{0:T(1024)} %slice_reduce_fusion) | copy-start | bytes 24580 | tf_op jit(solution)/shard_map/cond
  2552.2 72.6 %copy-start.41 = (pred[2048]{0:T(1024)(128)(4,1)S(1)}, pred[2048]{0:T(1024)(128)(4,1)}, u32[]{:S(2)}) copy-start(pred[2048]{0:T(1024)(128)(4,1)} %copy-done.38) | copy-start | bytes 6148 | tf_op jit(solution)/shard_map/cond
  (23 other events, 251.4 us)
Sparse Core Ops, SparseCore 0:
  61.9 217.5 all-gather.11
  281.3 160.7 all-gather.15
  444.0 245.6 all-gather.13
  691.3 295.7 all-gather.17
  988.8 263.2 all-gather.19
  1253.8 163.1 all-gather.21
  1418.9 241.8 all-gather.25
  1662.6 297.5 all-gather.23
